TPU v7x, 256 devices: a 8x8x2 block of a 8x8x16 slice. The times are simulated.
256 devices in a mesh: groups: 2 (over z), scan: 128 (over x, y, core).
Axes of the slice: x: 8, y: 8, z: 2, core: 2. Of those that a mesh axis runs over, the one named last changes fastest.
The devices are a block of a 8x8x16 slice.
Arguments:
- object_field: float32 [2, 6144, 1792], P(None, ('groups', 'scan')), parts along dimension 1, may hold values from -8 to 8
- probe_field: float32 [2, 2048, 256], P(None, 'groups'), parts along dimension 1, may hold values from -3 to 3
- amplitudes: float32 [1024, 256, 256], P(('groups', 'scan')), parts along dimension 0, may hold values from 0.2 to 3
- offsets: int32 [1024, 2], P(('groups', 'scan')), parts along dimension 0, may hold values from -8 to 2984, as said below
- live_counts: int32 [256], P(('groups', 'scan')), parts along dimension 0, may hold values from 1 to 4, as said below
Outputs:
- new_object: float32 [2, 6144, 1792], P(None, ('groups', 'scan')), parts along dimension 1
- new_probe: float32 [2, 2048, 256], P(None, ('groups', 'scan')), parts along dimension 1
There are 2 independent parts, one for each index of `groups`. A program takes and returns all parts, laid end to end along the dimension named above; each array names one. Nothing has to cross between parts.
Inputs may be any that keep to these rules, and one draw needn't show every extreme that they name: Position p lies in scan row p // 16, column p % 16: offsets[p, 0] is within 8 of 96 * (p // 16) and offsets[p, 1] within 8 of 48 + 96 * (p % 16); the first position of every block of 4, except position 511, has offsets[p, 0] = 96 * (p // 16) - 8; the single position 511 has offsets[p, 0] = 96 * (p // 16) + 8. Block b of 4 consecutive positions measures its first live_counts[b]; some block measures all 4 and some only one.
All inputs are finite; a program needn't handle non-finite values.
Results may differ from a plain program's by a relative error of at most 0.0013.
Values sent between devices are 32-bit elements; how exact they have to be, the bound alone decides.
A program may use at most 128 MiB of HBM per device.

v0:
```python
import math

import jax
import jax.numpy as jnp
from jax import lax
from jax.sharding import Mesh
from jax.sharding import PartitionSpec as P

SPLIT = 4
JITTER = 8
SCAN = ("scan_0", "scan_1", "scan_2")
GROUPS_SCAN = ("groups", "scan_0", "scan_1", "scan_2")


def from_behind(shard, axis, by):
    size = lax.axis_size(axis)
    pairs = [(i, i + by) for i in range(size) if 0 <= i + by < size]
    return lax.ppermute(shard, axis, pairs)


def one_axis_at_a_time(shard, axes):
    for axis in axes:
        shard = lax.psum(shard, axis)
    return shard


def dft_tables(length, sine_sign):
    numbers = jnp.arange(length, dtype=jnp.int32)
    product = numbers[:, None] * numbers[None, :] % length
    angles = product.astype(jnp.float32) * (2.0 * math.pi / length)
    scaling = 1.0 / math.sqrt(length)
    cosine = jnp.cos(angles) * scaling
    sine_part = jnp.sin(angles) * (sine_sign * scaling)
    left_table = jnp.stack(
        [jnp.stack([cosine, sine_part], 1), jnp.stack([-sine_part, cosine], 1)], 0
    ).astype(jnp.bfloat16)
    right_table = jnp.stack(
        [jnp.stack([cosine, -sine_part], 1), jnp.stack([sine_part, cosine], 1)], 0
    ).astype(jnp.bfloat16)
    return (left_table, right_table)


def transform(exit_wave, tables):
    left_table, right_table = tables
    half_done = jnp.einsum(
        "dkcm,camn->dakn", left_table, exit_wave, preferred_element_type=jnp.float32
    ).astype(jnp.bfloat16)
    return jnp.einsum("camn,cndk->damk", half_done, right_table, preferred_element_type=jnp.float32)


def exit_update(obj_patch, probe_modes, amplitude, forward, inverse):
    probe_re, probe_im = (probe_modes[0], probe_modes[1])
    patch_re, patch_im = (obj_patch[0], obj_patch[1])
    exit_wave = jnp.stack(
        [probe_re * patch_re - probe_im * patch_im, probe_re * patch_im + probe_im * patch_re]
    ).astype(jnp.bfloat16)
    far_field = transform(exit_wave, forward)
    intensity = jnp.sum(far_field[0] * far_field[0] + far_field[1] * far_field[1], axis=0)
    factor = amplitude / jnp.maximum(jnp.sqrt(intensity), 0.5) - 1.0
    far_change = (far_field * factor).astype(jnp.bfloat16)
    exit_change = transform(far_change, inverse)
    grad_re = jnp.sum(probe_re * exit_change[0] + probe_im * exit_change[1], axis=0)
    grad_im = jnp.sum(probe_re * exit_change[1] - probe_im * exit_change[0], axis=0)
    mode_re = patch_re * exit_change[0] + patch_im * exit_change[1]
    mode_im = patch_re * exit_change[1] - patch_im * exit_change[0]
    return (
        grad_re,
        grad_im,
        jnp.stack([mode_re, mode_im]),
        patch_re * patch_re + patch_im * patch_im,
    )


def on_device(object_field, probe_field, amplitudes, offsets, live_counts):
    strip_rows = object_field.shape[1]
    columns = object_field.shape[2]
    patch_size = amplitudes.shape[1]
    mode_count = probe_field.shape[1] // patch_size
    ahead_count = (JITTER + patch_size - 1) // strip_rows
    lead_rows = JITTER + (SPLIT - 1) * strip_rows
    device_index = lax.axis_index(SCAN)
    window_top = device_index * strip_rows - lead_rows
    zero_index = jnp.zeros((), jnp.int32)
    probe_modes = probe_field.reshape(2, mode_count, patch_size, patch_size)
    illum_one = jnp.sum(probe_modes[0] ** 2 + probe_modes[1] ** 2, axis=0)
    forward = dft_tables(patch_size, 1.0)
    inverse = dft_tables(patch_size, -1.0)

    def pull_window(field):
        pieces = []
        for distance in range(SPLIT, 0, -1):
            sent = field[:, strip_rows - JITTER :] if distance == SPLIT else field
            pieces.append(from_behind(sent, SCAN, distance))
        pieces.append(field)
        for distance in range(1, ahead_count + 1):
            pieces.append(from_behind(field, SCAN, -distance))
        return jnp.concatenate(pieces, 1)

    window = pull_window(object_field)
    window_rows = window.shape[1]
    live_here = live_counts[0]

    def visit(position, running):
        grad_grid, grad_probe, obj_norm = running
        corner = lax.dynamic_index_in_dim(offsets, position, 0, keepdims=False)
        top_row = corner[0] - window_top
        left_col = corner[1]
        obj_patch = lax.dynamic_slice(
            window, (zero_index, top_row, left_col), (2, patch_size, patch_size)
        )
        amplitude = lax.dynamic_index_in_dim(amplitudes, position, 0, keepdims=False)
        grad_re, grad_im, probe_part, norm_part = exit_update(
            obj_patch, probe_modes, amplitude, forward, inverse
        )
        contrib = jnp.stack([grad_re, grad_im, illum_one])
        current = lax.dynamic_slice(
            grad_grid, (zero_index, top_row, left_col), (3, patch_size, patch_size)
        )
        grad_grid = lax.dynamic_update_slice(
            grad_grid, current + contrib, (zero_index, top_row, left_col)
        )
        return (grad_grid, grad_probe + probe_part, obj_norm + norm_part)

    start_state = (
        jnp.zeros((3, window_rows, columns), jnp.float32),
        jnp.zeros((2, mode_count, patch_size, patch_size), jnp.float32),
        jnp.zeros((patch_size, patch_size), jnp.float32),
    )
    grad_grid, grad_probe, obj_norm = lax.fori_loop(0, live_here, visit, start_state)
    own_rows = grad_grid[:, lead_rows : lead_rows + strip_rows]
    for distance in range(SPLIT, 0, -1):
        first_row = 0 if distance == SPLIT else JITTER + (SPLIT - 1 - distance) * strip_rows
        row_span = JITTER if distance == SPLIT else strip_rows
        arrived = from_behind(grad_grid[:, first_row : first_row + row_span], SCAN, -distance)
        own_rows = own_rows.at[:, strip_rows - row_span :].add(arrived)
    for distance in range(1, ahead_count + 1):
        first_row = lead_rows + distance * strip_rows
        own_rows = own_rows + from_behind(
            grad_grid[:, first_row : first_row + strip_rows], SCAN, distance
        )
    obj_step = own_rows[:2] / (own_rows[2] + 1.0)
    part_uu = jnp.sum((obj_step[0] ** 2 + obj_step[1] ** 2) * own_rows[2])
    part_uc = jnp.sum(obj_step[0] * own_rows[0] + obj_step[1] * own_rows[1])
    step_window = pull_window(obj_step)

    def cross_terms(position, summed):
        corner = lax.dynamic_index_in_dim(offsets, position, 0, keepdims=False)
        top_row = corner[0] - window_top
        left_col = corner[1]
        obj_patch = lax.dynamic_slice(
            window, (zero_index, top_row, left_col), (2, patch_size, patch_size)
        )
        step_patch = lax.dynamic_slice(
            step_window, (zero_index, top_row, left_col), (2, patch_size, patch_size)
        )
        cross_re = step_patch[0] * obj_patch[0] + step_patch[1] * obj_patch[1]
        cross_im = step_patch[0] * obj_patch[1] - step_patch[1] * obj_patch[0]
        return summed + jnp.stack([cross_re, cross_im])

    cross_sum = lax.fori_loop(
        0, live_here, cross_terms, jnp.zeros((2, patch_size, patch_size), jnp.float32)
    )
    share_rows = probe_field.shape[1] // lax.axis_size(SCAN)
    row_start = device_index * share_rows
    probe_share = lax.dynamic_slice_in_dim(probe_field, row_start, share_rows, 1)
    summed_probe, summed_norm = lax.psum((grad_probe, obj_norm), SCAN)
    probe_step = summed_probe / (summed_norm + 1.0)
    conj_re = probe_modes[0] * probe_step[0] + probe_modes[1] * probe_step[1]
    conj_im = probe_modes[0] * probe_step[1] - probe_modes[1] * probe_step[0]
    part_uv = jnp.sum(conj_re * cross_sum[0] - conj_im * cross_sum[1])
    flat_rows = mode_count * patch_size
    step_share = lax.dynamic_slice_in_dim(
        probe_step.reshape(2, flat_rows, patch_size), row_start, share_rows, 1
    )
    grad_share = lax.dynamic_slice_in_dim(
        summed_probe.reshape(2, flat_rows, patch_size), row_start, share_rows, 1
    )
    norm_flat = jnp.broadcast_to(summed_norm[None], (mode_count, patch_size, patch_size)).reshape(
        flat_rows, patch_size
    )
    norm_share = lax.dynamic_slice_in_dim(norm_flat, row_start, share_rows, 0)
    part_vv = jnp.sum((step_share[0] ** 2 + step_share[1] ** 2) * norm_share)
    part_vc = jnp.sum(step_share * grad_share)
    totals = one_axis_at_a_time(jnp.stack([part_uu, part_uv, part_vv, part_uc, part_vc]), SCAN)
    diag_obj = 1.1 * totals[0] + 1e-06
    diag_probe = 1.1 * totals[2] + 1e-06
    determinant = diag_obj * diag_probe - totals[1] * totals[1]
    rate_obj = (totals[3] * diag_probe - totals[1] * totals[4]) / determinant
    rate_probe = (diag_obj * totals[4] - totals[1] * totals[3]) / determinant
    new_object = object_field + rate_obj * obj_step
    new_probe = probe_share + rate_probe * step_share
    return (new_object, new_probe)


def solution(mesh):
    split = Mesh(
        mesh.devices.reshape(mesh.shape["groups"], 8, 8, 2),
        ("groups", "scan_0", "scan_1", "scan_2"),
    )
    placed = (
        P(None, GROUPS_SCAN, None),
        P(None, "groups", None),
        P(GROUPS_SCAN, None, None),
        P(GROUPS_SCAN, None),
        P(GROUPS_SCAN),
    )
    return jax.shard_map(
        on_device,
        mesh=split,
        in_specs=placed,
        out_specs=(P(None, GROUPS_SCAN, None), P(None, GROUPS_SCAN, None)),
        check_vma=False,
    )
```

profile of v0, /device:TPU:513, one launch (start us, length us, event | category | flops | bytes accessed | tf_op | source)
XLA Modules:
  0.0 1123.3 jit_solution(11058947790315205256)
XLA Ops:
  7.3 8.8 collective-permute-start.1
  22.5 13.4 %collective-permute-start.4 = (f32[2,24,1792]{2,1,0:T(8,128)}, f32[2,24,1792]{2,1,0:T(8,128)}, u32[]{:S(2)}, u32[]{:S(2)}) collective-permute-start(f32[2,24,1792]{2,1,0:T(8,128)} %param.23), channel_id=1, source_target_pairs={{1,0},{2,1},{3,2},{4,3},{5,4},{6,5},{7,6},{8,7},{9,8},{10,9},{11,1... | collective-permute-start | bytes 1032200 | tf_op jit(solution)/shard_map/ppermute | solution.py:18
  69.5 10.1 collective-permute-done.5
  81.6 65.4 %collective-permute-done.6 = f32[2,24,1792]{2,1,0:T(8,128)S(1)} collective-permute-done((f32[2,24,1792]{2,1,0:T(8,128)S(1)}, f32[2,24,1792]{2,1,0:T(8,128)S(1)}, u32[]{:S(2)}, u32[]{:S(2)}) %collective-permute-start.6) | collective-permute-done | bytes 344096 | tf_op jit(solution)/shard_map/ppermute | solution.py:18
  149.0 42.5 %collective-permute-done.7 = f32[2,24,1792]{2,1,0:T(8,128)S(1)} collective-permute-done((f32[2,24,1792]{2,1,0:T(8,128)S(1)}, f32[2,24,1792]{2,1,0:T(8,128)S(1)}, u32[]{:S(2)}, u32[]{:S(2)}) %collective-permute-start.7) | collective-permute-done | bytes 344096 | tf_op jit(solution)/shard_map/ppermute | solution.py:18
  197.9 24.4 %collective-permute-done.12 = f32[2,24,1792]{2,1,0:T(8,128)S(1)} collective-permute-done((f32[2,24,1792]{2,1,0:T(8,128)S(1)}, f32[2,24,1792]{2,1,0:T(8,128)S(1)}, u32[]{:S(2)}, u32[]{:S(2)}) %collective-permute-start.12) | collective-permute-done | bytes 344096 | tf_op jit(solution)/shard_map/ppermute | solution.py:18
  230.8 65.3 %while.33 = (s32[]{:T(128)}, f32[3,344,1792]{2,1,0:T(8,128)}, f32[2,4,256,256]{3,2,0,1:T(8,128)}, f32[256,256]{1,0:T(8,128)S(1)}, s32[]{:T(128)}, /*index=5*/s32...) while((s32[]{:T(128)}, f32[3,344,1792]{2,1,0:T(8,128)}, ...), condition=%wide.region_5.6_spmd, body=%wide.region_1.5_spmd.sunk | while | flops 2160394240 | bytes 53477836 | solution.py:129
  244.2 4.5 convolution_bitcast_fusion.5
  254.4 8.9 dynamic_update_slice.7
  276.4 4.5 convolution_bitcast_fusion.5
  286.6 8.8 dynamic_update_slice.7
  296.1 4.7 fusion.45
  311.3 50.4 %collective-permute-done.14 = f32[3,8,1792]{2,1,0:T(8,128)S(1)} collective-permute-done((f32[3,8,1792]{2,1,0:T(8,128)S(1)}, f32[3,8,1792]{2,1,0:T(8,128)S(1)}, u32[]{:S(2)}, u32[]{:S(2)}) %collective-permute-start.14) | collective-permute-done | bytes 172064 | tf_op jit(solution)/shard_map/ppermute | solution.py:18
  361.7 28.0 %collective-permute-start.19 = (f32[3,24,1792]{2,1,0:T(8,128)S(1)}, f32[3,24,1792]{2,1,0:T(8,128)S(1)}, u32[]{:S(2)}, u32[]{:S(2)}) collective-permute-start(f32[3,24,1792]{2,1,0:T(8,128)S(1)} %get-tuple-element.410), channel_id=1, source_target_pairs={{0,2},{1,3},{2,4},{3,5},{4,6},{5,7},{6,8},{7,9},{8,10},{9,11},{10,... | collective-permute-start | bytes 1548296 | tf_op jit(solution)/shard_map/ppermute | solution.py:18
  389.8 17.4 %collective-permute-start.20 = (f32[3,24,1792]{2,1,0:T(8,128)S(1)}, f32[3,24,1792]{2,1,0:T(8,128)S(1)}, u32[]{:S(2)}, u32[]{:S(2)}) collective-permute-start(f32[3,24,1792]{2,1,0:T(8,128)S(1)} %get-tuple-element.409), channel_id=1, source_target_pairs={{0,3},{1,4},{2,5},{3,6},{4,7},{5,8},{6,9},{7,10},{8,11},{9,12},{10... | collective-permute-start | bytes 1548296 | tf_op jit(solution)/shard_map/ppermute | solution.py:18
  407.2 15.9 %collective-permute-start.21 = (f32[3,24,1792]{2,1,0:T(8,128)S(1)}, f32[3,24,1792]{2,1,0:T(8,128)S(1)}, u32[]{:S(2)}, u32[]{:S(2)}) collective-permute-start(f32[3,24,1792]{2,1,0:T(8,128)S(1)} %get-tuple-element.408), channel_id=1, source_target_pairs={{0,4},{1,5},{2,6},{3,7},{4,8},{5,9},{6,10},{7,11},{8,12},{9,13},{1... | collective-permute-start | bytes 1548296 | tf_op jit(solution)/shard_map/ppermute | solution.py:18
  423.2 6.9 collective-permute-start.22
  434.6 22.8 %collective-permute-start.25 = (f32[3,24,1792]{2,1,0:T(8,128)}, f32[3,24,1792]{2,1,0:T(8,128)}, u32[]{:S(2)}, u32[]{:S(2)}) collective-permute-start(f32[3,24,1792]{2,1,0:T(8,128)} %get-tuple-element.404), channel_id=1, source_target_pairs={{0,8},{1,9},{2,10},{3,11},{4,12},{5,13},{6,14},{7,15},{8,16},{9,17... | collective-permute-start | bytes 1548296 | tf_op jit(solution)/shard_map/ppermute | solution.py:18
  457.4 33.4 %collective-permute-start.26 = (f32[3,24,1792]{2,1,0:T(8,128)S(1)}, f32[3,24,1792]{2,1,0:T(8,128)}, u32[]{:S(2)}, u32[]{:S(2)}) collective-permute-start(f32[3,24,1792]{2,1,0:T(8,128)S(1)} %get-tuple-element.403), channel_id=1, source_target_pairs={{0,9},{1,10},{2,11},{3,12},{4,13},{5,14},{6,15},{7,16},{8,17},{9,1... | collective-permute-start | bytes 1548296 | tf_op jit(solution)/shard_map/ppermute | solution.py:18
  494.7 38.8 %collective-permute-done.26 = f32[3,24,1792]{2,1,0:T(8,128)} collective-permute-done((f32[3,24,1792]{2,1,0:T(8,128)S(1)}, f32[3,24,1792]{2,1,0:T(8,128)}, u32[]{:S(2)}, u32[]{:S(2)}) %collective-permute-start.26) | collective-permute-done | bytes 516128 | tf_op jit(solution)/shard_map/ppermute | solution.py:18
  533.6 5.5 collective-permute-done.27
  542.2 44.2 %collective-permute-start.29 = (f32[2,24,1792]{2,1,0:T(8,128)S(1)}, f32[2,24,1792]{2,1,0:T(8,128)S(1)}, u32[]{:S(2)}, u32[]{:S(2)}) collective-permute-start(f32[2,24,1792]{2,1,0:T(8,128)S(1)} %slice_divide_fusion), channel_id=1, source_target_pairs={{0,3},{1,4},{2,5},{3,6},{4,7},{5,8},{6,9},{7,10},{8,11},{9,12},{10... | collective-permute-start | bytes 1032200 | tf_op jit(solution)/shard_map/ppermute | solution.py:18
  592.8 8.3 collective-permute-start.28
  609.7 44.2 %collective-permute-done.33 = f32[2,24,1792]{2,1,0:T(8,128)S(1)} collective-permute-done((f32[2,24,1792]{2,1,0:T(8,128)S(1)}, f32[2,24,1792]{2,1,0:T(8,128)S(1)}, u32[]{:S(2)}, u32[]{:S(2)}) %collective-permute-start.33) | collective-permute-done | bytes 344096 | tf_op jit(solution)/shard_map/ppermute | solution.py:18
  655.3 122.8 %collective-permute-done.34 = f32[2,24,1792]{2,1,0:T(8,128)S(1)} collective-permute-done((f32[2,24,1792]{2,1,0:T(8,128)S(1)}, f32[2,24,1792]{2,1,0:T(8,128)S(1)}, u32[]{:S(2)}, u32[]{:S(2)}) %collective-permute-start.34) | collective-permute-done | bytes 344096 | tf_op jit(solution)/shard_map/ppermute | solution.py:18
  779.4 25.0 %collective-permute-done.35 = f32[2,24,1792]{2,1,0:T(8,128)S(1)} collective-permute-done((f32[2,24,1792]{2,1,0:T(8,128)S(1)}, f32[2,24,1792]{2,1,0:T(8,128)S(1)}, u32[]{:S(2)}, u32[]{:S(2)}) %collective-permute-start.35) | collective-permute-done | bytes 344096 | tf_op jit(solution)/shard_map/ppermute | solution.py:18
  807.3 24.4 %collective-permute-done.40 = f32[2,24,1792]{2,1,0:T(8,128)S(1)} collective-permute-done((f32[2,24,1792]{2,1,0:T(8,128)S(1)}, f32[2,24,1792]{2,1,0:T(8,128)S(1)}, u32[]{:S(2)}, u32[]{:S(2)}) %collective-permute-start.40) | collective-permute-done | bytes 344096 | tf_op jit(solution)/shard_map/ppermute | solution.py:18
  835.4 12.4 %while.34 = (s32[]{:T(128)}, f32[2,256,256]{2,1,0:T(8,128)S(1)}, s32[]{:T(128)}, s32[4,2]{0,1:T(2,128)S(1)}, s32[]{:T(128)}, /*index=5*/f32[2,344,1792]{2,1,0:T(...) while((s32[]{:T(128)}, f32[2,256,256]{2,1,0:T(8,128)S(1)}, ...), condition=%wide.region_10.11_spmd, body=%wide.region_9.10_spmd.sunk | while | flops 655373 | bytes 3146027 | solution.py:160
  848.5 213.8 %all-reduce.3.cloned.1.call-done = (f32[2,4,256,256]{3,2,0,1:T(8,128)}, f32[256,256]{1,0:T(8,128)}) async-done(((f32[2,4,256,256]{3,2,0,1:T(8,128)}, f32[256,256]{1,0:T(8,128)}), (f32[2,4,256,256]{3,2,0,1:T(8,128)}, f32[256,256]{1,0:T(8,128)})) %all-reduce.3.cloned.1.call-update) | async-done | bytes 2359312 | tf_op jit(solution)/shard_map/psum | solution.py:166
  1072.2 12.9 %psum.37 = f32[5]{0:T(128)S(1)} all-reduce(f32[5]{0:T(128)S(1)} %stack.185), channel_id=1, replica_groups=mesh['groups'=2,'scan_0'=8,'scan_1'=8,'scan_2'=2] {'scan_0'}, use_global_device_ids=true, to_apply=%region_15.16 | all-reduce | flops 5 | bytes 40 | tf_op jit(solution)/shard_map/psum | solution.py:23
  1085.1 14.0 %psum.38 = f32[5]{0:T(128)S(1)} all-reduce(f32[5]{0:T(128)S(1)} %psum.37), channel_id=1, replica_groups=mesh['groups'=2,'scan_0'=8,'scan_1'=8,'scan_2'=2] {'scan_1'}, use_global_device_ids=true, to_apply=%region_16.17 | all-reduce | flops 5 | bytes 40 | tf_op jit(solution)/shard_map/psum | solution.py:23
  1099.1 8.4 psum.39
  (212 shorter events, 154.3 us)
Async XLA Ops:
  7.2 1055.2 %all-reduce.3.cloned.1.call-start = ((), (), s32[]{:S(2)}) async-start(), calls=%async_computation | async-start | bytes 4718592 | tf_op jit(solution)/shard_map/psum | solution.py:166
  7.3 49.2 %collective-permute-start.1 = (f32[2,24,1792]{2,1,0:T(8,128)}, f32[2,24,1792]{2,1,0:T(8,128)}, u32[]{:S(2)}, u32[]{:S(2)}) collective-permute-start(f32[2,24,1792]{2,1,0:T(8,128)} %param.23), channel_id=1, source_target_pairs={{0,3},{1,4},{2,5},{3,6},{4,7},{5,8},{6,9},{7,10},{8,11},{9,12},{10... | collective-permute-start | bytes 1032200 | tf_op jit(solution)/shard_map/ppermute | solution.py:18
  16.1 43.5 %collective-permute-start.2 = (f32[2,24,1792]{2,1,0:T(8,128)}, f32[2,24,1792]{2,1,0:T(8,128)}, u32[]{:S(2)}, u32[]{:S(2)}) collective-permute-start(f32[2,24,1792]{2,1,0:T(8,128)} %param.23), channel_id=1, source_target_pairs={{0,2},{1,3},{2,4},{3,5},{4,6},{5,7},{6,8},{7,9},{8,10},{9,11},{10,... | collective-permute-start | bytes 1032200 | tf_op jit(solution)/shard_map/ppermute | solution.py:18
  20.5 42.1 %collective-permute-start.3 = (f32[2,24,1792]{2,1,0:T(8,128)}, f32[2,24,1792]{2,1,0:T(8,128)}, u32[]{:S(2)}, u32[]{:S(2)}) collective-permute-start(f32[2,24,1792]{2,1,0:T(8,128)} %param.23), channel_id=1, source_target_pairs={{0,1},{1,2},{2,3},{3,4},{4,5},{5,6},{6,7},{7,8},{8,9},{9,10},{10,1... | collective-permute-start | bytes 1032200 | tf_op jit(solution)/shard_map/ppermute | solution.py:18
  22.5 44.0 %collective-permute-start.4 = (f32[2,24,1792]{2,1,0:T(8,128)}, f32[2,24,1792]{2,1,0:T(8,128)}, u32[]{:S(2)}, u32[]{:S(2)}) collective-permute-start(f32[2,24,1792]{2,1,0:T(8,128)} %param.23), channel_id=1, source_target_pairs={{1,0},{2,1},{3,2},{4,3},{5,4},{6,5},{7,6},{8,7},{9,8},{10,9},{11,1... | collective-permute-start | bytes 1032200 | tf_op jit(solution)/shard_map/ppermute | solution.py:18
  56.5 90.5 %collective-permute-start.6 = (f32[2,24,1792]{2,1,0:T(8,128)S(1)}, f32[2,24,1792]{2,1,0:T(8,128)S(1)}, u32[]{:S(2)}, u32[]{:S(2)}) collective-permute-start(f32[2,24,1792]{2,1,0:T(8,128)S(1)} %copy-done.8), channel_id=1, source_target_pairs={{3,0},{4,1},{5,2},{6,3},{7,4},{8,5},{9,6},{10,7},{11,8},{12,9},{13... | collective-permute-start | bytes 1032200 | tf_op jit(solution)/shard_map/ppermute | solution.py:18
  59.6 131.9 %collective-permute-start.7 = (f32[2,24,1792]{2,1,0:T(8,128)S(1)}, f32[2,24,1792]{2,1,0:T(8,128)S(1)}, u32[]{:S(2)}, u32[]{:S(2)}) collective-permute-start(f32[2,24,1792]{2,1,0:T(8,128)S(1)} %copy-done.8), channel_id=1, source_target_pairs={{4,0},{5,1},{6,2},{7,3},{8,4},{9,5},{10,6},{11,7},{12,8},{13,9},{1... | collective-permute-start | bytes 1032200 | tf_op jit(solution)/shard_map/ppermute | solution.py:18
  62.7 130.9 %collective-permute-start.8 = (f32[2,24,1792]{2,1,0:T(8,128)S(1)}, f32[2,24,1792]{2,1,0:T(8,128)S(1)}, u32[]{:S(2)}, u32[]{:S(2)}) collective-permute-start(f32[2,24,1792]{2,1,0:T(8,128)S(1)} %copy-done.8), channel_id=1, source_target_pairs={{5,0},{6,1},{7,2},{8,3},{9,4},{10,5},{11,6},{12,7},{13,8},{14,9},{... | collective-permute-start | bytes 1032200 | tf_op jit(solution)/shard_map/ppermute | solution.py:18
  66.4 129.2 %collective-permute-start.9 = (f32[2,24,1792]{2,1,0:T(8,128)S(1)}, f32[2,24,1792]{2,1,0:T(8,128)S(1)}, u32[]{:S(2)}, u32[]{:S(2)}) collective-permute-start(f32[2,24,1792]{2,1,0:T(8,128)S(1)} %copy-done.8), channel_id=1, source_target_pairs={{6,0},{7,1},{8,2},{9,3},{10,4},{11,5},{12,6},{13,7},{14,8},{15,9},... | collective-permute-start | bytes 1032200 | tf_op jit(solution)/shard_map/ppermute | solution.py:18
  79.5 116.9 %collective-permute-start.10 = (f32[2,24,1792]{2,1,0:T(8,128)S(1)}, f32[2,24,1792]{2,1,0:T(8,128)S(1)}, u32[]{:S(2)}, u32[]{:S(2)}) collective-permute-start(f32[2,24,1792]{2,1,0:T(8,128)S(1)} %copy-done.8), channel_id=1, source_target_pairs={{7,0},{8,1},{9,2},{10,3},{11,4},{12,5},{13,6},{14,7},{15,8},{16,9}... | collective-permute-start | bytes 1032200 | tf_op jit(solution)/shard_map/ppermute | solution.py:18
  147.0 50.2 %collective-permute-start.11 = (f32[2,24,1792]{2,1,0:T(8,128)S(1)}, f32[2,24,1792]{2,1,0:T(8,128)S(1)}, u32[]{:S(2)}, u32[]{:S(2)}) collective-permute-start(f32[2,24,1792]{2,1,0:T(8,128)S(1)} %copy-done.8), channel_id=1, source_target_pairs={{8,0},{9,1},{10,2},{11,3},{12,4},{13,5},{14,6},{15,7},{16,8},{17,9... | collective-permute-start | bytes 1032200 | tf_op jit(solution)/shard_map/ppermute | solution.py:18
  300.8 88.9 %collective-permute-start.15 = (f32[3,24,1792]{2,1,0:T(8,128)S(1)}, f32[3,24,1792]{2,1,0:T(8,128)S(1)}, u32[]{:S(2)}, u32[]{:S(2)}) collective-permute-start(f32[3,24,1792]{2,1,0:T(8,128)S(1)} %get-tuple-element.401), channel_id=1, source_target_pairs={{3,0},{4,1},{5,2},{6,3},{7,4},{8,5},{9,6},{10,7},{11,8},{12,9},{13... | collective-permute-start | bytes 1548296 | tf_op jit(solution)/shard_map/ppermute | solution.py:18
  302.1 105.1 %collective-permute-start.16 = (f32[3,24,1792]{2,1,0:T(8,128)S(1)}, f32[3,24,1792]{2,1,0:T(8,128)S(1)}, u32[]{:S(2)}, u32[]{:S(2)}) collective-permute-start(f32[3,24,1792]{2,1,0:T(8,128)S(1)} %get-tuple-element.413), channel_id=1, source_target_pairs={{2,0},{3,1},{4,2},{5,3},{6,4},{7,5},{8,6},{9,7},{10,8},{11,9},{12,... | collective-permute-start | bytes 1548296 | tf_op jit(solution)/shard_map/ppermute | solution.py:18
  303.5 119.7 %collective-permute-start.17 = (f32[3,24,1792]{2,1,0:T(8,128)S(1)}, f32[3,24,1792]{2,1,0:T(8,128)S(1)}, u32[]{:S(2)}, u32[]{:S(2)}) collective-permute-start(f32[3,24,1792]{2,1,0:T(8,128)S(1)} %get-tuple-element.412), channel_id=1, source_target_pairs={{1,0},{2,1},{3,2},{4,3},{5,4},{6,5},{7,6},{8,7},{9,8},{10,9},{11,1... | collective-permute-start | bytes 1548296 | tf_op jit(solution)/shard_map/ppermute | solution.py:18
  306.3 55.3 %collective-permute-start.14 = (f32[3,8,1792]{2,1,0:T(8,128)S(1)}, f32[3,8,1792]{2,1,0:T(8,128)S(1)}, u32[]{:S(2)}, u32[]{:S(2)}) collective-permute-start(f32[3,8,1792]{2,1,0:T(8,128)S(1)} %slice.305), channel_id=1, source_target_pairs={{4,0},{5,1},{6,2},{7,3},{8,4},{9,5},{10,6},{11,7},{12,8},{13,9},{1... | collective-permute-start | bytes 516104 | tf_op jit(solution)/shard_map/ppermute | solution.py:18
  307.7 122.4 %collective-permute-start.18 = (f32[3,24,1792]{2,1,0:T(8,128)S(1)}, f32[3,24,1792]{2,1,0:T(8,128)S(1)}, u32[]{:S(2)}, u32[]{:S(2)}) collective-permute-start(f32[3,24,1792]{2,1,0:T(8,128)S(1)} %get-tuple-element.411), channel_id=1, source_target_pairs={{0,1},{1,2},{2,3},{3,4},{4,5},{5,6},{6,7},{7,8},{8,9},{9,10},{10,1... | collective-permute-start | bytes 1548296 | tf_op jit(solution)/shard_map/ppermute | solution.py:18
  361.7 70.8 %collective-permute-start.19 = (f32[3,24,1792]{2,1,0:T(8,128)S(1)}, f32[3,24,1792]{2,1,0:T(8,128)S(1)}, u32[]{:S(2)}, u32[]{:S(2)}) collective-permute-start(f32[3,24,1792]{2,1,0:T(8,128)S(1)} %get-tuple-element.410), channel_id=1, source_target_pairs={{0,2},{1,3},{2,4},{3,5},{4,6},{5,7},{6,8},{7,9},{8,10},{9,11},{10,... | collective-permute-start | bytes 1548296 | tf_op jit(solution)/shard_map/ppermute | solution.py:18
  389.8 44.9 %collective-permute-start.20 = (f32[3,24,1792]{2,1,0:T(8,128)S(1)}, f32[3,24,1792]{2,1,0:T(8,128)S(1)}, u32[]{:S(2)}, u32[]{:S(2)}) collective-permute-start(f32[3,24,1792]{2,1,0:T(8,128)S(1)} %get-tuple-element.409), channel_id=1, source_target_pairs={{0,3},{1,4},{2,5},{3,6},{4,7},{5,8},{6,9},{7,10},{8,11},{9,12},{10... | collective-permute-start | bytes 1548296 | tf_op jit(solution)/shard_map/ppermute | solution.py:18
  407.2 50.2 %collective-permute-start.21 = (f32[3,24,1792]{2,1,0:T(8,128)S(1)}, f32[3,24,1792]{2,1,0:T(8,128)S(1)}, u32[]{:S(2)}, u32[]{:S(2)}) collective-permute-start(f32[3,24,1792]{2,1,0:T(8,128)S(1)} %get-tuple-element.408), channel_id=1, source_target_pairs={{0,4},{1,5},{2,6},{3,7},{4,8},{5,9},{6,10},{7,11},{8,12},{9,13},{1... | collective-permute-start | bytes 1548296 | tf_op jit(solution)/shard_map/ppermute | solution.py:18
  423.2 67.6 %collective-permute-start.22 = (f32[3,24,1792]{2,1,0:T(8,128)S(1)}, f32[3,24,1792]{2,1,0:T(8,128)S(1)}, u32[]{:S(2)}, u32[]{:S(2)}) collective-permute-start(f32[3,24,1792]{2,1,0:T(8,128)S(1)} %get-tuple-element.407), channel_id=1, source_target_pairs={{0,5},{1,6},{2,7},{3,8},{4,9},{5,10},{6,11},{7,12},{8,13},{9,14},{... | collective-permute-start | bytes 1548296 | tf_op jit(solution)/shard_map/ppermute | solution.py:18
  430.1 64.6 %collective-permute-start.23 = (f32[3,24,1792]{2,1,0:T(8,128)}, f32[3,24,1792]{2,1,0:T(8,128)}, u32[]{:S(2)}, u32[]{:S(2)}) collective-permute-start(f32[3,24,1792]{2,1,0:T(8,128)} %get-tuple-element.406), channel_id=1, source_target_pairs={{0,6},{1,7},{2,8},{3,9},{4,10},{5,11},{6,12},{7,13},{8,14},{9,15},... | collective-permute-start | bytes 1548296 | tf_op jit(solution)/shard_map/ppermute | solution.py:18
  432.5 62.2 %collective-permute-start.24 = (f32[3,24,1792]{2,1,0:T(8,128)}, f32[3,24,1792]{2,1,0:T(8,128)}, u32[]{:S(2)}, u32[]{:S(2)}) collective-permute-start(f32[3,24,1792]{2,1,0:T(8,128)} %get-tuple-element.405), channel_id=1, source_target_pairs={{0,7},{1,8},{2,9},{3,10},{4,11},{5,12},{6,13},{7,14},{8,15},{9,16}... | collective-permute-start | bytes 1548296 | tf_op jit(solution)/shard_map/ppermute | solution.py:18
  434.6 60.1 %collective-permute-start.25 = (f32[3,24,1792]{2,1,0:T(8,128)}, f32[3,24,1792]{2,1,0:T(8,128)}, u32[]{:S(2)}, u32[]{:S(2)}) collective-permute-start(f32[3,24,1792]{2,1,0:T(8,128)} %get-tuple-element.404), channel_id=1, source_target_pairs={{0,8},{1,9},{2,10},{3,11},{4,12},{5,13},{6,14},{7,15},{8,16},{9,17... | collective-permute-start | bytes 1548296 | tf_op jit(solution)/shard_map/ppermute | solution.py:18
  457.4 76.2 %collective-permute-start.26 = (f32[3,24,1792]{2,1,0:T(8,128)S(1)}, f32[3,24,1792]{2,1,0:T(8,128)}, u32[]{:S(2)}, u32[]{:S(2)}) collective-permute-start(f32[3,24,1792]{2,1,0:T(8,128)S(1)} %get-tuple-element.403), channel_id=1, source_target_pairs={{0,9},{1,10},{2,11},{3,12},{4,13},{5,14},{6,15},{7,16},{8,17},{9,1... | collective-permute-start | bytes 1548296 | tf_op jit(solution)/shard_map/ppermute | solution.py:18
  491.6 47.5 %collective-permute-start.27 = (f32[3,24,1792]{2,1,0:T(8,128)S(1)}, f32[3,24,1792]{2,1,0:T(8,128)}, u32[]{:S(2)}, u32[]{:S(2)}) collective-permute-start(f32[3,24,1792]{2,1,0:T(8,128)S(1)} %get-tuple-element.402), channel_id=1, source_target_pairs={{0,10},{1,11},{2,12},{3,13},{4,14},{5,15},{6,16},{7,17},{8,18},{9,... | collective-permute-start | bytes 1548296 | tf_op jit(solution)/shard_map/ppermute | solution.py:18
  542.2 62.1 %collective-permute-start.29 = (f32[2,24,1792]{2,1,0:T(8,128)S(1)}, f32[2,24,1792]{2,1,0:T(8,128)S(1)}, u32[]{:S(2)}, u32[]{:S(2)}) collective-permute-start(f32[2,24,1792]{2,1,0:T(8,128)S(1)} %slice_divide_fusion), channel_id=1, source_target_pairs={{0,3},{1,4},{2,5},{3,6},{4,7},{5,8},{6,9},{7,10},{8,11},{9,12},{10... | collective-permute-start | bytes 1032200 | tf_op jit(solution)/shard_map/ppermute | solution.py:18
  602.9 51.0 %collective-permute-start.33 = (f32[2,24,1792]{2,1,0:T(8,128)S(1)}, f32[2,24,1792]{2,1,0:T(8,128)S(1)}, u32[]{:S(2)}, u32[]{:S(2)}) collective-permute-start(f32[2,24,1792]{2,1,0:T(8,128)S(1)} %slice_divide_fusion), channel_id=1, source_target_pairs={{2,0},{3,1},{4,2},{5,3},{6,4},{7,5},{8,6},{9,7},{10,8},{11,9},{12,... | collective-permute-start | bytes 1032200 | tf_op jit(solution)/shard_map/ppermute | solution.py:18
  604.3 173.8 %collective-permute-start.34 = (f32[2,24,1792]{2,1,0:T(8,128)S(1)}, f32[2,24,1792]{2,1,0:T(8,128)S(1)}, u32[]{:S(2)}, u32[]{:S(2)}) collective-permute-start(f32[2,24,1792]{2,1,0:T(8,128)S(1)} %slice_divide_fusion), channel_id=1, source_target_pairs={{3,0},{4,1},{5,2},{6,3},{7,4},{8,5},{9,6},{10,7},{11,8},{12,9},{13... | collective-permute-start | bytes 1032200 | tf_op jit(solution)/shard_map/ppermute | solution.py:18
  605.6 198.8 %collective-permute-start.35 = (f32[2,24,1792]{2,1,0:T(8,128)S(1)}, f32[2,24,1792]{2,1,0:T(8,128)S(1)}, u32[]{:S(2)}, u32[]{:S(2)}) collective-permute-start(f32[2,24,1792]{2,1,0:T(8,128)S(1)} %slice_divide_fusion), channel_id=1, source_target_pairs={{4,0},{5,1},{6,2},{7,3},{8,4},{9,5},{10,6},{11,7},{12,8},{13,9},{1... | collective-permute-start | bytes 1032200 | tf_op jit(solution)/shard_map/ppermute | solution.py:18
  607.0 198.8 %collective-permute-start.36 = (f32[2,24,1792]{2,1,0:T(8,128)S(1)}, f32[2,24,1792]{2,1,0:T(8,128)S(1)}, u32[]{:S(2)}, u32[]{:S(2)}) collective-permute-start(f32[2,24,1792]{2,1,0:T(8,128)S(1)} %slice_divide_fusion), channel_id=1, source_target_pairs={{5,0},{6,1},{7,2},{8,3},{9,4},{10,5},{11,6},{12,7},{13,8},{14,9},{... | collective-permute-start | bytes 1032200 | tf_op jit(solution)/shard_map/ppermute | solution.py:18
  608.4 198.8 %collective-permute-start.37 = (f32[2,24,1792]{2,1,0:T(8,128)S(1)}, f32[2,24,1792]{2,1,0:T(8,128)S(1)}, u32[]{:S(2)}, u32[]{:S(2)}) collective-permute-start(f32[2,24,1792]{2,1,0:T(8,128)S(1)} %slice_divide_fusion), channel_id=1, source_target_pairs={{6,0},{7,1},{8,2},{9,3},{10,4},{11,5},{12,6},{13,7},{14,8},{15,9},... | collective-permute-start | bytes 1032200 | tf_op jit(solution)/shard_map/ppermute | solution.py:18
  654.0 153.2 %collective-permute-start.38 = (f32[2,24,1792]{2,1,0:T(8,128)S(1)}, f32[2,24,1792]{2,1,0:T(8,128)S(1)}, u32[]{:S(2)}, u32[]{:S(2)}) collective-permute-start(f32[2,24,1792]{2,1,0:T(8,128)S(1)} %slice_divide_fusion), channel_id=1, source_target_pairs={{7,0},{8,1},{9,2},{10,3},{11,4},{12,5},{13,6},{14,7},{15,8},{16,9}... | collective-permute-start | bytes 1032200 | tf_op jit(solution)/shard_map/ppermute | solution.py:18
  (34 other events, 702.3 us)
Sparse Core Ops, SparseCore 0:
  493.9 568.4 all-reduce.2
where the time goes:
time: 1130 us; the launch traced here: 1120 us
  waiting for transfers between devices  672 us (59%)
  starting transfers between devices  254 us (22%)
  local copies, waits for them, and re-layouts  67.5 us (6%)
  other arithmetic  42.3 us (4%)
  blocking collectives  35.3 us (3%)
  between operations  21.1 us (2%)
  matrix products  16.8 us (1%)
  loops' own time  14.8 us (1%)
    ppermute x42, waiting for transfers between devices, from_behind(): return lax.ppermute(shard, axis, pairs)  458 us
    ppermute x42, starting transfers between devices, from_behind(): return lax.ppermute(shard, axis, pairs)  253 us
    psum x1, waiting for transfers between devices, on_device(): summed_probe, summed_norm = lax.psum((grad_probe, obj_norm), SCAN)  214 us
    psum x3, blocking collectives, one_axis_at_a_time(): shard = lax.psum(shard, axis)  35.3 us
  transfers between devices with their start and end apart: 43, of which 15 were waited for; matrix products, arithmetic and copies ran while one was open for 4% of the time, Pallas kernels for 0%

commit v1 on v0

v1 whole, which is shorter than its diff:
```python
import functools
import math

import jax
import jax.numpy as jnp
import numpy as np
from jax import lax
from jax.experimental import pallas as pl
from jax.experimental.pallas import tpu as pltpu
from jax.sharding import PartitionSpec as P

MESH = pl.DeviceIdType.MESH
SPLIT = 4
JITTER = 8
STEP = 96
PATCH = 256
MODES = 4
STRIP = 24
LANES = 128
OWN = 512
WIN = 640
ROWS = JITTER + 2 * STEP + 72
ZTOP = 104
KROWS = 408
KCOLS = 384
F32 = jnp.float32
BF16 = jnp.bfloat16


def mult(value, of):
    return pl.multiple_of(value, of)


class Messages:
    def __init__(self, send, recv):
        self.send, self.recv, self.count, self.open = send, recv, 0, []

    def make(self, src, dst, scan, when=None):
        at = self.count
        self.count += 1
        copy = pltpu.make_async_remote_copy(
            src_ref=src,
            dst_ref=dst,
            send_sem=self.send.at[at],
            recv_sem=self.recv.at[at],
            device_id={"scan": scan},
            device_id_type=MESH,
        )
        self.open.append((copy, when))
        return copy

    def drain(self):
        for copy, when in self.open:
            if when is None:
                copy.wait_send()
            else:
                pl.when(when)(copy.wait_send)


def greet(peers):
    barrier = pltpu.get_barrier_semaphore()
    for peer in peers:
        pl.semaphore_signal(barrier, inc=1, device_id={"scan": peer}, device_id_type=MESH)
    pl.semaphore_wait(barrier, len(peers))


def gather_kernel(n, obj, meta, own, sib, metas, send, recv, msend, mrecv):
    me = lax.axis_index("scan")
    q = me % SPLIT
    core = me % 2
    first = me - q
    up = (me - SPLIT + n) % n
    down = (me + SPLIT) % n
    sibling = me + 1 - 2 * core
    msg = Messages(send, recv)
    peers = [(first + SPLIT * e + k + 2 * n) % n for e in (-2, -1, 1, 2) for k in range(SPLIT)]
    peers += [first + (q + k) % SPLIT for k in range(1, SPLIT)]
    greet(peers)

    def columns(quarter):
        return pl.ds(mult(768 * (quarter // 2) + OWN * (quarter % 2), LANES), OWN)

    def rows(start, size):
        return pl.ds(mult(start, 8), size)

    own[:, rows(JITTER + STRIP * q, STRIP), :] = obj[:, :, columns(q)]
    strips = []
    for k in range(1, SPLIT):
        there = (q + k) % SPLIT
        copy = msg.make(
            obj.at[:, :, columns(there)],
            own.at[:, rows(JITTER + STRIP * q, STRIP), :],
            first + there,
        )
        copy.start()
        strips.append(copy)
    metas[2 * SPLIT + q] = meta[...]
    meta_copies = []
    for e in (-1, 0, 1, 2):
        for k in range(SPLIT):
            if e == 0 and k == 0:
                continue
            there = (first + SPLIT * e + (q + k) % SPLIT + n) % n
            at = len(meta_copies)
            copy = pltpu.make_async_remote_copy(
                src_ref=meta,
                dst_ref=metas.at[(2 - e) * SPLIT + q],
                send_sem=msend.at[at],
                recv_sem=mrecv,
                device_id={"scan": there},
                device_id_type=MESH,
            )
            copy.start()
            meta_copies.append(copy)

    ahead = []
    for k in range(SPLIT):
        if k > 0:
            strips[k - 1].wait_recv()
        strip = (q - k + SPLIT) % SPLIT
        copy = msg.make(
            own.at[:, rows(JITTER + STRIP * strip, STRIP), :] if k else obj.at[:, :, columns(q)],
            own.at[:, rows(JITTER + STEP + STRIP * strip, STRIP), :],
            up,
        )
        copy.start()
        ahead.append(copy)
    tail = msg.make(own.at[:, rows(STEP, JITTER), :], own.at[:, rows(0, JITTER), :], down)
    tail.start()
    edge = pl.ds(mult(384 * (1 - core), LANES), LANES)

    def border(start, size):
        copy = msg.make(
            own.at[:, pl.ds(start, size), edge], sib.at[:, pl.ds(start, size), :], sibling
        )
        copy.start()
        return copy

    borders = [border(JITTER, STEP)]
    relays = []
    for k in range(SPLIT):
        ahead[k].wait_recv()
        strip = (q - k + SPLIT) % SPLIT
        low = jnp.minimum(strip, SPLIT - 2)
        copy = msg.make(
            own.at[:, rows(JITTER + STEP + STRIP * low, STRIP), :],
            own.at[:, rows(JITTER + 2 * STEP + STRIP * low, STRIP), :],
            up,
            when=strip != SPLIT - 1,
        )
        pl.when(strip != SPLIT - 1)(copy.start)
        relays.append((copy, strip != SPLIT - 1))
    borders.append(border(JITTER + STEP, STEP))
    tail.wait_recv()
    for copy, when in relays:
        pl.when(when)(copy.wait_recv)
    borders.append(border(0, JITTER))
    borders.append(border(JITTER + 2 * STEP, 72))
    for copy in borders:
        copy.wait_recv()
    pltpu.make_async_copy(metas.at[pl.ds(0, 15)], metas.at[pl.ds(0, 15)], mrecv).wait()
    msg.drain()
    for copy in meta_copies:
        copy.wait_send()


def gather(n, obj, meta):
    vmem = pl.BlockSpec(memory_space=pltpu.VMEM)
    return pl.pallas_call(
        functools.partial(gather_kernel, n),
        out_shape=(
            jax.ShapeDtypeStruct((2, ROWS, OWN), F32),
            jax.ShapeDtypeStruct((2, ROWS, LANES), F32),
            jax.ShapeDtypeStruct((4 * SPLIT, 8, LANES), jnp.int32),
        ),
        in_specs=[vmem] * 2,
        out_specs=[vmem] * 3,
        scratch_shapes=[
            pltpu.SemaphoreType.DMA((16,)),
            pltpu.SemaphoreType.DMA((16,)),
            pltpu.SemaphoreType.DMA((16,)),
            pltpu.SemaphoreType.DMA,
        ],
        compiler_params=pltpu.CompilerParams(collective_id=0, has_side_effects=True),
        name="gather_window",
    )(obj, meta)


def spread(n, kernel_pad, out, metas):
    me = lax.axis_index("scan")
    row = me // SPLIT
    parts = out.shape[0]
    out[...] = jnp.zeros_like(out)

    def one(at, carry):
        line, col = at // 16, at % 16
        slot = line * SPLIT + col // SPLIT
        place = col % SPLIT
        top = metas[slot, 2 * place]
        left = metas[slot, 2 * place + 1]
        there = row - 2 + line
        inside = jnp.logical_and(there >= 0, there < n // SPLIT)
        weight = jnp.where(jnp.logical_and(inside, place < metas[slot, 8]), 1.0, 0.0).astype(F32)
        start = mult(STRIP * (me % SPLIT) + STEP * (2 - line) - JITTER + ZTOP, 8)
        ahead = jnp.clip(STEP * there - top + JITTER, 0, 2 * JITTER)
        base = mult((STEP * col + 40) // LANES * LANES, LANES)
        shift = jnp.clip(left - base, 0, LANES)
        for part in range(parts):
            value = kernel_pad[part, pl.ds(start, STRIP + 2 * JITTER), :]
            value = pltpu.roll(value, (STRIP + 2 * JITTER - ahead) % (STRIP + 2 * JITTER), 0)[0:STRIP]
            value = pltpu.roll(value, shift, 1) * weight
            out[part, :, pl.ds(base, KCOLS)] += value
        return carry

    lax.fori_loop(0, 4 * 16, one, 0)


def position_kernel(
    n, metas, own, sib, probe, amps, cos, sin, g_own, g_sib, q_out, illum,
    win, grad, patch, wave, half, far, acc, kpad, ta, tb,
):
    me = lax.axis_index("scan")
    row = me // SPLIT
    q = me % SPLIT
    core = me % 2
    total = n * STRIP
    c, s = cos[...], sin[...]
    ta[0:256, 0:256] = c
    ta[0:256, 256:512] = s
    ta[256:512, 0:256] = -s
    ta[256:512, 256:512] = c
    tb[0:256, 0:256] = c
    tb[0:256, 256:512] = -s
    tb[256:512, 0:256] = s
    tb[256:512, 256:512] = c

    def valid(width):
        at = lax.broadcasted_iota(jnp.int32, (ROWS, width), 0) + (STEP * row - JITTER)
        return jnp.logical_and(at >= 0, at < total)

    own_at = mult(LANES * core, LANES)
    sib_at = mult(OWN * (1 - core), LANES)
    for part in range(2):
        win[part, 0:ROWS, pl.ds(own_at, OWN)] = jnp.where(valid(OWN), own[part], 0.0)
        win[part, 0:ROWS, pl.ds(sib_at, LANES)] = jnp.where(valid(LANES), sib[part], 0.0)
    win[:, ROWS:, :] = jnp.zeros((2, 8, WIN), F32)
    grad[...] = jnp.zeros_like(grad)
    acc[...] = jnp.zeros_like(acc)
    kpad[...] = jnp.zeros_like(kpad)
    light = jnp.zeros((PATCH, PATCH), F32)
    for m in range(MODES):
        light = light + (probe[0, m] * probe[0, m] + probe[1, m] * probe[1, m])
    kpad[0, ZTOP : ZTOP + PATCH, 0:PATCH] = light
    spread(n, kpad, illum, metas)

    chunk = 32
    chunks = PATCH // chunk
    slot = 2 * SPLIT + q

    def transform(left, right):
        for m in range(MODES):
            cols = slice(m * PATCH, (m + 1) * PATCH)
            y = jnp.dot(left[...], wave[:, cols], preferred_element_type=F32)
            half[cols, 0:PATCH] = y[0:PATCH].astype(BF16)
            half[cols, PATCH : 2 * PATCH] = y[PATCH : 2 * PATCH].astype(BF16)
        for m in range(MODES):
            cols = slice(m * PATCH, (m + 1) * PATCH)
            far[m] = jnp.dot(half[cols, :], right[...], preferred_element_type=F32)

    def visit(p, carry):
        down = metas[slot, 2 * p] - (STEP * row - JITTER)
        off = down % 8
        base = mult((STEP * p + 40) // LANES * LANES, LANES)
        shift = metas[slot, 2 * p + 1] - STEP * SPLIT * q - base

        def exits(i, carry):
            rows = pl.ds(mult(i * chunk, chunk), chunk)
            low = pl.ds(mult(PATCH + i * chunk, chunk), chunk)
            o = []
            for part in range(2):
                v = win[part, pl.ds(mult(down - off + i * chunk, 8), chunk + 8), pl.ds(base, KCOLS)]
                v = pltpu.roll(v, (chunk + 8 - off) % (chunk + 8), 0)[0:chunk]
                v = pltpu.roll(v, KCOLS - shift, 1)[:, 0:PATCH]
                patch[part, rows, :] = v
                o.append(v)
            for m in range(MODES):
                pr, pi = probe[0, m, rows, :], probe[1, m, rows, :]
                wave[rows, m * PATCH : (m + 1) * PATCH] = (pr * o[0] - pi * o[1]).astype(BF16)
                wave[low, m * PATCH : (m + 1) * PATCH] = (pr * o[1] + pi * o[0]).astype(BF16)
            return carry

        lax.fori_loop(0, chunks, exits, 0)
        transform(ta, tb)

        def changes(i, carry):
            rows = pl.ds(mult(i * chunk, chunk), chunk)
            low = pl.ds(mult(PATCH + i * chunk, chunk), chunk)
            bright = jnp.zeros((chunk, PATCH), F32)
            for m in range(MODES):
                fr, fi = far[m, rows, 0:PATCH], far[m, rows, PATCH : 2 * PATCH]
                bright = bright + (fr * fr + fi * fi)
            factor = amps[p, rows, :] / jnp.maximum(jnp.sqrt(bright), 0.5) - 1.0
            for m in range(MODES):
                fr, fi = far[m, rows, 0:PATCH], far[m, rows, PATCH : 2 * PATCH]
                wave[rows, m * PATCH : (m + 1) * PATCH] = (fr * factor).astype(BF16)
                wave[low, m * PATCH : (m + 1) * PATCH] = (fi * factor).astype(BF16)
            return carry

        lax.fori_loop(0, chunks, changes, 0)
        transform(tb, ta)

        def grads(i, carry):
            rows = pl.ds(mult(i * chunk, chunk), chunk)
            o_re, o_im = patch[0, rows, :], patch[1, rows, :]
            g_re = jnp.zeros((chunk, PATCH), F32)
            g_im = jnp.zeros((chunk, PATCH), F32)
            for m in range(MODES):
                pr, pi = probe[0, m, rows, :], probe[1, m, rows, :]
                cr, ci = far[m, rows, 0:PATCH], far[m, rows, PATCH : 2 * PATCH]
                g_re = g_re + (pr * cr + pi * ci)
                g_im = g_im + (pr * ci - pi * cr)
                acc[m, rows, :] += o_re * cr + o_im * ci
                acc[MODES + m, rows, :] += o_re * ci - o_im * cr
            acc[2 * MODES, rows, :] += o_re * o_re + o_im * o_im
            blank = jnp.zeros((chunk, KCOLS - PATCH), F32)
            below = jnp.zeros((8, KCOLS), F32)
            for part, g in enumerate((g_re, g_im)):
                v = pltpu.roll(jnp.concatenate([g, blank], 1), shift, 1)
                v = pltpu.roll(jnp.concatenate([v, below], 0), off, 0)
                grad[part, pl.ds(mult(down - off + i * chunk, 8), chunk + 8), pl.ds(base, KCOLS)] += v
            return carry

        lax.fori_loop(0, chunks, grads, 0)
        return carry

    lax.fori_loop(0, metas[slot, 8], visit, 0)

    for part in range(2):
        g_own[part] = jnp.where(valid(OWN), grad[part, 0:ROWS, pl.ds(own_at, OWN)], 0.0)
        g_sib[part] = jnp.where(valid(LANES), grad[part, 0:ROWS, pl.ds(sib_at, LANES)], 0.0)
    for band in range(PATCH // 8):
        y = (band // 2) % 8
        for side in range(2):
            x = (band // 16) * 4 + (band % 2) * 2 + side
            rows, cols = slice(8 * band, 8 * band + 8), slice(LANES * side, LANES * side + LANES)
            for k in range(2):
                for i, m in enumerate((2 * k, 2 * k + 1, MODES + 2 * k, MODES + 2 * k + 1, 8)):
                    q_out[k, x, y, i] = acc[m, rows, cols]


def positions(n, metas, own, sib, probe, amps, cos, sin):
    vmem = pl.BlockSpec(memory_space=pltpu.VMEM)
    return pl.pallas_call(
        functools.partial(position_kernel, n),
        out_shape=(
            jax.ShapeDtypeStruct((2, ROWS, OWN), F32),
            jax.ShapeDtypeStruct((2, ROWS, LANES), F32),
            jax.ShapeDtypeStruct((2, 8, 8, 5, 8, LANES), F32),
            jax.ShapeDtypeStruct((1, STRIP, 14 * LANES), F32),
        ),
        in_specs=[pl.BlockSpec(memory_space=pltpu.SMEM)] + [vmem] * 6,
        out_specs=[vmem] * 4,
        scratch_shapes=[
            pltpu.VMEM((2, ROWS + 8, WIN), F32),
            pltpu.VMEM((2, ROWS + 8, WIN), F32),
            pltpu.VMEM((2, PATCH, PATCH), F32),
            pltpu.VMEM((2 * PATCH, MODES * PATCH), BF16),
            pltpu.VMEM((MODES * PATCH, 2 * PATCH), BF16),
            pltpu.VMEM((MODES, PATCH, 2 * PATCH), F32),
            pltpu.VMEM((2 * MODES + 1, PATCH, PATCH), F32),
            pltpu.VMEM((1, KROWS, KCOLS), F32),
            pltpu.VMEM((2 * PATCH, 2 * PATCH), BF16),
            pltpu.VMEM((2 * PATCH, 2 * PATCH), BF16),
        ],
        name="positions",
    )(metas, own, sib, probe, amps, cos, sin)


def update_kernel(
    n, metas, g_own, g_sib, q_in, illum, obj, probe, new_obj, new_probe,
    gs, sib_in, t2_in, t1_in, t8_in, piece, q_sib, acc, minus_in, plus_in, y_in,
    p_tile, p_share, tile, dp, dp_in, kmine, ksib, kk, kpad, place, dobj, vec, vec1, vec2,
    send, recv, ysem, kysem, kxsem, v1sem, v2sem, bsend, dpsem, psem, lsem,
):
    me = lax.axis_index("scan")
    q = me % SPLIT
    core = me % 2
    first = me - q
    up = (me - SPLIT + n) % n
    down = (me + SPLIT) % n
    sibling = me + 1 - 2 * core
    side = 8
    x, y = me // (2 * side), (me // 2) % side
    msg = Messages(send, recv)

    def chip(at_x, at_y, at_core):
        return ((at_x % side) * side + at_y % side) * 2 + at_core

    peers = [chip(x + k, y, cc) for k in range(1, side) for cc in range(2)]
    peers += [chip(x, y + k, cc) for k in range(1, side) for cc in range(2)]
    peers += [sibling, up, down]
    greet(peers)

    to_sib = msg.make(g_sib, sib_in, sibling)
    to_sib.start()
    q_copy = msg.make(q_in.at[1 - core], q_sib, sibling)
    q_copy.start()

    band = (x // 4) * 16 + y * 2 + (x // 2) % 2
    lane = x % 2
    out_mode = x // 2
    out_band = (x % 2) * 16 + y * 2 + core
    load_tile = pltpu.make_async_copy(
        probe.at[:, pl.ds(2 * core, 2), pl.ds(mult(8 * band, 8), 8), pl.ds(mult(LANES * lane, LANES), LANES)],
        p_tile,
        lsem.at[0],
    )
    load_tile.start()
    load_share = pltpu.make_async_copy(
        probe.at[:, out_mode, pl.ds(mult(8 * out_band, 8), 8), :], p_share, lsem.at[1]
    )
    load_share.start()

    gs[...] = g_own[...]
    to_sib.wait_recv()
    edge = pl.ds(mult(384 * (1 - core), LANES), LANES)
    gs[:, :, edge] += sib_in[...]

    t2 = []
    for j in range(3):
        lo = JITTER + 2 * STEP + STRIP * j
        copy = msg.make(gs.at[:, pl.ds(lo, STRIP), :], t2_in.at[j], down)
        copy.start()
        t2.append(copy)
    t8 = msg.make(gs.at[:, pl.ds(0, JITTER), :], t8_in, up)
    t8.start()

    def send_t1(j):
        lo = JITTER + STEP + STRIP * j
        copy = msg.make(gs.at[:, pl.ds(lo, STRIP), :], t1_in.at[j], down)
        copy.start()
        return copy

    t1 = {3: send_t1(3)}

    q_copy.wait_recv()
    acc[...] = q_in[core] + q_sib[...]

    def send_minus(step):
        dest = (x - (4 - step) + side) % side
        copy = msg.make(acc.at[dest], minus_in.at[step], chip(x - 1 + side, y, core))
        copy.start()
        return copy

    def send_plus(step):
        dest = (x + 3 - step) % side
        copy = msg.make(acc.at[dest], plus_in.at[step], chip(x + 1, y, core))
        copy.start()
        return copy

    minus = [send_minus(0)]
    plus = [send_plus(0)]

    def x_step(step):
        minus[step].wait_recv()
        acc[(x - (3 - step) + side) % side] += minus_in[step]
        if step < 3:
            minus.append(send_minus(step + 1))
            plus[step].wait_recv()
            acc[(x + 2 - step) % side] += plus_in[step]
            if step < 2:
                plus.append(send_plus(step + 1))

    def t2_step(j):
        t2[j].wait_recv()
        lo = JITTER + STEP + STRIP * j
        gs[:, lo : lo + STRIP, :] += t2_in[j]
        t1[j] = send_t1(j)

    t2_step(0)
    x_step(0)
    t2_step(1)
    x_step(1)
    t2_step(2)
    x_step(2)
    x_step(3)

    y_copies = []
    for k in range(1, side):
        copy = pltpu.make_async_remote_copy(
            src_ref=acc.at[x, (y + k) % side],
            dst_ref=y_in.at[k - 1],
            send_sem=bsend.at[k - 1],
            recv_sem=ysem,
            device_id={"scan": chip(x, y + k, core)},
            device_id_type=MESH,
        )
        copy.start()
        y_copies.append(copy)
    pltpu.make_async_copy(y_in, y_in, ysem).wait()
    tile[...] = acc[x, y] + jnp.sum(y_in[...], 0)
    load_tile.wait()
    norm = tile[4]
    inverse = norm + 1.0
    k_re = jnp.zeros((8, LANES), F32)
    k_im = jnp.zeros((8, LANES), F32)
    s_vv = jnp.zeros((8, LANES), F32)
    s_vc = jnp.zeros((8, LANES), F32)
    for m in range(2):
        g_re, g_im = tile[m], tile[2 + m]
        d_re, d_im = g_re / inverse, g_im / inverse
        dp[m, 0] = d_re
        dp[m, 1] = d_im
        p_re, p_im = p_tile[0, m], p_tile[1, m]
        k_re = k_re + (p_re * d_re + p_im * d_im)
        k_im = k_im + (p_re * d_im - p_im * d_re)
        s_vv = s_vv + (d_re * d_re + d_im * d_im) * norm
        s_vc = s_vc + (d_re * g_re + d_im * g_im)
    kmine[0] = k_re
    kmine[1] = k_im
    k_copy = msg.make(kmine.at[1 - core], ksib, sibling)
    k_copy.start()

    dp_sends = []
    for m in range(2):
        dest = chip(2 * (2 * core + m) + x // 4, y, (x // 2) % 2)
        away = dest != me
        copy = pltpu.make_async_remote_copy(
            src_ref=dp.at[m],
            dst_ref=dp_in.at[lane],
            send_sem=bsend.at[21 + m],
            recv_sem=dpsem.at[lane],
            device_id={"scan": dest},
            device_id_type=MESH,
        )
        pl.when(away)(copy.start)
        dp_sends.append((copy, away))

        @pl.when(jnp.logical_not(away))
        def _():
            dp_in[lane] = dp[m]

    k_copy.wait_recv()
    kk[core, x, y] = kmine[core] + ksib[...]
    ky_copies = []
    for k in range(1, side):
        copy = pltpu.make_async_remote_copy(
            src_ref=kk.at[core, x, y],
            dst_ref=kk.at[core, x, y],
            send_sem=bsend.at[7 + k - 1],
            recv_sem=kysem,
            device_id={"scan": chip(x, y + k, core)},
            device_id_type=MESH,
        )
        copy.start()
        ky_copies.append(copy)

    pieces = []
    for j in (3, 0, 1, 2):
        t1[j].wait_recv()
        lo = JITTER + STRIP * j
        gs[:, lo : lo + STRIP, :] += t1_in[j]
        if j == 3:
            t8.wait_recv()
            gs[:, STEP : STEP + JITTER, :] += t8_in[...]
        slot = (j - q + SPLIT) % SPLIT
        copy = pltpu.make_async_remote_copy(
            src_ref=gs.at[:, pl.ds(lo, STRIP), :],
            dst_ref=piece.at[slot],
            send_sem=bsend.at[23 + j],
            recv_sem=psem.at[slot],
            device_id={"scan": first + j},
            device_id_type=MESH,
        )
        pl.when(q != j)(copy.start)
        pieces.append((copy, q != j))

    pltpu.make_async_copy(kk.at[0, 0, pl.ds(0, 7)], kk.at[0, 0, pl.ds(0, 7)], kysem).wait()
    kx_copies = []
    for k in range(1, side):
        copy = pltpu.make_async_remote_copy(
            src_ref=kk.at[core, x],
            dst_ref=kk.at[core, x],
            send_sem=bsend.at[14 + k - 1],
            recv_sem=kxsem,
            device_id={"scan": chip(x + k, y, core)},
            device_id_type=MESH,
        )
        copy.start()
        kx_copies.append(copy)
    piece[0] = gs[:, pl.ds(mult(JITTER + STRIP * q, 8), STRIP), :]

    pltpu.make_async_copy(kk.at[0, pl.ds(0, 7)], kk.at[0, pl.ds(0, 7)], kxsem).wait()
    ks_copy = msg.make(kk.at[core], kk.at[core], sibling)
    ks_copy.start()

    dobj[...] = jnp.zeros_like(dobj)
    for k in range(SPLIT):
        if k > 0:
            pltpu.make_async_copy(piece.at[k], piece.at[k], psem.at[k]).wait()
        source = (q - k + SPLIT) % SPLIT
        at = pl.ds(mult(768 * (source // 2) + OWN * (source % 2), LANES), OWN)
        dobj[:, :, at] += piece[k]
    bright = illum[0]
    g_re, g_im = dobj[0], dobj[1]
    o_re, o_im = obj[0], obj[1]
    d_re, d_im = g_re / (bright + 1.0), g_im / (bright + 1.0)
    s_uu = jnp.sum((d_re * d_re + d_im * d_im) * bright)
    s_uc = jnp.sum(d_re * g_re + d_im * g_im)
    dobj[0] = d_re
    dobj[1] = d_im

    ks_copy.wait_recv()
    kpad[...] = jnp.zeros_like(kpad)
    for at_band in range(PATCH // 8):
        for at_lane in range(2):
            xx = (at_band // 16) * 4 + (at_band % 2) * 2 + at_lane
            yy = (at_band // 2) % 8
            rows = slice(ZTOP + 8 * at_band, ZTOP + 8 * at_band + 8)
            cols = slice(LANES * at_lane, LANES * at_lane + LANES)
            kpad[0, rows, cols] = kk[0, xx, yy]
            kpad[1, rows, cols] = kk[1, xx, yy]
    spread(n, kpad, place, metas)
    d_re, d_im = dobj[0], dobj[1]
    s_uv = jnp.sum(
        place[0] * (d_re * o_re + d_im * o_im) - place[1] * (d_re * o_im - d_im * o_re)
    )

    at = lax.broadcasted_iota(jnp.int32, (8, LANES), 1)
    own_sums = jnp.zeros((8, LANES), F32)
    for i, value in enumerate((s_uu, s_uv, jnp.sum(s_vv), s_uc, jnp.sum(s_vc))):
        own_sums = jnp.where(at == i, value, own_sums)
    vec[...] = own_sums
    v1_copies = []
    for k in range(1, 2 * side):
        copy = pltpu.make_async_remote_copy(
            src_ref=vec,
            dst_ref=vec1.at[k - 1],
            send_sem=bsend.at[27 + k - 1],
            recv_sem=v1sem,
            device_id={"scan": chip(x, y + k // 2, (core + k) % 2)},
            device_id_type=MESH,
        )
        copy.start()
        v1_copies.append(copy)
    pltpu.make_async_copy(vec1, vec1, v1sem).wait()
    for copy in v1_copies:
        copy.wait_send()
    vec[...] = own_sums + jnp.sum(vec1[...], 0)
    v2_copies = []
    for k in range(1, side):
        copy = pltpu.make_async_remote_copy(
            src_ref=vec,
            dst_ref=vec2.at[k - 1],
            send_sem=bsend.at[42 + k - 1],
            recv_sem=v2sem,
            device_id={"scan": chip(x + k, y, core)},
            device_id_type=MESH,
        )
        copy.start()
        v2_copies.append(copy)
    load_share.wait()
    for at_lane in range(2):
        source = chip((x % 2) * 4 + core * 2 + at_lane, y, x // 4)
        arrived = pltpu.make_async_copy(dp_in.at[at_lane], dp_in.at[at_lane], dpsem.at[at_lane])
        pl.when(source != me)(arrived.wait)
    pltpu.make_async_copy(vec2, vec2, v2sem).wait()
    totals = vec[...] + jnp.sum(vec2[...], 0)
    uu, uv, vv, uc, vc = (totals[0:1, i : i + 1] for i in range(5))
    a = 1.1 * uu + 1e-06
    d = 1.1 * vv + 1e-06
    det = a * d - uv * uv
    rate_obj = (uc * d - uv * vc) / det
    rate_probe = (a * vc - uv * uc) / det
    for part in range(2):
        new_obj[part] = obj[part] + rate_obj * dobj[part]
        for at_lane in range(2):
            cols = slice(LANES * at_lane, LANES * at_lane + LANES)
            new_probe[part, :, cols] = p_share[part, :, cols] + rate_probe * dp_in[at_lane, part]

    msg.drain()
    for copy in y_copies + ky_copies + kx_copies + v2_copies:
        copy.wait_send()
    for copy, when in dp_sends + pieces:
        pl.when(when)(copy.wait_send)


def update(n, metas, g_own, g_sib, q_in, illum, obj, probe):
    vmem = pl.BlockSpec(memory_space=pltpu.VMEM)
    dma = pltpu.SemaphoreType.DMA
    columns = obj.shape[2]
    return pl.pallas_call(
        functools.partial(update_kernel, n),
        out_shape=(
            jax.ShapeDtypeStruct((2, STRIP, columns), F32),
            jax.ShapeDtypeStruct((2, 8, PATCH), F32),
        ),
        in_specs=[pl.BlockSpec(memory_space=pltpu.SMEM)] + [vmem] * 5 + [pl.BlockSpec(memory_space=pl.ANY)],
        out_specs=[vmem] * 2,
        scratch_shapes=[
            pltpu.VMEM((2, ROWS, OWN), F32),
            pltpu.VMEM((2, ROWS, LANES), F32),
            pltpu.VMEM((3, 2, STRIP, OWN), F32),
            pltpu.VMEM((4, 2, STRIP, OWN), F32),
            pltpu.VMEM((2, JITTER, OWN), F32),
            pltpu.VMEM((4, 2, STRIP, OWN), F32),
            pltpu.VMEM((8, 8, 5, 8, LANES), F32),
            pltpu.VMEM((8, 8, 5, 8, LANES), F32),
            pltpu.VMEM((4, 8, 5, 8, LANES), F32),
            pltpu.VMEM((3, 8, 5, 8, LANES), F32),
            pltpu.VMEM((7, 5, 8, LANES), F32),
            pltpu.VMEM((2, 2, 8, LANES), F32),
            pltpu.VMEM((2, 8, PATCH), F32),
            pltpu.VMEM((5, 8, LANES), F32),
            pltpu.VMEM((2, 2, 8, LANES), F32),
            pltpu.VMEM((2, 2, 8, LANES), F32),
            pltpu.VMEM((2, 8, LANES), F32),
            pltpu.VMEM((8, LANES), F32),
            pltpu.VMEM((2, 8, 8, 8, LANES), F32),
            pltpu.VMEM((2, KROWS, KCOLS), F32),
            pltpu.VMEM((2, STRIP, columns), F32),
            pltpu.VMEM((2, STRIP, columns), F32),
            pltpu.VMEM((8, LANES), F32),
            pltpu.VMEM((15, 8, LANES), F32),
            pltpu.VMEM((7, 8, LANES), F32),
            dma((24,)),
            dma((24,)),
            dma,
            dma,
            dma,
            dma,
            dma,
            dma((50,)),
            dma((2,)),
            dma((4,)),
            dma((2,)),
        ],
        compiler_params=pltpu.CompilerParams(collective_id=1, has_side_effects=True),
        name="update",
    )(metas, g_own, g_sib, q_in, illum, obj, probe)


def tables(length):
    numbers = np.arange(length, dtype=np.int64)
    angles = (numbers[:, None] * numbers[None, :] % length).astype(np.float32)
    angles = angles * np.float32(2.0 * math.pi / length)
    scaling = np.float32(1.0 / math.sqrt(length))
    return tuple(jnp.asarray(f(angles) * scaling).astype(BF16) for f in (np.cos, np.sin))


def on_device(n, object_field, probe_field, amplitudes, offsets, live_counts):
    probe = probe_field.reshape(2, MODES, PATCH, PATCH)
    meta = jnp.concatenate([offsets.reshape(-1), live_counts])
    meta = jnp.broadcast_to(jnp.pad(meta, (0, LANES - meta.shape[0]))[None], (8, LANES))
    cos, sin = tables(PATCH)
    own, sib, metas = gather(n, object_field, meta)
    metas = metas[:, 0, 0:16]
    g_own, g_sib, q_out, illum = positions(n, metas, own, sib, probe, amplitudes, cos, sin)
    return update(n, metas, g_own, g_sib, q_out, illum, object_field, probe)


def solution(mesh):
    groups_scan = ("groups", "scan")
    placed = (
        P(None, groups_scan, None),
        P(None, "groups", None),
        P(groups_scan, None, None),
        P(groups_scan, None),
        P(groups_scan),
    )
    return jax.shard_map(
        functools.partial(on_device, mesh.shape["scan"]),
        mesh=mesh,
        in_specs=placed,
        out_specs=(P(None, groups_scan, None), P(None, groups_scan, None)),
        check_vma=False,
    )
```

time: 1130 us -> 190 us (0.17)
  waiting for transfers between devices: 672 us -> 0 us
  starting transfers between devices: 254 us -> 0 us
  Pallas kernels: 0 us -> 183 us
  local copies, waits for them, and re-layouts: 67.5 us -> 5.96 us
  other arithmetic: 42.3 us -> 0.08 us
  blocking collectives: 35.3 us -> 0 us
  between operations: 21.1 us -> 1.3 us
  matrix products: 16.8 us -> 0 us
  loops' own time: 14.8 us -> 0 us
    ppermute x42 -> x0, waiting for transfers between devices: 458 us -> none  [from_behind(): return lax.ppermute(shard, axis, pairs)]
    ppermute x42 -> x0, starting transfers between devices: 253 us -> none  [from_behind(): return lax.ppermute(shard, axis, pairs)]
    psum x1 -> x0, waiting for transfers between devices: 214 us -> none  [on_device(): summed_probe, summed_norm = lax.psum((grad_probe, obj_norm), SCAN)]
    pallas_call x0 -> x3, Pallas kernels: none -> 183 us  [the longest x1 84.5 us: update(): pl.pallas_call(functools.partial(update_kernel, n), out_shape=(jax.ShapeD...]
    psum x3 -> x0, blocking collectives: 35.3 us -> none  [one_axis_at_a_time(): shard = lax.psum(shard, axis)]
    add x17 -> x0, other arithmetic: 21.7 us -> none  [the longest x2 4.58 us: exit_update(): mode_re = patch_re * exit_change[0] + patch_im * exit_change[1]]
    dynamic_update_slice x2 -> x0, local copies, waits for them, and re-layouts: 17.7 us -> none  [visit(): lax.dynamic_update_slice(grad_grid, current + contrib, (zero_index, top_r...]
    dot_general x4 -> x0, matrix products: 16.8 us -> none  [transform(): jnp.einsum('camn,cndk->damk', half_done, right_table, preferred_element_t...]
  transfers between devices with their start and end apart: 43 -> 0, of which waited for: 15 -> 0; matrix products, arithmetic and copies ran while one was open for 4% -> 0% of each run, Pallas kernels for 0% -> 0%
where the time goes in v1:
time: 190 us
  Pallas kernels  183 us (96%)
  local copies, waits for them, and re-layouts  5.96 us (3%)
    pallas_call x1, Pallas kernels, update(): pl.pallas_call(functools.partial(update_kernel, n), out_shape=(jax.ShapeD...  84.5 us
    pallas_call x1, Pallas kernels, gather(): pl.pallas_call(functools.partial(gather_kernel, n), out_shape=(jax.ShapeD...  63 us
    pallas_call x1, Pallas kernels, positions(): pl.pallas_call(functools.partial(position_kernel, n), out_shape=(jax.Shap...  35.2 us
    unnamed x3, local copies, waits for them, and re-layouts  3.82 us

profile of v1, /device:TPU:513, one launch (start us, length us, event | category | flops | bytes accessed | tf_op | source)
XLA Modules:
  0.0 190.1 jit_solution(15927087736386889936)
XLA Ops:
  1.3 0.8 copy.11
  2.0 0.1 reshape.11
  2.1 0.1 pad_add_fusion
  2.2 0.6 broadcast_in_dim.2.meta
  2.8 63.0 %gather_window.1 = (f32[2,272,512]{2,1,0:T(8,128)}, f32[2,272,128]{2,1,0:T(8,128)}, s32[16,8,128]{2,1,0:T(8,128)}) custom-call(f32[2,24,1792]{2,1,0:T(8,128)} %obj.3, s32[8,128]{1,0:T(8,128)} %broadcast_in_dim.2.meta), custom_call_target="tpu_custom_call" | custom-call | tf_op jit(solution)/shard_map/gather_window/pallas_call | solution.py:169
  65.8 0.9 copy.12
  66.7 0.6 slice_bitcast_fusion.metas
  67.3 35.2 %positions.1 = (f32[2,272,512]{2,1,0:T(8,128)}, f32[2,272,128]{2,1,0:T(8,128)}, f32[2,8,8,5,8,128]{5,4,3,2,1,0:T(8,128)}, f32[1,24,1792]{2,1,0:T(8,128)}) custom-call(s32[16,16]{1,0:T(8,128)} %slice_bitcast_fusion.metas, f32[2,272,512]{2,1,0:T(8,128)} %get-tuple-element.10.own, f32[2,272,128]{2,1,0:T(8,128)} %get-tuple-element.11.sib, ...), custom_call_target="tpu_custom_call" | custom-call | tf_op jit(solution)/shard_map/positions/pallas_call | solution.py:353
  102.5 84.5 %update.1 = (f32[2,24,1792]{2,1,0:T(8,128)}, f32[2,8,256]{2,1,0:T(8,128)}) custom-call(s32[16,16]{1,0:T(8,128)} %slice_bitcast_fusion.metas, f32[2,272,512]{2,1,0:T(8,128)} %get-tuple-element.12.g_own, f32[2,272,128]{2,1,0:T(8,128)} %get-tuple-element.13.g_sib, f32[2,8,8,5,8,128]{5,4,3,2,1,0:T(8,128)} %get-tuple-element.14.q_in, ...), custom_call_target="tpu_custom_call" | custom-call | tf_op jit(solution)/shard_map/update/pallas_call | solution.py:692
  187.0 1.7 copy.16
  188.8 1.3 copy.17
  (1 shorter events, 0.0 us)

commit v2 on v1

--- a/solution.py
+++ b/solution.py
@@ -64,7 +64,25 @@
     pl.semaphore_wait(barrier, len(peers))
 
 
-def gather_kernel(n, obj, meta, own, sib, metas, send, recv, msend, mrecv):
+def long_way(me, step):
+    line, at, q = me // 16, (me // SPLIT) % 4, me % SPLIT
+    scale = 16
+
+    def device(at_line, at_row):
+        return (at_line + 8) % 8 * scale + (at_row + 8) % 4 * SPLIT + q
+
+    def turn(row):
+        row = (row + 8) % 4
+        return jnp.where(jnp.logical_or(row == 0, row == 3), 0, 1)
+
+    relay = device(line, at - step)
+    origin = device(line, at + step)
+    target = device(line + step * turn(at), at - step)
+    source = device(line - step * turn(at + step), at + step)
+    return relay, origin, target, source
+
+
+def gather_kernel(n, obj, meta, own, sib, metas, relay_in, send, recv, msend, mrecv):
     me = lax.axis_index("scan")
     q = me % SPLIT
     core = me % 2
@@ -72,9 +90,11 @@
     up = (me - SPLIT + n) % n
     down = (me + SPLIT) % n
     sibling = me + 1 - 2 * core
+    relay, origin, target, source = long_way(me, -1)
     msg = Messages(send, recv)
     peers = [(first + SPLIT * e + k + 2 * n) % n for e in (-2, -1, 1, 2) for k in range(SPLIT)]
     peers += [first + (q + k) % SPLIT for k in range(1, SPLIT)]
+    peers += [relay, origin, target, source]
     greet(peers)
 
     def columns(quarter):
@@ -83,7 +103,6 @@
     def rows(start, size):
         return pl.ds(mult(start, 8), size)
 
-    own[:, rows(JITTER + STRIP * q, STRIP), :] = obj[:, :, columns(q)]
     strips = []
     for k in range(1, SPLIT):
         there = (q + k) % SPLIT
@@ -94,37 +113,40 @@
         )
         copy.start()
         strips.append(copy)
-    metas[2 * SPLIT + q] = meta[...]
-    meta_copies = []
-    for e in (-1, 0, 1, 2):
-        for k in range(SPLIT):
-            if e == 0 and k == 0:
-                continue
-            there = (first + SPLIT * e + (q + k) % SPLIT + n) % n
-            at = len(meta_copies)
-            copy = pltpu.make_async_remote_copy(
-                src_ref=meta,
-                dst_ref=metas.at[(2 - e) * SPLIT + q],
-                send_sem=msend.at[at],
-                recv_sem=mrecv,
-                device_id={"scan": there},
-                device_id_type=MESH,
-            )
-            copy.start()
-            meta_copies.append(copy)
-
-    ahead = []
+
+    ahead, relays = [], []
     for k in range(SPLIT):
         if k > 0:
             strips[k - 1].wait_recv()
         strip = (q - k + SPLIT) % SPLIT
-        copy = msg.make(
-            own.at[:, rows(JITTER + STRIP * strip, STRIP), :] if k else obj.at[:, :, columns(q)],
-            own.at[:, rows(JITTER + STEP + STRIP * strip, STRIP), :],
-            up,
-        )
+        block = own.at[:, rows(JITTER + STRIP * strip, STRIP), :] if k else obj.at[:, :, columns(q)]
+        copy = msg.make(block, own.at[:, rows(JITTER + STEP + STRIP * strip, STRIP), :], up)
         copy.start()
         ahead.append(copy)
+        far = jnp.logical_or(strip == 1, strip == 2)
+        copy = msg.make(block, relay_in.at[k], relay, when=far)
+        pl.when(far)(copy.start)
+        relays.append((copy, far))
+        if k == 0:
+            own[:, rows(JITTER + STRIP * q, STRIP), :] = obj[:, :, columns(q)]
+            metas[2 * SPLIT + q] = meta[...]
+            meta_copies = []
+            for e in (-1, 0, 1, 2):
+                for kk in range(SPLIT):
+                    if e == 0 and kk == 0:
+                        continue
+                    there = (first + SPLIT * e + (q + kk) % SPLIT + n) % n
+                    at = len(meta_copies)
+                    copy = pltpu.make_async_remote_copy(
+                        src_ref=meta,
+                        dst_ref=metas.at[(2 - e) * SPLIT + q],
+                        send_sem=msend.at[at],
+                        recv_sem=mrecv,
+                        device_id={"scan": there},
+                        device_id_type=MESH,
+                    )
+                    copy.start()
+                    meta_copies.append(copy)
     tail = msg.make(own.at[:, rows(STEP, JITTER), :], own.at[:, rows(0, JITTER), :], down)
     tail.start()
     edge = pl.ds(mult(384 * (1 - core), LANES), LANES)
@@ -137,24 +159,26 @@
         return copy
 
     borders = [border(JITTER, STEP)]
-    relays = []
+    finals = []
     for k in range(SPLIT):
+        strip = (q - k + SPLIT) % SPLIT
+        far = jnp.logical_or(strip == 1, strip == 2)
+        near = strip == 0
+        place = own.at[:, rows(JITTER + 2 * STEP + STRIP * jnp.minimum(strip, 2), STRIP), :]
+        pl.when(far)(relays[k][0].wait_recv)
+        copy = msg.make(relay_in.at[k], place, target, when=far)
+        pl.when(far)(copy.start)
+        finals.append((copy, far))
         ahead[k].wait_recv()
-        strip = (q - k + SPLIT) % SPLIT
-        low = jnp.minimum(strip, SPLIT - 2)
-        copy = msg.make(
-            own.at[:, rows(JITTER + STEP + STRIP * low, STRIP), :],
-            own.at[:, rows(JITTER + 2 * STEP + STRIP * low, STRIP), :],
-            up,
-            when=strip != SPLIT - 1,
-        )
-        pl.when(strip != SPLIT - 1)(copy.start)
-        relays.append((copy, strip != SPLIT - 1))
+        block = own.at[:, rows(JITTER + STEP + STRIP * strip, STRIP), :]
+        copy = msg.make(block, place, up, when=near)
+        pl.when(near)(copy.start)
+        finals.append((copy, near))
     borders.append(border(JITTER + STEP, STEP))
     tail.wait_recv()
-    for copy, when in relays:
+    borders.append(border(0, JITTER))
+    for copy, when in finals:
         pl.when(when)(copy.wait_recv)
-    borders.append(border(0, JITTER))
     borders.append(border(JITTER + 2 * STEP, 72))
     for copy in borders:
         copy.wait_recv()
@@ -176,8 +200,9 @@
         in_specs=[vmem] * 2,
         out_specs=[vmem] * 3,
         scratch_shapes=[
-            pltpu.SemaphoreType.DMA((16,)),
-            pltpu.SemaphoreType.DMA((16,)),
+            pltpu.VMEM((SPLIT, 2, STRIP, OWN), F32),
+            pltpu.SemaphoreType.DMA((24,)),
+            pltpu.SemaphoreType.DMA((24,)),
             pltpu.SemaphoreType.DMA((16,)),
             pltpu.SemaphoreType.DMA,
         ],
@@ -186,38 +211,38 @@
     )(obj, meta)
 
 
-def spread(n, kernel_pad, out, metas):
+def spread(n, kernel_pad, out, metas, line):
     me = lax.axis_index("scan")
-    row = me // SPLIT
+    q = me % SPLIT
+    line = line + jnp.where(q == SPLIT - 1, 1, 0)
+    there = me // SPLIT - 2 + line
+    inside = jnp.logical_and(there >= 0, there < n // SPLIT)
+    start = mult(STRIP * q + STEP * (2 - line) - JITTER + ZTOP, 8)
     parts = out.shape[0]
-    out[...] = jnp.zeros_like(out)
-
-    def one(at, carry):
-        line, col = at // 16, at % 16
+    tall = STRIP + 2 * JITTER
+
+    def one(col, carry):
         slot = line * SPLIT + col // SPLIT
         place = col % SPLIT
         top = metas[slot, 2 * place]
         left = metas[slot, 2 * place + 1]
-        there = row - 2 + line
-        inside = jnp.logical_and(there >= 0, there < n // SPLIT)
         weight = jnp.where(jnp.logical_and(inside, place < metas[slot, 8]), 1.0, 0.0).astype(F32)
-        start = mult(STRIP * (me % SPLIT) + STEP * (2 - line) - JITTER + ZTOP, 8)
         ahead = jnp.clip(STEP * there - top + JITTER, 0, 2 * JITTER)
         base = mult((STEP * col + 40) // LANES * LANES, LANES)
         shift = jnp.clip(left - base, 0, LANES)
         for part in range(parts):
-            value = kernel_pad[part, pl.ds(start, STRIP + 2 * JITTER), :]
-            value = pltpu.roll(value, (STRIP + 2 * JITTER - ahead) % (STRIP + 2 * JITTER), 0)[0:STRIP]
+            value = kernel_pad[part, pl.ds(start, tall), :]
+            value = pltpu.roll(value, (tall - ahead) % tall, 0)[0:STRIP]
             value = pltpu.roll(value, shift, 1) * weight
             out[part, :, pl.ds(base, KCOLS)] += value
         return carry
 
-    lax.fori_loop(0, 4 * 16, one, 0)
+    lax.fori_loop(0, 16, one, 0, unroll=4)
 
 
 def position_kernel(
-    n, metas, own, sib, probe, amps, cos, sin, g_own, g_sib, q_out, illum,
-    win, grad, patch, wave, half, far, acc, kpad, ta, tb,
+    n, metas, own, sib, probe, amps, cos, sin, g_own, g_sib, q_out, light_out,
+    win, grad, patch, wave, half, far, acc, ta, tb,
 ):
     me = lax.axis_index("scan")
     row = me // SPLIT
@@ -246,12 +271,10 @@
     win[:, ROWS:, :] = jnp.zeros((2, 8, WIN), F32)
     grad[...] = jnp.zeros_like(grad)
     acc[...] = jnp.zeros_like(acc)
-    kpad[...] = jnp.zeros_like(kpad)
     light = jnp.zeros((PATCH, PATCH), F32)
     for m in range(MODES):
         light = light + (probe[0, m] * probe[0, m] + probe[1, m] * probe[1, m])
-    kpad[0, ZTOP : ZTOP + PATCH, 0:PATCH] = light
-    spread(n, kpad, illum, metas)
+    light_out[...] = light
 
     chunk = 32
     chunks = PATCH // chunk
@@ -356,7 +379,7 @@
             jax.ShapeDtypeStruct((2, ROWS, OWN), F32),
             jax.ShapeDtypeStruct((2, ROWS, LANES), F32),
             jax.ShapeDtypeStruct((2, 8, 8, 5, 8, LANES), F32),
-            jax.ShapeDtypeStruct((1, STRIP, 14 * LANES), F32),
+            jax.ShapeDtypeStruct((PATCH, PATCH), F32),
         ),
         in_specs=[pl.BlockSpec(memory_space=pltpu.SMEM)] + [vmem] * 6,
         out_specs=[vmem] * 4,
@@ -368,7 +391,6 @@
             pltpu.VMEM((MODES * PATCH, 2 * PATCH), BF16),
             pltpu.VMEM((MODES, PATCH, 2 * PATCH), F32),
             pltpu.VMEM((2 * MODES + 1, PATCH, PATCH), F32),
-            pltpu.VMEM((1, KROWS, KCOLS), F32),
             pltpu.VMEM((2 * PATCH, 2 * PATCH), BF16),
             pltpu.VMEM((2 * PATCH, 2 * PATCH), BF16),
         ],
@@ -377,9 +399,9 @@
 
 
 def update_kernel(
-    n, metas, g_own, g_sib, q_in, illum, obj, probe, new_obj, new_probe,
-    gs, sib_in, t2_in, t1_in, t8_in, piece, q_sib, acc, minus_in, plus_in, y_in,
-    p_tile, p_share, tile, dp, dp_in, kmine, ksib, kk, kpad, place, dobj, vec, vec1, vec2,
+    n, metas, g_own, g_sib, q_in, light, obj, probe, new_obj, new_probe,
+    gs, sib_in, t2_in, t1_in, t8_in, relay_in, far_in, piece, q_sib, acc, minus_in, plus_in, y_in,
+    p_tile, p_share, tile, dp, dp_in, kmine, ksib, kk, kpad, illum, place, dobj, vec, vec1, vec2,
     send, recv, ysem, kysem, kxsem, v1sem, v2sem, bsend, dpsem, psem, lsem,
 ):
     me = lax.axis_index("scan")
@@ -398,13 +420,18 @@
 
     peers = [chip(x + k, y, cc) for k in range(1, side) for cc in range(2)]
     peers += [chip(x, y + k, cc) for k in range(1, side) for cc in range(2)]
-    peers += [sibling, up, down]
+    relay, origin, target, source = long_way(me, 1)
+    peers += [sibling, up, down, relay, origin, target, source]
     greet(peers)
 
     to_sib = msg.make(g_sib, sib_in, sibling)
     to_sib.start()
-    q_copy = msg.make(q_in.at[1 - core], q_sib, sibling)
-    q_copy.start()
+    chunks = [(x + k) % side for k in (4, 5, 3, 6, 2, 7, 1, 0)]
+    q_copies = []
+    for at in chunks:
+        copy = msg.make(q_in.at[1 - core, at], q_sib.at[at], sibling)
+        copy.start()
+        q_copies.append(copy)
 
     band = (x // 4) * 16 + y * 2 + (x // 2) % 2
     lane = x % 2
@@ -426,64 +453,87 @@
     edge = pl.ds(mult(384 * (1 - core), LANES), LANES)
     gs[:, :, edge] += sib_in[...]
 
-    t2 = []
-    for j in range(3):
-        lo = JITTER + 2 * STEP + STRIP * j
-        copy = msg.make(gs.at[:, pl.ds(lo, STRIP), :], t2_in.at[j], down)
-        copy.start()
-        t2.append(copy)
+    def sums(start):
+        return gs.at[:, pl.ds(start, STRIP), :]
+
+    far_out = []
+    for j in (1, 2):
+        copy = msg.make(sums(JITTER + 2 * STEP + STRIP * j), relay_in.at[j - 1], relay)
+        copy.start()
+        far_out.append(copy)
+    t2 = msg.make(sums(JITTER + 2 * STEP), t2_in, down)
+    t2.start()
     t8 = msg.make(gs.at[:, pl.ds(0, JITTER), :], t8_in, up)
     t8.start()
 
     def send_t1(j):
-        lo = JITTER + STEP + STRIP * j
-        copy = msg.make(gs.at[:, pl.ds(lo, STRIP), :], t1_in.at[j], down)
+        copy = msg.make(sums(JITTER + STEP + STRIP * j), t1_in.at[j], down)
         copy.start()
         return copy
 
-    t1 = {3: send_t1(3)}
-
-    q_copy.wait_recv()
-    acc[...] = q_in[core] + q_sib[...]
-
-    def send_minus(step):
-        dest = (x - (4 - step) + side) % side
-        copy = msg.make(acc.at[dest], minus_in.at[step], chip(x - 1 + side, y, core))
+    t1 = {j: send_t1(j) for j in (1, 2, 3)}
+
+    def add_sibling(i):
+        q_copies[i].wait_recv()
+        acc[chunks[i]] = q_in[core, chunks[i]] + q_sib[chunks[i]]
+
+    half = side // 2
+
+    def send_chain(way, i):
+        which = (i % 2 if way < 0 else 1 - i % 2) * half
+        reach = (4 if i % 2 == 0 else 3) - i // 2
+        dest = (x + way * reach + side) % side
+        copy = msg.make(
+            acc.at[dest, pl.ds(which, half)],
+            (minus_in if way < 0 else plus_in).at[i],
+            chip(x + way + side, y, core),
+        )
         copy.start()
         return copy
 
-    def send_plus(step):
-        dest = (x + 3 - step) % side
-        copy = msg.make(acc.at[dest], plus_in.at[step], chip(x + 1, y, core))
-        copy.start()
-        return copy
-
-    minus = [send_minus(0)]
-    plus = [send_plus(0)]
-
-    def x_step(step):
-        minus[step].wait_recv()
-        acc[(x - (3 - step) + side) % side] += minus_in[step]
-        if step < 3:
-            minus.append(send_minus(step + 1))
-            plus[step].wait_recv()
-            acc[(x + 2 - step) % side] += plus_in[step]
-            if step < 2:
-                plus.append(send_plus(step + 1))
-
-    def t2_step(j):
-        t2[j].wait_recv()
-        lo = JITTER + STEP + STRIP * j
-        gs[:, lo : lo + STRIP, :] += t2_in[j]
-        t1[j] = send_t1(j)
-
-    t2_step(0)
+    chains = {}
+    add_sibling(0)
+    chains[-1, 0], chains[1, 0] = send_chain(-1, 0), send_chain(1, 0)
+    add_sibling(1)
+    chains[-1, 1] = send_chain(-1, 1)
+    add_sibling(2)
+    chains[1, 1] = send_chain(1, 1)
+    for i in range(3, 8):
+        add_sibling(i)
+
+    def x_step(i):
+        for way, arrived in ((-1, minus_in), (1, plus_in)):
+            which = (i % 2 if way < 0 else 1 - i % 2) * half
+            reach = (4 if i % 2 == 0 else 3) - 1 - i // 2
+            dest = (x + way * reach + side) % side
+            chains[way, i].wait_recv()
+            acc[dest, which : which + half] += arrived[i]
+            if reach > 0:
+                chains[way, i + 2] = send_chain(way, i + 2)
+
+    kpad[...] = jnp.zeros_like(kpad)
+    illum[...] = jnp.zeros_like(illum)
+    kpad[0, ZTOP : ZTOP + PATCH, 0:PATCH] = light[...]
+    dim = kpad.at[pl.ds(0, 1)]
     x_step(0)
-    t2_step(1)
+    t2.wait_recv()
+    gs[:, JITTER + STEP : JITTER + STEP + STRIP, :] += t2_in[...]
+    t1[0] = send_t1(0)
+    far_final = []
+    for j in range(2):
+        far_out[j].wait_recv()
+        copy = msg.make(relay_in.at[j], far_in.at[j], target)
+        copy.start()
+        far_final.append(copy)
     x_step(1)
-    t2_step(2)
+    spread(n, dim, illum, metas, 0)
     x_step(2)
+    spread(n, dim, illum, metas, 1)
     x_step(3)
+    spread(n, dim, illum, metas, 2)
+    x_step(4)
+    x_step(5)
+    x_step(6)
 
     y_copies = []
     for k in range(1, side):
@@ -556,13 +606,16 @@
         ky_copies.append(copy)
 
     pieces = []
-    for j in (3, 0, 1, 2):
+    for j in (3, 1, 2, 0):
         t1[j].wait_recv()
         lo = JITTER + STRIP * j
         gs[:, lo : lo + STRIP, :] += t1_in[j]
         if j == 3:
             t8.wait_recv()
             gs[:, STEP : STEP + JITTER, :] += t8_in[...]
+        if j in (1, 2):
+            far_final[j - 1].wait_recv()
+            gs[:, lo : lo + STRIP, :] += far_in[j - 1]
         slot = (j - q + SPLIT) % SPLIT
         copy = pltpu.make_async_remote_copy(
             src_ref=gs.at[:, pl.ds(lo, STRIP), :],
@@ -610,8 +663,8 @@
     dobj[0] = d_re
     dobj[1] = d_im
 
+    place[...] = jnp.zeros_like(place)
     ks_copy.wait_recv()
-    kpad[...] = jnp.zeros_like(kpad)
     for at_band in range(PATCH // 8):
         for at_lane in range(2):
             xx = (at_band // 16) * 4 + (at_band % 2) * 2 + at_lane
@@ -620,7 +673,8 @@
             cols = slice(LANES * at_lane, LANES * at_lane + LANES)
             kpad[0, rows, cols] = kk[0, xx, yy]
             kpad[1, rows, cols] = kk[1, xx, yy]
-    spread(n, kpad, place, metas)
+    for line in range(3):
+        spread(n, kpad, place, metas, line)
     d_re, d_im = dobj[0], dobj[1]
     s_uv = jnp.sum(
         place[0] * (d_re * o_re + d_im * o_im) - place[1] * (d_re * o_im - d_im * o_re)
@@ -685,7 +739,7 @@
         pl.when(when)(copy.wait_send)
 
 
-def update(n, metas, g_own, g_sib, q_in, illum, obj, probe):
+def update(n, metas, g_own, g_sib, q_in, light, obj, probe):
     vmem = pl.BlockSpec(memory_space=pltpu.VMEM)
     dma = pltpu.SemaphoreType.DMA
     columns = obj.shape[2]
@@ -700,14 +754,16 @@
         scratch_shapes=[
             pltpu.VMEM((2, ROWS, OWN), F32),
             pltpu.VMEM((2, ROWS, LANES), F32),
-            pltpu.VMEM((3, 2, STRIP, OWN), F32),
+            pltpu.VMEM((2, STRIP, OWN), F32),
             pltpu.VMEM((4, 2, STRIP, OWN), F32),
             pltpu.VMEM((2, JITTER, OWN), F32),
+            pltpu.VMEM((2, 2, STRIP, OWN), F32),
+            pltpu.VMEM((2, 2, STRIP, OWN), F32),
             pltpu.VMEM((4, 2, STRIP, OWN), F32),
             pltpu.VMEM((8, 8, 5, 8, LANES), F32),
             pltpu.VMEM((8, 8, 5, 8, LANES), F32),
-            pltpu.VMEM((4, 8, 5, 8, LANES), F32),
-            pltpu.VMEM((3, 8, 5, 8, LANES), F32),
+            pltpu.VMEM((7, 4, 5, 8, LANES), F32),
+            pltpu.VMEM((7, 4, 5, 8, LANES), F32),
             pltpu.VMEM((7, 5, 8, LANES), F32),
             pltpu.VMEM((2, 2, 8, LANES), F32),
             pltpu.VMEM((2, 8, PATCH), F32),
@@ -718,13 +774,14 @@
             pltpu.VMEM((8, LANES), F32),
             pltpu.VMEM((2, 8, 8, 8, LANES), F32),
             pltpu.VMEM((2, KROWS, KCOLS), F32),
+            pltpu.VMEM((1, STRIP, columns), F32),
             pltpu.VMEM((2, STRIP, columns), F32),
             pltpu.VMEM((2, STRIP, columns), F32),
             pltpu.VMEM((8, LANES), F32),
             pltpu.VMEM((15, 8, LANES), F32),
             pltpu.VMEM((7, 8, LANES), F32),
-            dma((24,)),
-            dma((24,)),
+            dma((48,)),
+            dma((48,)),
             dma,
             dma,
             dma,
@@ -737,7 +794,7 @@
         ],
         compiler_params=pltpu.CompilerParams(collective_id=1, has_side_effects=True),
         name="update",
-    )(metas, g_own, g_sib, q_in, illum, obj, probe)
+    )(metas, g_own, g_sib, q_in, light, obj, probe)
 
 
 def tables(length):
@@ -755,8 +812,8 @@
     cos, sin = tables(PATCH)
     own, sib, metas = gather(n, object_field, meta)
     metas = metas[:, 0, 0:16]
-    g_own, g_sib, q_out, illum = positions(n, metas, own, sib, probe, amplitudes, cos, sin)
-    return update(n, metas, g_own, g_sib, q_out, illum, object_field, probe)
+    g_own, g_sib, q_out, light = positions(n, metas, own, sib, probe, amplitudes, cos, sin)
+    return update(n, metas, g_own, g_sib, q_out, light, object_field, probe)
 
 
 def solution(mesh):

time: 190 us -> 165 us (0.87)
  Pallas kernels: 183 us -> 159 us
    pallas_call x1, Pallas kernels: 35.2 us -> 16.5 us  [positions(): pl.pallas_call(functools.partial(position_kernel, n), out_shape=(jax.Shap...]
    pallas_call x1, Pallas kernels: 63 us -> 57.5 us  [gather(): pl.pallas_call(functools.partial(gather_kernel, n), out_shape=(jax.ShapeD...]
where the time goes in v2:
time: 165 us; the launch traced here: 167 us
  Pallas kernels  159 us (96%)
  local copies, waits for them, and re-layouts  5.96 us (4%)
    pallas_call x1, Pallas kernels, update(): pl.pallas_call(functools.partial(update_kernel, n), out_shape=(jax.ShapeD...  85.3 us
    pallas_call x1, Pallas kernels, gather(): pl.pallas_call(functools.partial(gather_kernel, n), out_shape=(jax.ShapeD...  57.5 us
    pallas_call x1, Pallas kernels, positions(): pl.pallas_call(functools.partial(position_kernel, n), out_shape=(jax.Shap...  16.5 us
    unnamed x3, local copies, waits for them, and re-layouts  3.82 us

profile of v2, /device:TPU:513, one launch (start us, length us, event | category | flops | bytes accessed | tf_op | source)
XLA Modules:
  0.0 166.6 jit_solution(3879258227624374929)
XLA Ops:
  1.3 0.8 copy.11
  2.0 0.1 reshape.11
  2.1 0.1 pad_add_fusion
  2.2 0.6 broadcast_in_dim.2.meta
  2.8 57.5 %gather_window.1 = (f32[2,272,512]{2,1,0:T(8,128)}, f32[2,272,128]{2,1,0:T(8,128)}, s32[16,8,128]{2,1,0:T(8,128)}) custom-call(f32[2,24,1792]{2,1,0:T(8,128)} %obj.3, s32[8,128]{1,0:T(8,128)} %broadcast_in_dim.2.meta), custom_call_target="tpu_custom_call" | custom-call | tf_op jit(solution)/shard_map/gather_window/pallas_call | solution.py:193
  60.3 0.9 copy.12
  61.2 0.6 slice_bitcast_fusion.metas
  61.8 16.5 %positions.1 = (f32[2,272,512]{2,1,0:T(8,128)}, f32[2,272,128]{2,1,0:T(8,128)}, f32[2,8,8,5,8,128]{5,4,3,2,1,0:T(8,128)}, f32[256,256]{1,0:T(8,128)}) custom-call(s32[16,16]{1,0:T(8,128)} %slice_bitcast_fusion.metas, f32[2,272,512]{2,1,0:T(8,128)} %get-tuple-element.10.own, f32[2,272,128]{2,1,0:T(8,128)} %get-tuple-element.11.sib, ...), custom_call_target="tpu_custom_call" | custom-call | tf_op jit(solution)/shard_map/positions/pallas_call | solution.py:376
  78.2 85.3 %update.1 = (f32[2,24,1792]{2,1,0:T(8,128)}, f32[2,8,256]{2,1,0:T(8,128)}) custom-call(s32[16,16]{1,0:T(8,128)} %slice_bitcast_fusion.metas, f32[2,272,512]{2,1,0:T(8,128)} %get-tuple-element.12.g_own, f32[2,272,128]{2,1,0:T(8,128)} %get-tuple-element.13.g_sib, f32[2,8,8,5,8,128]{5,4,3,2,1,0:T(8,128)} %get-tuple-element.14.q_in, ...), custom_call_target="tpu_custom_call" | custom-call | tf_op jit(solution)/shard_map/update/pallas_call | solution.py:746
  163.6 1.7 %copy.16 = f32[2,24,1792]{2,1,0:T(8,128)} copy(f32[2,24,1792]{2,1,0:T(8,128)} %get-tuple-element.18) | data formatting | bytes 688128
  165.3 1.3 copy.17
  (1 shorter events, 0.0 us)

commit v3 on v2

v3 whole, which is shorter than its diff:
```python
import functools
import math

import jax
import jax.numpy as jnp
import numpy as np
from jax import lax
from jax.experimental import pallas as pl
from jax.experimental.pallas import tpu as pltpu
from jax.sharding import PartitionSpec as P

MESH = pl.DeviceIdType.MESH
SPLIT = 4
JITTER = 8
STEP = 96
PATCH = 256
MODES = 4
STRIP = 24
LANES = 128
OWN = 512
WIN = 640
ROWS = JITTER + 2 * STEP + 72
ZTOP = 104
KROWS = 408
KCOLS = 384
F32 = jnp.float32
BF16 = jnp.bfloat16


def mult(value, of):
    return pl.multiple_of(value, of)


class Messages:
    def __init__(self, send, recv):
        self.send, self.recv, self.count, self.open = send, recv, 0, []

    def make(self, src, dst, scan, when=None):
        at = self.count
        self.count += 1
        copy = pltpu.make_async_remote_copy(
            src_ref=src,
            dst_ref=dst,
            send_sem=self.send.at[at],
            recv_sem=self.recv.at[at],
            device_id={"scan": scan},
            device_id_type=MESH,
        )
        self.open.append((copy, when))
        return copy

    def drain(self):
        for copy, when in self.open:
            if when is None:
                copy.wait_send()
            else:
                pl.when(when)(copy.wait_send)
        self.open = []


def greet(peers):
    barrier = pltpu.get_barrier_semaphore()
    for peer in peers:
        pl.semaphore_signal(barrier, inc=1, device_id={"scan": peer}, device_id_type=MESH)
    pl.semaphore_wait(barrier, len(peers))


def long_way(me, step):
    line, at, q = me // 16, (me // SPLIT) % 4, me % SPLIT
    scale = 16

    def device(at_line, at_row):
        return (at_line + 8) % 8 * scale + (at_row + 8) % 4 * SPLIT + q

    def turn(row):
        row = (row + 8) % 4
        return jnp.where(jnp.logical_or(row == 0, row == 3), 0, 1)

    relay = device(line, at - step)
    origin = device(line, at + step)
    target = device(line + step * turn(at), at - step)
    source = device(line - step * turn(at + step), at + step)
    return relay, origin, target, source


def spread(n, kernel_pad, out, metas, line):
    me = lax.axis_index("scan")
    q = me % SPLIT
    line = line + jnp.where(q == SPLIT - 1, 1, 0)
    there = me // SPLIT - 2 + line
    inside = jnp.logical_and(there >= 0, there < n // SPLIT)
    start = mult(STRIP * q + STEP * (2 - line) - JITTER + ZTOP, 8)
    parts = out.shape[0]
    tall = STRIP + 2 * JITTER

    def one(col, carry):
        slot = line * SPLIT + col // SPLIT
        place = col % SPLIT
        top = metas[slot, 0, 2 * place]
        left = metas[slot, 0, 2 * place + 1]
        weight = jnp.where(jnp.logical_and(inside, place < metas[slot, 0, 8]), 1.0, 0.0).astype(F32)
        ahead = jnp.clip(STEP * there - top + JITTER, 0, 2 * JITTER)
        base = mult((STEP * col + 40) // LANES * LANES, LANES)
        shift = jnp.clip(left - base, 0, LANES)
        for part in range(parts):
            value = kernel_pad[part, pl.ds(start, tall), :]
            value = pltpu.roll(value, (tall - ahead) % tall, 0)[0:STRIP]
            value = pltpu.roll(value, shift, 1) * weight
            out[part, :, pl.ds(base, KCOLS)] += value
        return carry

    lax.fori_loop(0, 16, one, 0, unroll=4)


def step_kernel(
    n, offsets, live, meta, obj, probe_hbm, amps_hbm, cos, sin, new_obj, new_probe,
    metas_in, metas, probe, amps, win, relay_in, grad, patch, wave, half_done, far, sums9, ta, tb,
    q_in, sib_in, t2_in, t1_in, t8_in, back_in, far_in, piece, q_sib, acc, minus_in, plus_in, y_in,
    tile, dp, dp_in, kmine, ksib, kk, kpad, illum, place, dobj, vec, vec1, vec2,
    send, recv, ysem, kysem, kxsem, v1sem, v2sem, bsend, dpsem, psem, lsem,
    gsend, ownsem, aheadsem, relaysem, finalsem, tailsem, mrecv, msem,
):
    me = lax.axis_index("scan")
    q = me % SPLIT
    core = me % 2
    first = me - q
    row = me // SPLIT
    rows_all = n // SPLIT
    up = (me - SPLIT + n) % n
    down = (me + SPLIT) % n
    sibling = me + 1 - 2 * core
    side = 8
    x, y = me // (2 * side), (me // 2) % side
    msg = Messages(send, recv)

    def chip(at_x, at_y, at_core):
        return ((at_x % side) * side + at_y % side) * 2 + at_core

    def columns(quarter):
        return pl.ds(mult(768 * (quarter // 2) + OWN * (quarter % 2), LANES), OWN)

    def rows(start, size):
        return pl.ds(mult(start, 8), size)

    load_probe = pltpu.make_async_copy(probe_hbm, probe, lsem.at[0])
    load_probe.start()
    load_amps = pltpu.make_async_copy(amps_hbm, amps, lsem.at[1])
    load_amps.start()
    peers = [(first + SPLIT * e + k + 2 * n) % n for e in (-2, -1, 1, 2) for k in range(SPLIT)]
    peers += [chip(x + k, y, cc) for k in range(1, side) for cc in range(2)]
    peers += [chip(x, y + k, cc) for k in range(1, side) for cc in range(2)]
    peers += [sibling]
    greet(peers)

    sends = []

    def put(src, dst, recv_sem, there, when=None):
        copy = pltpu.make_async_remote_copy(
            src_ref=src,
            dst_ref=dst,
            send_sem=gsend.at[len(sends)],
            recv_sem=recv_sem,
            device_id={"scan": there},
            device_id_type=MESH,
        )
        sends.append((copy, when))
        if when is None:
            copy.start()
        else:
            pl.when(when)(copy.start)

    def landing(quarter, start, size=STRIP):
        return win.at[:, rows(start, size), pl.ds(mult(LANES * (quarter % 2), LANES), OWN)]

    relay, origin, target, source = long_way(me, -1)
    middle = jnp.logical_or(q == 1, q == 2)
    middle_at = jnp.clip(q - 1, 0, 1)
    around = [(q + k) % SPLIT for k in range(SPLIT)]
    for there in around:
        block = obj.at[:, :, columns(there)]
        put(block, relay_in.at[middle_at], relaysem.at[middle_at], relay - q + there, when=middle)
        put(block, landing(there, JITTER + STEP + STRIP * q), aheadsem.at[q], (first - SPLIT + there + n) % n)
    for there in around[1:]:
        block = obj.at[:, :, columns(there)]
        put(block, landing(there, JITTER + STRIP * q), ownsem.at[q], first + there)
    for there in around:
        block = obj.at[:, pl.ds(STRIP - JITTER, JITTER), columns(there)]
        put(block, landing(there, 0, JITTER), tailsem, (first + SPLIT + there) % n, when=q == SPLIT - 1)
    for e in (-1, 0, 1, 2):
        for k in range(SPLIT):
            if e or k:
                there = (first + SPLIT * e + (q + k) % SPLIT + n) % n
                put(meta, metas_in.at[(2 - e) * SPLIT + q], mrecv, there)
    own_at = mult(LANES * core, LANES)
    own_cols = pl.ds(own_at, OWN)
    sib_cols = pl.ds(mult(OWN * (1 - core), LANES), LANES)
    win[:, rows(JITTER + STRIP * q, STRIP), own_cols] = obj[:, :, columns(q)]
    metas_in[2 * SPLIT + q] = meta[...]

    c, s = cos[...], sin[...]
    ta[0:256, 0:256] = c
    ta[0:256, 256:512] = s
    ta[256:512, 0:256] = -s
    ta[256:512, 256:512] = c
    tb[0:256, 0:256] = c
    tb[0:256, 256:512] = -s
    tb[256:512, 0:256] = s
    tb[256:512, 256:512] = c
    grad[...] = jnp.zeros_like(grad)
    sums9[...] = jnp.zeros_like(sums9)
    kpad[...] = jnp.zeros_like(kpad)
    illum[...] = jnp.zeros_like(illum)
    place[...] = jnp.zeros_like(place)
    dobj[...] = jnp.zeros_like(dobj)
    win[:, ROWS:, :] = jnp.zeros((2, 16, WIN), F32)
    load_probe.wait()
    light = jnp.zeros((PATCH, PATCH), F32)
    for m in range(MODES):
        light = light + (probe[0, m] * probe[0, m] + probe[1, m] * probe[1, m])
    kpad[0, ZTOP : ZTOP + PATCH, 0:PATCH] = light

    def arrived(ref, sem):
        return pltpu.make_async_copy(ref, ref, sem)

    def border(start, size):
        mine = pl.ds(mult(LANES * core + 384 * (1 - core), LANES), LANES)
        src = win.at[:, pl.ds(start, size), mine]
        dst = win.at[:, pl.ds(start, size), pl.ds(mult(OWN * core, LANES), LANES)]
        copy = msg.make(src, dst, sibling)
        copy.start()
        return copy

    def far_on(j):
        arrived(relay_in.at[j - 1], relaysem.at[j - 1]).wait()
        put(relay_in.at[j - 1], landing(q, JITTER + 2 * STEP + STRIP * j), finalsem.at[j], target)

    for j in range(SPLIT):
        pl.when(q != j)(arrived(landing(q, JITTER + STRIP * j), ownsem.at[j]).wait)
        if j == 0:
            arrived(landing(q, JITTER + STEP), aheadsem.at[0]).wait()
            put(landing(q, JITTER + STEP), landing(q, JITTER + 2 * STEP), finalsem.at[0], up)
            far_on(1)
        if j == 1:
            far_on(2)
    borders = [border(JITTER, STEP)]
    arrived(metas_in.at[pl.ds(0, 15)], mrecv).wait()
    to_smem = pltpu.make_async_copy(metas_in, metas, msem)
    to_smem.start()
    to_smem.wait()
    for line in range(3):
        spread(n, kpad.at[pl.ds(0, 1)], illum, metas, line)
    arrived(landing(q, 0, JITTER), tailsem).wait()
    borders.append(border(0, JITTER))
    for j in range(1, SPLIT):
        arrived(landing(q, JITTER + STEP + STRIP * j), aheadsem.at[j]).wait()
    borders.append(border(JITTER + STEP, STEP))
    for j in range(3):
        arrived(landing(q, JITTER + 2 * STEP + STRIP * j), finalsem.at[j]).wait()
    borders.append(border(JITTER + 2 * STEP, 72))
    load_amps.wait()
    for copy in borders:
        copy.wait_recv()

    def clear_outside(ref):
        @pl.when(row == 0)
        def _():
            ref[:, 0:JITTER, :] = jnp.zeros((2, JITTER, WIN), F32)

        @pl.when(row == rows_all - 1)
        def _():
            ref[:, JITTER + STEP : JITTER + 2 * STEP, :] = jnp.zeros((2, STEP, WIN), F32)

        @pl.when(row >= rows_all - 2)
        def _():
            ref[:, JITTER + 2 * STEP : ROWS, :] = jnp.zeros((2, 72, WIN), F32)

    msg.drain()
    for copy, when in sends:
        if when is None:
            copy.wait_send()
        else:
            pl.when(when)(copy.wait_send)
    clear_outside(win)

    chunk = 32
    chunks = PATCH // chunk
    slab = chunk + 2 * JITTER

    def transform(left, right):
        for m in range(MODES):
            cols = slice(m * PATCH, (m + 1) * PATCH)
            z = jnp.dot(left[...], wave[:, cols], preferred_element_type=F32)
            half_done[cols, 0:PATCH] = z[0:PATCH].astype(BF16)
            half_done[cols, PATCH : 2 * PATCH] = z[PATCH : 2 * PATCH].astype(BF16)
        for m in range(MODES):
            cols = slice(m * PATCH, (m + 1) * PATCH)
            far[m] = jnp.dot(half_done[cols, :], right[...], preferred_element_type=F32)

    def visit(p, carry):
        ahead = jnp.clip(offsets[p, 0] - (STEP * row - JITTER), 0, 2 * JITTER)
        base = mult((STEP * p + 40) // LANES * LANES, LANES)
        shift = jnp.clip(offsets[p, 1] - STEP * SPLIT * q - base, 0, LANES)
        weight = jnp.where(p < live[0], 1.0, 0.0).astype(F32)

        def exits(i, carry):
            at = pl.ds(mult(i * chunk, chunk), chunk)
            low = pl.ds(mult(PATCH + i * chunk, chunk), chunk)
            o = []
            for part in range(2):
                v = win[part, pl.ds(mult(i * chunk, chunk), slab), pl.ds(base, KCOLS)]
                v = pltpu.roll(v, (slab - ahead) % slab, 0)[0:chunk]
                v = pltpu.roll(v, KCOLS - shift, 1)[:, 0:PATCH]
                patch[part, at, :] = v
                o.append(v)
            for m in range(MODES):
                pr, pi = probe[0, m, at, :], probe[1, m, at, :]
                wave[at, m * PATCH : (m + 1) * PATCH] = (pr * o[0] - pi * o[1]).astype(BF16)
                wave[low, m * PATCH : (m + 1) * PATCH] = (pr * o[1] + pi * o[0]).astype(BF16)
            return carry

        lax.fori_loop(0, chunks, exits, 0)
        transform(ta, tb)

        def changes(i, carry):
            at = pl.ds(mult(i * chunk, chunk), chunk)
            low = pl.ds(mult(PATCH + i * chunk, chunk), chunk)
            bright = jnp.zeros((chunk, PATCH), F32)
            for m in range(MODES):
                fr, fi = far[m, at, 0:PATCH], far[m, at, PATCH : 2 * PATCH]
                bright = bright + (fr * fr + fi * fi)
            factor = (amps[p, at, :] / jnp.maximum(jnp.sqrt(bright), 0.5) - 1.0) * weight
            for m in range(MODES):
                fr, fi = far[m, at, 0:PATCH], far[m, at, PATCH : 2 * PATCH]
                wave[at, m * PATCH : (m + 1) * PATCH] = (fr * factor).astype(BF16)
                wave[low, m * PATCH : (m + 1) * PATCH] = (fi * factor).astype(BF16)
            return carry

        lax.fori_loop(0, chunks, changes, 0)
        transform(tb, ta)

        def grads(i, carry):
            at = pl.ds(mult(i * chunk, chunk), chunk)
            o_re, o_im = patch[0, at, :], patch[1, at, :]
            g_re = jnp.zeros((chunk, PATCH), F32)
            g_im = jnp.zeros((chunk, PATCH), F32)
            for m in range(MODES):
                pr, pi = probe[0, m, at, :], probe[1, m, at, :]
                cr, ci = far[m, at, 0:PATCH], far[m, at, PATCH : 2 * PATCH]
                g_re = g_re + (pr * cr + pi * ci)
                g_im = g_im + (pr * ci - pi * cr)
                sums9[m, at, :] += o_re * cr + o_im * ci
                sums9[MODES + m, at, :] += o_re * ci - o_im * cr
            sums9[2 * MODES, at, :] += (o_re * o_re + o_im * o_im) * weight
            blank = jnp.zeros((chunk, KCOLS - PATCH), F32)
            below = jnp.zeros((2 * JITTER, KCOLS), F32)
            for part, g in enumerate((g_re, g_im)):
                v = pltpu.roll(jnp.concatenate([g, blank], 1), shift, 1)
                v = pltpu.roll(jnp.concatenate([v, below], 0), ahead, 0)
                grad[part, pl.ds(mult(i * chunk, chunk), slab), pl.ds(base, KCOLS)] += v
            return carry

        lax.fori_loop(0, chunks, grads, 0)
        return carry

    lax.fori_loop(0, SPLIT, visit, 0)
    clear_outside(grad)

    to_sib = msg.make(grad.at[:, pl.ds(0, ROWS), sib_cols], sib_in, sibling)
    to_sib.start()
    for at_band in range(PATCH // 8):
        yy = (at_band // 2) % 8
        for at_lane in range(2):
            xx = (at_band // 16) * 4 + (at_band % 2) * 2 + at_lane
            at_rows = slice(8 * at_band, 8 * at_band + 8)
            at_cols = slice(LANES * at_lane, LANES * at_lane + LANES)
            for k in range(2):
                for i, m in enumerate((2 * k, 2 * k + 1, MODES + 2 * k, MODES + 2 * k + 1, 8)):
                    q_in[k, xx, yy, i] = sums9[m, at_rows, at_cols]
    chunks = [(x + k) % side for k in (4, 5, 3, 6, 2, 7, 1, 0)]
    q_copies = []
    for at in chunks:
        copy = msg.make(q_in.at[1 - core, at], q_sib.at[at], sibling)
        copy.start()
        q_copies.append(copy)
    relay, origin, target, source = long_way(me, 1)

    band = (x // 4) * 16 + y * 2 + (x // 2) % 2
    lane = x % 2
    out_mode = x // 2
    out_band = (x % 2) * 16 + y * 2 + core
    p_tile = probe[:, pl.ds(2 * core, 2), pl.ds(mult(8 * band, 8), 8), pl.ds(mult(LANES * lane, LANES), LANES)]

    to_sib.wait_recv()
    edge = pl.ds(mult(LANES * core + 384 * (1 - core), LANES), LANES)
    grad[:, 0:ROWS, edge] += sib_in[...]

    def sums(start):
        return grad.at[:, pl.ds(start, STRIP), own_cols]

    def add_sibling(i):
        q_copies[i].wait_recv()
        acc[chunks[i]] = q_in[core, chunks[i]] + q_sib[chunks[i]]

    halves = side // 2

    def send_chain(way, i):
        which = (i % 2 if way < 0 else 1 - i % 2) * halves
        reach = (4 if i % 2 == 0 else 3) - i // 2
        dest = (x + way * reach + side) % side
        copy = msg.make(
            acc.at[dest, pl.ds(which, halves)],
            (minus_in if way < 0 else plus_in).at[i],
            chip(x + way + side, y, core),
        )
        copy.start()
        return copy

    chains = {}
    add_sibling(0)
    chains[-1, 0], chains[1, 0] = send_chain(-1, 0), send_chain(1, 0)
    add_sibling(1)
    chains[-1, 1] = send_chain(-1, 1)
    add_sibling(2)
    chains[1, 1] = send_chain(1, 1)
    far_out = []
    for j in (1, 2):
        copy = msg.make(sums(JITTER + 2 * STEP + STRIP * j), back_in.at[j - 1], relay)
        copy.start()
        far_out.append(copy)
    t2 = msg.make(sums(JITTER + 2 * STEP), t2_in, down)
    t2.start()
    t8 = msg.make(grad.at[:, pl.ds(0, JITTER), own_cols], t8_in, up)
    t8.start()

    def send_t1(j):
        copy = msg.make(sums(JITTER + STEP + STRIP * j), t1_in.at[j], down)
        copy.start()
        return copy

    t1 = {3: send_t1(3)}

    for i in range(3, 8):
        add_sibling(i)

    def x_step(i):
        for way, arrived in ((-1, minus_in), (1, plus_in)):
            which = (i % 2 if way < 0 else 1 - i % 2) * halves
            reach = (4 if i % 2 == 0 else 3) - 1 - i // 2
            dest = (x + way * reach + side) % side
            chains[way, i].wait_recv()
            acc[dest, which : which + halves] += arrived[i]
            if reach > 0:
                chains[way, i + 2] = send_chain(way, i + 2)

    x_step(0)
    t1[1] = send_t1(1)
    x_step(1)
    t1[2] = send_t1(2)
    x_step(2)
    t2.wait_recv()
    grad[:, JITTER + STEP : JITTER + STEP + STRIP, own_cols] += t2_in[...]
    t1[0] = send_t1(0)
    x_step(3)
    far_final = []
    for j in range(2):
        far_out[j].wait_recv()
        copy = msg.make(back_in.at[j], far_in.at[j], target)
        copy.start()
        far_final.append(copy)
    x_step(4)
    x_step(5)
    x_step(6)

    y_copies = []
    for k in range(1, side):
        copy = pltpu.make_async_remote_copy(
            src_ref=acc.at[x, (y + k) % side],
            dst_ref=y_in.at[k - 1],
            send_sem=bsend.at[k - 1],
            recv_sem=ysem,
            device_id={"scan": chip(x, y + k, core)},
            device_id_type=MESH,
        )
        copy.start()
        y_copies.append(copy)
    pltpu.make_async_copy(y_in, y_in, ysem).wait()
    tile[...] = acc[x, y] + jnp.sum(y_in[...], 0)
    norm = tile[4]
    inverse = norm + 1.0
    k_re = jnp.zeros((8, LANES), F32)
    k_im = jnp.zeros((8, LANES), F32)
    s_vv = jnp.zeros((8, LANES), F32)
    s_vc = jnp.zeros((8, LANES), F32)
    for m in range(2):
        g_re, g_im = tile[m], tile[2 + m]
        d_re, d_im = g_re / inverse, g_im / inverse
        dp[m, 0] = d_re
        dp[m, 1] = d_im
        p_re, p_im = p_tile[0, m], p_tile[1, m]
        k_re = k_re + (p_re * d_re + p_im * d_im)
        k_im = k_im + (p_re * d_im - p_im * d_re)
        s_vv = s_vv + (d_re * d_re + d_im * d_im) * norm
        s_vc = s_vc + (d_re * g_re + d_im * g_im)
    kmine[0] = k_re
    kmine[1] = k_im
    k_copy = msg.make(kmine.at[1 - core], ksib, sibling)
    k_copy.start()

    dp_sends = []
    for m in range(2):
        dest = chip(2 * (2 * core + m) + x // 4, y, (x // 2) % 2)
        away = dest != me
        copy = pltpu.make_async_remote_copy(
            src_ref=dp.at[m],
            dst_ref=dp_in.at[lane],
            send_sem=bsend.at[21 + m],
            recv_sem=dpsem.at[lane],
            device_id={"scan": dest},
            device_id_type=MESH,
        )
        pl.when(away)(copy.start)
        dp_sends.append((copy, away))

        @pl.when(jnp.logical_not(away))
        def _():
            dp_in[lane] = dp[m]

    k_copy.wait_recv()
    kk[core, x, y] = kmine[core] + ksib[...]
    ky_copies = []
    for k in range(1, side):
        copy = pltpu.make_async_remote_copy(
            src_ref=kk.at[core, x, y],
            dst_ref=kk.at[core, x, y],
            send_sem=bsend.at[7 + k - 1],
            recv_sem=kysem,
            device_id={"scan": chip(x, y + k, core)},
            device_id_type=MESH,
        )
        copy.start()
        ky_copies.append(copy)

    pieces = []
    for j in (3, 1, 2, 0):
        t1[j].wait_recv()
        lo = JITTER + STRIP * j
        grad[:, lo : lo + STRIP, own_cols] += t1_in[j]
        if j == 3:
            t8.wait_recv()
            grad[:, STEP : STEP + JITTER, own_cols] += t8_in[...]
        if j in (1, 2):
            far_final[j - 1].wait_recv()
            grad[:, lo : lo + STRIP, own_cols] += far_in[j - 1]
        slot = (j - q + SPLIT) % SPLIT
        copy = pltpu.make_async_remote_copy(
            src_ref=grad.at[:, pl.ds(lo, STRIP), own_cols],
            dst_ref=piece.at[slot],
            send_sem=bsend.at[23 + j],
            recv_sem=psem.at[slot],
            device_id={"scan": first + j},
            device_id_type=MESH,
        )
        pl.when(q != j)(copy.start)
        pieces.append((copy, q != j))

    pltpu.make_async_copy(kk.at[0, 0, pl.ds(0, 7)], kk.at[0, 0, pl.ds(0, 7)], kysem).wait()
    kx_copies = []
    for k in range(1, side):
        copy = pltpu.make_async_remote_copy(
            src_ref=kk.at[core, x],
            dst_ref=kk.at[core, x],
            send_sem=bsend.at[14 + k - 1],
            recv_sem=kxsem,
            device_id={"scan": chip(x + k, y, core)},
            device_id_type=MESH,
        )
        copy.start()
        kx_copies.append(copy)
    piece[0] = grad[:, pl.ds(mult(JITTER + STRIP * q, 8), STRIP), own_cols]

    pltpu.make_async_copy(kk.at[0, pl.ds(0, 7)], kk.at[0, pl.ds(0, 7)], kxsem).wait()
    ks_copy = msg.make(kk.at[core], kk.at[core], sibling)
    ks_copy.start()

    for k in range(SPLIT):
        if k > 0:
            pltpu.make_async_copy(piece.at[k], piece.at[k], psem.at[k]).wait()
        source = (q - k + SPLIT) % SPLIT
        at = pl.ds(mult(768 * (source // 2) + OWN * (source % 2), LANES), OWN)
        dobj[:, :, at] += piece[k]
    bright = illum[0]
    g_re, g_im = dobj[0], dobj[1]
    o_re, o_im = obj[0], obj[1]
    d_re, d_im = g_re / (bright + 1.0), g_im / (bright + 1.0)
    s_uu = jnp.sum((d_re * d_re + d_im * d_im) * bright)
    s_uc = jnp.sum(d_re * g_re + d_im * g_im)
    dobj[0] = d_re
    dobj[1] = d_im

    ks_copy.wait_recv()
    for at_band in range(PATCH // 8):
        for at_lane in range(2):
            xx = (at_band // 16) * 4 + (at_band % 2) * 2 + at_lane
            yy = (at_band // 2) % 8
            rows = slice(ZTOP + 8 * at_band, ZTOP + 8 * at_band + 8)
            cols = slice(LANES * at_lane, LANES * at_lane + LANES)
            kpad[0, rows, cols] = kk[0, xx, yy]
            kpad[1, rows, cols] = kk[1, xx, yy]
    for line in range(3):
        spread(n, kpad, place, metas, line)
    d_re, d_im = dobj[0], dobj[1]
    s_uv = jnp.sum(
        place[0] * (d_re * o_re + d_im * o_im) - place[1] * (d_re * o_im - d_im * o_re)
    )

    at = lax.broadcasted_iota(jnp.int32, (8, LANES), 1)
    own_sums = jnp.zeros((8, LANES), F32)
    for i, value in enumerate((s_uu, s_uv, jnp.sum(s_vv), s_uc, jnp.sum(s_vc))):
        own_sums = jnp.where(at == i, value, own_sums)
    vec[...] = own_sums
    v1_copies = []
    for k in range(1, 2 * side):
        copy = pltpu.make_async_remote_copy(
            src_ref=vec,
            dst_ref=vec1.at[k - 1],
            send_sem=bsend.at[27 + k - 1],
            recv_sem=v1sem,
            device_id={"scan": chip(x, y + k // 2, (core + k) % 2)},
            device_id_type=MESH,
        )
        copy.start()
        v1_copies.append(copy)
    pltpu.make_async_copy(vec1, vec1, v1sem).wait()
    for copy in v1_copies:
        copy.wait_send()
    vec[...] = own_sums + jnp.sum(vec1[...], 0)
    v2_copies = []
    for k in range(1, side):
        copy = pltpu.make_async_remote_copy(
            src_ref=vec,
            dst_ref=vec2.at[k - 1],
            send_sem=bsend.at[42 + k - 1],
            recv_sem=v2sem,
            device_id={"scan": chip(x + k, y, core)},
            device_id_type=MESH,
        )
        copy.start()
        v2_copies.append(copy)
    for at_lane in range(2):
        source = chip((x % 2) * 4 + core * 2 + at_lane, y, x // 4)
        arrived = pltpu.make_async_copy(dp_in.at[at_lane], dp_in.at[at_lane], dpsem.at[at_lane])
        pl.when(source != me)(arrived.wait)
    pltpu.make_async_copy(vec2, vec2, v2sem).wait()
    totals = vec[...] + jnp.sum(vec2[...], 0)
    uu, uv, vv, uc, vc = (totals[0:1, i : i + 1] for i in range(5))
    a = 1.1 * uu + 1e-06
    d = 1.1 * vv + 1e-06
    det = a * d - uv * uv
    rate_obj = (uc * d - uv * vc) / det
    rate_probe = (a * vc - uv * uc) / det
    for part in range(2):
        new_obj[part] = obj[part] + rate_obj * dobj[part]
        for at_lane in range(2):
            cols = slice(LANES * at_lane, LANES * at_lane + LANES)
            new_probe[part, :, cols] = probe[part, out_mode, pl.ds(mult(8 * out_band, 8), 8), cols] + rate_probe * dp_in[at_lane, part]

    msg.drain()
    for copy in y_copies + ky_copies + kx_copies + v2_copies:
        copy.wait_send()
    for copy, when in dp_sends + pieces:
        pl.when(when)(copy.wait_send)


def step(n, offsets, live, meta, obj, probe, amps, cos, sin):
    vmem = pl.BlockSpec(memory_space=pltpu.VMEM)
    smem = pl.BlockSpec(memory_space=pltpu.SMEM)
    hbm = pl.BlockSpec(memory_space=pl.ANY)
    dma = pltpu.SemaphoreType.DMA
    columns = obj.shape[2]

    def f32(*shape):
        return pltpu.VMEM(shape, F32)

    return pl.pallas_call(
        functools.partial(step_kernel, n),
        out_shape=(
            jax.ShapeDtypeStruct((2, STRIP, columns), F32),
            jax.ShapeDtypeStruct((2, 8, PATCH), F32),
        ),
        in_specs=[smem, smem, vmem, vmem, hbm, hbm, vmem, vmem],
        out_specs=[vmem] * 2,
        scratch_shapes=[
            pltpu.VMEM((4 * SPLIT, 8, LANES), jnp.int32),
            pltpu.SMEM((4 * SPLIT, 8, LANES), jnp.int32),
            f32(2, MODES, PATCH, PATCH),
            f32(SPLIT, PATCH, PATCH),
            f32(2, ROWS + 16, WIN),
            f32(2, 2, STRIP, OWN),
            f32(2, ROWS + 16, WIN),
            f32(2, PATCH, PATCH),
            pltpu.VMEM((2 * PATCH, MODES * PATCH), BF16),
            pltpu.VMEM((MODES * PATCH, 2 * PATCH), BF16),
            f32(MODES, PATCH, 2 * PATCH),
            f32(2 * MODES + 1, PATCH, PATCH),
            pltpu.VMEM((2 * PATCH, 2 * PATCH), BF16),
            pltpu.VMEM((2 * PATCH, 2 * PATCH), BF16),
            f32(2, 8, 8, 5, 8, LANES),
            f32(2, ROWS, LANES),
            f32(2, STRIP, OWN),
            f32(4, 2, STRIP, OWN),
            f32(2, JITTER, OWN),
            f32(2, 2, STRIP, OWN),
            f32(2, 2, STRIP, OWN),
            f32(4, 2, STRIP, OWN),
            f32(8, 8, 5, 8, LANES),
            f32(8, 8, 5, 8, LANES),
            f32(7, 4, 5, 8, LANES),
            f32(7, 4, 5, 8, LANES),
            f32(7, 5, 8, LANES),
            f32(5, 8, LANES),
            f32(2, 2, 8, LANES),
            f32(2, 2, 8, LANES),
            f32(2, 8, LANES),
            f32(8, LANES),
            f32(2, 8, 8, 8, LANES),
            f32(2, KROWS, KCOLS),
            f32(1, STRIP, columns),
            f32(2, STRIP, columns),
            f32(2, STRIP, columns),
            f32(8, LANES),
            f32(15, 8, LANES),
            f32(7, 8, LANES),
            dma((48,)),
            dma((48,)),
            dma,
            dma,
            dma,
            dma,
            dma,
            dma((50,)),
            dma((2,)),
            dma((4,)),
            dma((2,)),
            dma((40,)),
            dma((4,)),
            dma((4,)),
            dma((2,)),
            dma((3,)),
            dma,
            dma,
            dma,
        ],
        compiler_params=pltpu.CompilerParams(collective_id=0, has_side_effects=True),
        name="step",
    )(offsets, live, meta, obj, probe, amps, cos, sin)


def tables(length):
    numbers = np.arange(length, dtype=np.int64)
    angles = (numbers[:, None] * numbers[None, :] % length).astype(np.float32)
    angles = angles * np.float32(2.0 * math.pi / length)
    scaling = np.float32(1.0 / math.sqrt(length))
    return tuple(jnp.asarray(f(angles) * scaling).astype(BF16) for f in (np.cos, np.sin))


def on_device(n, object_field, probe_field, amplitudes, offsets, live_counts):
    probe = probe_field.reshape(2, MODES, PATCH, PATCH)
    meta = jnp.concatenate([offsets.reshape(-1), live_counts])
    meta = jnp.broadcast_to(jnp.pad(meta, (0, LANES - meta.shape[0]))[None], (8, LANES))
    cos, sin = tables(PATCH)
    return step(n, offsets, live_counts, meta, object_field, probe, amplitudes, cos, sin)


def solution(mesh):
    groups_scan = ("groups", "scan")
    placed = (
        P(None, groups_scan, None),
        P(None, "groups", None),
        P(groups_scan, None, None),
        P(groups_scan, None),
        P(groups_scan),
    )
    return jax.shard_map(
        functools.partial(on_device, mesh.shape["scan"]),
        mesh=mesh,
        in_specs=placed,
        out_specs=(P(None, groups_scan, None), P(None, groups_scan, None)),
        check_vma=False,
    )
```

time: 165 us -> 151 us (0.915); the launches traced: 167 us -> 151 us
  Pallas kernels: 159 us -> 145 us
    pallas_call x3 -> x1, Pallas kernels: 159 us -> 145 us  [step(): pl.pallas_call(functools.partial(step_kernel, n), out_shape=(jax.ShapeDty...]
    unnamed x3 -> x5, local copies, waits for them, and re-layouts: 3.82 us -> 3.82 us
where the time goes in v3:
time: 151 us
  Pallas kernels  145 us (96%)
  local copies, waits for them, and re-layouts  4.51 us (3%)
    pallas_call x1, Pallas kernels, step(): pl.pallas_call(functools.partial(step_kernel, n), out_shape=(jax.ShapeDty...  145 us
    unnamed x5, local copies, waits for them, and re-layouts  3.82 us

profile of v3, /device:TPU:513, one launch (start us, length us, event | category | flops | bytes accessed | tf_op | source)
XLA Modules:
  0.0 150.8 jit_solution(8948523682739228284)
XLA Ops:
  1.3 0.8 copy.12.offsets
  2.0 0.0 copy-start
  2.0 0.1 reshape.11
  2.1 0.1 pad_add_fusion
  2.2 0.6 broadcast_in_dim.2.meta
  2.8 0.0 copy-done
  2.8 144.9 %step.1 = (f32[2,24,1792]{2,1,0:T(8,128)}, f32[2,8,256]{2,1,0:T(8,128)}) custom-call(s32[4,2]{1,0:T(4,128)} %copy-done, s32[1]{0:T(128)S(6)} %copy.15.live, s32[8,128]{1,0:T(8,128)} %broadcast_in_dim.2.meta, f32[2,24,1792]{2,1,0:T(8,128)} %obj.1, f32[2,4,256,256]{3,2,1,0:T(8,128)} %bitcast.1, f32[4,256,256]{2,1,0:T(8,128)} %amps_hbm.1, ...), custom_call_target="tpu_custom_call" | custom-call | tf_op jit(solution)/shard_map/step/pallas_call | solution.py:684
  147.7 1.7 %copy.16 = f32[2,24,1792]{2,1,0:T(8,128)} copy(f32[2,24,1792]{2,1,0:T(8,128)} %get-tuple-element.4) | data formatting | bytes 688128
  149.5 1.3 copy.17
  (1 shorter events, 0.0 us)
Async XLA Ops:
  2.0 0.8 copy-start

commit v4 on v3

--- a/solution.py
+++ b/solution.py
@@ -38,6 +38,7 @@
     def make(self, src, dst, scan, when=None):
         at = self.count
         self.count += 1
+        self.last = self.recv.at[at]
         copy = pltpu.make_async_remote_copy(
             src_ref=src,
             dst_ref=dst,
@@ -115,10 +116,10 @@
 def step_kernel(
     n, offsets, live, meta, obj, probe_hbm, amps_hbm, cos, sin, new_obj, new_probe,
     metas_in, metas, probe, amps, win, relay_in, grad, patch, wave, half_done, far, sums9, ta, tb,
-    q_in, sib_in, t2_in, t1_in, t8_in, back_in, far_in, piece, q_sib, acc, minus_in, plus_in, y_in,
+    q_in, sib_in, t2_in, t1_in, t8_in, back_in, far_in, piece, q_sib, acc, minus_in, plus_in, y_in, hold_t1, hold_far,
     tile, dp, dp_in, kmine, ksib, kk, kpad, illum, place, dobj, vec, vec1, vec2,
     send, recv, ysem, kysem, kxsem, v1sem, v2sem, bsend, dpsem, psem, lsem,
-    gsend, ownsem, aheadsem, relaysem, finalsem, tailsem, mrecv, msem,
+    gsend, ownsem, aheadsem, relaysem, finalsem, tailsem, mrecv, msem, holdsem,
 ):
     me = lax.axis_index("scan")
     q = me % SPLIT
@@ -172,6 +173,11 @@
     def landing(quarter, start, size=STRIP):
         return win.at[:, rows(start, size), pl.ds(mult(LANES * (quarter % 2), LANES), OWN)]
 
+    for e in (-1, 0, 1, 2):
+        for k in range(SPLIT):
+            if e or k:
+                there = (first + SPLIT * e + (q + k) % SPLIT + n) % n
+                put(meta, metas_in.at[(2 - e) * SPLIT + q], mrecv, there)
     relay, origin, target, source = long_way(me, -1)
     middle = jnp.logical_or(q == 1, q == 2)
     middle_at = jnp.clip(q - 1, 0, 1)
@@ -186,11 +192,6 @@
     for there in around:
         block = obj.at[:, pl.ds(STRIP - JITTER, JITTER), columns(there)]
         put(block, landing(there, 0, JITTER), tailsem, (first + SPLIT + there) % n, when=q == SPLIT - 1)
-    for e in (-1, 0, 1, 2):
-        for k in range(SPLIT):
-            if e or k:
-                there = (first + SPLIT * e + (q + k) % SPLIT + n) % n
-                put(meta, metas_in.at[(2 - e) * SPLIT + q], mrecv, there)
     own_at = mult(LANES * core, LANES)
     own_cols = pl.ds(own_at, OWN)
     sib_cols = pl.ds(mult(OWN * (1 - core), LANES), LANES)
@@ -243,12 +244,6 @@
         if j == 1:
             far_on(2)
     borders = [border(JITTER, STEP)]
-    arrived(metas_in.at[pl.ds(0, 15)], mrecv).wait()
-    to_smem = pltpu.make_async_copy(metas_in, metas, msem)
-    to_smem.start()
-    to_smem.wait()
-    for line in range(3):
-        spread(n, kpad.at[pl.ds(0, 1)], illum, metas, line)
     arrived(landing(q, 0, JITTER), tailsem).wait()
     borders.append(border(0, JITTER))
     for j in range(1, SPLIT):
@@ -257,6 +252,9 @@
     for j in range(3):
         arrived(landing(q, JITTER + 2 * STEP + STRIP * j), finalsem.at[j]).wait()
     borders.append(border(JITTER + 2 * STEP, 72))
+    arrived(metas_in.at[pl.ds(0, 15)], mrecv).wait()
+    to_smem = pltpu.make_async_copy(metas_in, metas, msem)
+    to_smem.start()
     load_amps.wait()
     for copy in borders:
         copy.wait_recv()
@@ -432,13 +430,49 @@
     t8 = msg.make(grad.at[:, pl.ds(0, JITTER), own_cols], t8_in, up)
     t8.start()
 
-    def send_t1(j):
-        copy = msg.make(sums(JITTER + STEP + STRIP * j), t1_in.at[j], down)
-        copy.start()
-        return copy
-
-    t1 = {3: send_t1(3)}
-
+    at_row = (me // SPLIT) % 4
+    crossing = at_row == 3
+    holder = at_row == 0
+    turning = jnp.logical_or(at_row == 1, at_row == 2)
+    far_holder = at_row <= 1
+    below = x * 2 * side + (at_row + 1) % 4 * SPLIT + q
+    beside = chip(x + 1, y, core)
+
+    def start_t1(j):
+        src = sums(JITTER + STEP + STRIP * j)
+        t1[j] = msg.make(src, t1_in.at[j], below, when=jnp.logical_not(crossing))
+        final_sem = msg.last
+        pl.when(jnp.logical_not(crossing))(t1[j].start)
+        copy = msg.make(src, hold_t1.at[j], below, when=crossing)
+        pl.when(crossing)(copy.start)
+        held.append((copy, holder, hold_t1.at[j], t1_in.at[j], final_sem))
+
+    def pass_far(j):
+        there = x * 2 * side + (at_row + 3) % 4 * SPLIT + q
+        final = msg.make(back_in.at[j], far_in.at[j], there, when=jnp.logical_not(turning))
+        final_sem = msg.last
+        pl.when(jnp.logical_not(turning))(final.start)
+        copy = msg.make(back_in.at[j], hold_far.at[j], there, when=turning)
+        pl.when(turning)(copy.start)
+        held.append((copy, far_holder, hold_far.at[j], far_in.at[j], final_sem))
+        return final
+
+    def release(i):
+        copy, here, src, dst, final_sem = held[i]
+        pl.when(here)(copy.wait_recv)
+        onward = pltpu.make_async_remote_copy(
+            src_ref=src,
+            dst_ref=dst,
+            send_sem=holdsem.at[i],
+            recv_sem=final_sem,
+            device_id={"scan": beside},
+            device_id_type=MESH,
+        )
+        pl.when(here)(onward.start)
+        msg.open.append((onward, here))
+
+    t1, held = {}, []
+    start_t1(3)
     for i in range(3, 8):
         add_sibling(i)
 
@@ -452,22 +486,24 @@
             if reach > 0:
                 chains[way, i + 2] = send_chain(way, i + 2)
 
+    to_smem.wait()
     x_step(0)
-    t1[1] = send_t1(1)
+    start_t1(1)
+    spread(n, kpad.at[pl.ds(0, 1)], illum, metas, 0)
     x_step(1)
-    t1[2] = send_t1(2)
+    start_t1(2)
+    spread(n, kpad.at[pl.ds(0, 1)], illum, metas, 1)
     x_step(2)
     t2.wait_recv()
     grad[:, JITTER + STEP : JITTER + STEP + STRIP, own_cols] += t2_in[...]
-    t1[0] = send_t1(0)
+    start_t1(0)
     x_step(3)
     far_final = []
     for j in range(2):
         far_out[j].wait_recv()
-        copy = msg.make(back_in.at[j], far_in.at[j], target)
-        copy.start()
-        far_final.append(copy)
+        far_final.append(pass_far(j))
     x_step(4)
+    spread(n, kpad.at[pl.ds(0, 1)], illum, metas, 2)
     x_step(5)
     x_step(6)
 
@@ -483,6 +519,8 @@
         )
         copy.start()
         y_copies.append(copy)
+    for i in range(len(held)):
+        release(i)
     pltpu.make_async_copy(y_in, y_in, ysem).wait()
     tile[...] = acc[x, y] + jnp.sum(y_in[...], 0)
     norm = tile[4]
@@ -540,6 +578,19 @@
         copy.start()
         ky_copies.append(copy)
 
+    pltpu.make_async_copy(kk.at[0, 0, pl.ds(0, 7)], kk.at[0, 0, pl.ds(0, 7)], kysem).wait()
+    kx_copies = []
+    for k in range(1, side):
+        copy = pltpu.make_async_remote_copy(
+            src_ref=kk.at[core, x],
+            dst_ref=kk.at[core, x],
+            send_sem=bsend.at[14 + k - 1],
+            recv_sem=kxsem,
+            device_id={"scan": chip(x + k, y, core)},
+            device_id_type=MESH,
+        )
+        copy.start()
+        kx_copies.append(copy)
     pieces = []
     for j in (3, 1, 2, 0):
         t1[j].wait_recv()
@@ -563,19 +614,6 @@
         pl.when(q != j)(copy.start)
         pieces.append((copy, q != j))
 
-    pltpu.make_async_copy(kk.at[0, 0, pl.ds(0, 7)], kk.at[0, 0, pl.ds(0, 7)], kysem).wait()
-    kx_copies = []
-    for k in range(1, side):
-        copy = pltpu.make_async_remote_copy(
-            src_ref=kk.at[core, x],
-            dst_ref=kk.at[core, x],
-            send_sem=bsend.at[14 + k - 1],
-            recv_sem=kxsem,
-            device_id={"scan": chip(x + k, y, core)},
-            device_id_type=MESH,
-        )
-        copy.start()
-        kx_copies.append(copy)
     piece[0] = grad[:, pl.ds(mult(JITTER + STRIP * q, 8), STRIP), own_cols]
 
     pltpu.make_async_copy(kk.at[0, pl.ds(0, 7)], kk.at[0, pl.ds(0, 7)], kxsem).wait()
@@ -621,8 +659,8 @@
     v1_copies = []
     for k in range(1, 2 * side):
         copy = pltpu.make_async_remote_copy(
-            src_ref=vec,
-            dst_ref=vec1.at[k - 1],
+            src_ref=vec.at[pl.ds(0, 1)],
+            dst_ref=vec1.at[pl.ds(k - 1, 1)],
             send_sem=bsend.at[27 + k - 1],
             recv_sem=v1sem,
             device_id={"scan": chip(x, y + k // 2, (core + k) % 2)},
@@ -630,15 +668,15 @@
         )
         copy.start()
         v1_copies.append(copy)
-    pltpu.make_async_copy(vec1, vec1, v1sem).wait()
+    pltpu.make_async_copy(vec1.at[pl.ds(0, 15)], vec1.at[pl.ds(0, 15)], v1sem).wait()
     for copy in v1_copies:
         copy.wait_send()
-    vec[...] = own_sums + jnp.sum(vec1[...], 0)
+    vec[...] = own_sums + jnp.sum(vec1[0:15, :], 0, keepdims=True)
     v2_copies = []
     for k in range(1, side):
         copy = pltpu.make_async_remote_copy(
-            src_ref=vec,
-            dst_ref=vec2.at[k - 1],
+            src_ref=vec.at[pl.ds(0, 1)],
+            dst_ref=vec2.at[pl.ds(k - 1, 1)],
             send_sem=bsend.at[42 + k - 1],
             recv_sem=v2sem,
             device_id={"scan": chip(x + k, y, core)},
@@ -650,8 +688,8 @@
         source = chip((x % 2) * 4 + core * 2 + at_lane, y, x // 4)
         arrived = pltpu.make_async_copy(dp_in.at[at_lane], dp_in.at[at_lane], dpsem.at[at_lane])
         pl.when(source != me)(arrived.wait)
-    pltpu.make_async_copy(vec2, vec2, v2sem).wait()
-    totals = vec[...] + jnp.sum(vec2[...], 0)
+    pltpu.make_async_copy(vec2.at[pl.ds(0, 7)], vec2.at[pl.ds(0, 7)], v2sem).wait()
+    totals = vec[...] + jnp.sum(vec2[0:7, :], 0, keepdims=True)
     uu, uv, vv, uc, vc = (totals[0:1, i : i + 1] for i in range(5))
     a = 1.1 * uu + 1e-06
     d = 1.1 * vv + 1e-06
@@ -717,6 +755,8 @@
             f32(7, 4, 5, 8, LANES),
             f32(7, 4, 5, 8, LANES),
             f32(7, 5, 8, LANES),
+            f32(4, 2, STRIP, OWN),
+            f32(2, 2, STRIP, OWN),
             f32(5, 8, LANES),
             f32(2, 2, 8, LANES),
             f32(2, 2, 8, LANES),
@@ -728,8 +768,8 @@
             f32(2, STRIP, columns),
             f32(2, STRIP, columns),
             f32(8, LANES),
-            f32(15, 8, LANES),
-            f32(7, 8, LANES),
+            f32(16, LANES),
+            f32(8, LANES),
             dma((48,)),
             dma((48,)),
             dma,
@@ -749,6 +789,7 @@
             dma,
             dma,
             dma,
+            dma((6,)),
         ],
         compiler_params=pltpu.CompilerParams(collective_id=0, has_side_effects=True),
         name="step",

time: 151 us -> 144 us (0.954)
  Pallas kernels: 145 us -> 138 us
    pallas_call x1, Pallas kernels: 145 us -> 138 us  [step(): pl.pallas_call(functools.partial(step_kernel, n), out_shape=(jax.ShapeDty...]
where the time goes in v4:
time: 144 us
  Pallas kernels  138 us (96%)
  local copies, waits for them, and re-layouts  4.51 us (3%)
    pallas_call x1, Pallas kernels, step(): pl.pallas_call(functools.partial(step_kernel, n), out_shape=(jax.ShapeDty...  138 us
    unnamed x5, local copies, waits for them, and re-layouts  3.82 us

profile of v4, /device:TPU:513, one launch (start us, length us, event | category | flops | bytes accessed | tf_op | source)
XLA Modules:
  0.0 144.2 jit_solution(11495947289555258170)
XLA Ops:
  1.3 0.8 copy.12.offsets
  2.0 0.0 copy-start
  2.0 0.1 reshape.11
  2.1 0.1 pad_add_fusion
  2.2 0.6 broadcast_in_dim.2.meta
  2.8 0.0 copy-done
  2.8 138.4 %step.1 = (f32[2,24,1792]{2,1,0:T(8,128)}, f32[2,8,256]{2,1,0:T(8,128)}) custom-call(s32[4,2]{1,0:T(4,128)} %copy-done, s32[1]{0:T(128)S(6)} %copy.15.live, s32[8,128]{1,0:T(8,128)} %broadcast_in_dim.2.meta, f32[2,24,1792]{2,1,0:T(8,128)} %obj.1, f32[2,4,256,256]{3,2,1,0:T(8,128)} %bitcast.1, f32[4,256,256]{2,1,0:T(8,128)} %amps_hbm.1, ...), custom_call_target="tpu_custom_call" | custom-call | tf_op jit(solution)/shard_map/step/pallas_call | solution.py:722
  141.2 1.7 %copy.16 = f32[2,24,1792]{2,1,0:T(8,128)} copy(f32[2,24,1792]{2,1,0:T(8,128)} %get-tuple-element.4) | data formatting | bytes 688128
  142.9 1.3 copy.17
  (1 shorter events, 0.0 us)
Async XLA Ops:
  2.0 0.8 copy-start

commit v5 on v4

--- a/solution.py
+++ b/solution.py
@@ -115,7 +115,8 @@
 
 def step_kernel(
     n, offsets, live, meta, obj, probe_hbm, amps_hbm, cos, sin, new_obj, new_probe,
-    metas_in, metas, probe, amps, win, relay_in, grad, patch, wave, half_done, far, sums9, ta, tb,
+    metas_in, metas, probe, amps, win, relay_in, grad, patch, share, bright, sums9, ta, tb,
+    w0, w1, w2, w3, h0, h1, h2, h3, f0, f1, f2, f3,
     q_in, sib_in, t2_in, t1_in, t8_in, back_in, far_in, piece, q_sib, acc, minus_in, plus_in, y_in, hold_t1, hold_far,
     tile, dp, dp_in, kmine, ksib, kk, kpad, illum, place, dobj, vec, vec1, vec2,
     send, recv, ysem, kysem, kxsem, v1sem, v2sem, bsend, dpsem, psem, lsem,
@@ -280,84 +281,81 @@
             pl.when(when)(copy.wait_send)
     clear_outside(win)
 
+    wave, half_done, far = (w0, w1, w2, w3), (h0, h1, h2, h3), (f0, f1, f2, f3)
     chunk = 32
     chunks = PATCH // chunk
     slab = chunk + 2 * JITTER
-
-    def transform(left, right):
-        for m in range(MODES):
-            cols = slice(m * PATCH, (m + 1) * PATCH)
-            z = jnp.dot(left[...], wave[:, cols], preferred_element_type=F32)
-            half_done[cols, 0:PATCH] = z[0:PATCH].astype(BF16)
-            half_done[cols, PATCH : 2 * PATCH] = z[PATCH : 2 * PATCH].astype(BF16)
-        for m in range(MODES):
-            cols = slice(m * PATCH, (m + 1) * PATCH)
-            far[m] = jnp.dot(half_done[cols, :], right[...], preferred_element_type=F32)
 
     def visit(p, carry):
         ahead = jnp.clip(offsets[p, 0] - (STEP * row - JITTER), 0, 2 * JITTER)
         base = mult((STEP * p + 40) // LANES * LANES, LANES)
         shift = jnp.clip(offsets[p, 1] - STEP * SPLIT * q - base, 0, LANES)
         weight = jnp.where(p < live[0], 1.0, 0.0).astype(F32)
-
-        def exits(i, carry):
-            at = pl.ds(mult(i * chunk, chunk), chunk)
-            low = pl.ds(mult(PATCH + i * chunk, chunk), chunk)
-            o = []
+        steps = [slice(i * chunk, (i + 1) * chunk) for i in range(chunks)]
+        lows = [slice(PATCH + i * chunk, PATCH + (i + 1) * chunk) for i in range(chunks)]
+        left_half, right_half = slice(0, PATCH), slice(PATCH, 2 * PATCH)
+
+        def across(table, m):
+            z = jnp.dot(table[...], wave[m][...], preferred_element_type=F32)
+            half_done[m][:, left_half] = z[left_half].astype(BF16)
+            half_done[m][:, right_half] = z[right_half].astype(BF16)
+
+        def along(table, m):
+            far[m][...] = jnp.dot(half_done[m][...], table[...], preferred_element_type=F32)
+
+        for i, at in enumerate(steps):
             for part in range(2):
-                v = win[part, pl.ds(mult(i * chunk, chunk), slab), pl.ds(base, KCOLS)]
+                v = win[part, i * chunk : i * chunk + slab, pl.ds(base, KCOLS)]
                 v = pltpu.roll(v, (slab - ahead) % slab, 0)[0:chunk]
-                v = pltpu.roll(v, KCOLS - shift, 1)[:, 0:PATCH]
-                patch[part, at, :] = v
-                o.append(v)
-            for m in range(MODES):
+                patch[part, at, :] = pltpu.roll(v, KCOLS - shift, 1)[:, 0:PATCH]
+        for m in range(MODES):
+            for at, low in zip(steps, lows):
                 pr, pi = probe[0, m, at, :], probe[1, m, at, :]
-                wave[at, m * PATCH : (m + 1) * PATCH] = (pr * o[0] - pi * o[1]).astype(BF16)
-                wave[low, m * PATCH : (m + 1) * PATCH] = (pr * o[1] + pi * o[0]).astype(BF16)
-            return carry
-
-        lax.fori_loop(0, chunks, exits, 0)
-        transform(ta, tb)
-
-        def changes(i, carry):
-            at = pl.ds(mult(i * chunk, chunk), chunk)
-            low = pl.ds(mult(PATCH + i * chunk, chunk), chunk)
-            bright = jnp.zeros((chunk, PATCH), F32)
-            for m in range(MODES):
-                fr, fi = far[m, at, 0:PATCH], far[m, at, PATCH : 2 * PATCH]
-                bright = bright + (fr * fr + fi * fi)
-            factor = (amps[p, at, :] / jnp.maximum(jnp.sqrt(bright), 0.5) - 1.0) * weight
-            for m in range(MODES):
-                fr, fi = far[m, at, 0:PATCH], far[m, at, PATCH : 2 * PATCH]
-                wave[at, m * PATCH : (m + 1) * PATCH] = (fr * factor).astype(BF16)
-                wave[low, m * PATCH : (m + 1) * PATCH] = (fi * factor).astype(BF16)
-            return carry
-
-        lax.fori_loop(0, chunks, changes, 0)
-        transform(tb, ta)
-
-        def grads(i, carry):
-            at = pl.ds(mult(i * chunk, chunk), chunk)
-            o_re, o_im = patch[0, at, :], patch[1, at, :]
-            g_re = jnp.zeros((chunk, PATCH), F32)
-            g_im = jnp.zeros((chunk, PATCH), F32)
-            for m in range(MODES):
+                o_re, o_im = patch[0, at, :], patch[1, at, :]
+                wave[m][at, :] = (pr * o_re - pi * o_im).astype(BF16)
+                wave[m][low, :] = (pr * o_im + pi * o_re).astype(BF16)
+            across(ta, m)
+        for m in range(MODES):
+            along(tb, m)
+            for at in steps:
+                fr, fi = far[m][at, left_half], far[m][at, right_half]
+                power = fr * fr + fi * fi
+                bright[at, :] = power if m == 0 else bright[at, :] + power
+        for m in range(MODES):
+            for at, low in zip(steps, lows):
+                if m == 0:
+                    root = jnp.maximum(jnp.sqrt(bright[at, :]), 0.5)
+                    factor = (amps[p, at, :] / root - 1.0) * weight
+                    bright[at, :] = factor
+                else:
+                    factor = bright[at, :]
+                wave[m][at, :] = (far[m][at, left_half] * factor).astype(BF16)
+                wave[m][low, :] = (far[m][at, right_half] * factor).astype(BF16)
+            across(tb, m)
+        for m in range(MODES):
+            along(ta, m)
+            for at in steps:
                 pr, pi = probe[0, m, at, :], probe[1, m, at, :]
-                cr, ci = far[m, at, 0:PATCH], far[m, at, PATCH : 2 * PATCH]
-                g_re = g_re + (pr * cr + pi * ci)
-                g_im = g_im + (pr * ci - pi * cr)
+                o_re, o_im = patch[0, at, :], patch[1, at, :]
+                cr, ci = far[m][at, left_half], far[m][at, right_half]
+                g_re = pr * cr + pi * ci
+                g_im = pr * ci - pi * cr
+                if m > 0:
+                    g_re = g_re + share[0, at, :]
+                    g_im = g_im + share[1, at, :]
+                share[0, at, :] = g_re
+                share[1, at, :] = g_im
                 sums9[m, at, :] += o_re * cr + o_im * ci
                 sums9[MODES + m, at, :] += o_re * ci - o_im * cr
+        blank = jnp.zeros((chunk, KCOLS - PATCH), F32)
+        below = jnp.zeros((2 * JITTER, KCOLS), F32)
+        for i, at in enumerate(steps):
+            o_re, o_im = patch[0, at, :], patch[1, at, :]
             sums9[2 * MODES, at, :] += (o_re * o_re + o_im * o_im) * weight
-            blank = jnp.zeros((chunk, KCOLS - PATCH), F32)
-            below = jnp.zeros((2 * JITTER, KCOLS), F32)
-            for part, g in enumerate((g_re, g_im)):
-                v = pltpu.roll(jnp.concatenate([g, blank], 1), shift, 1)
+            for part in range(2):
+                v = pltpu.roll(jnp.concatenate([share[part, at, :], blank], 1), shift, 1)
                 v = pltpu.roll(jnp.concatenate([v, below], 0), ahead, 0)
-                grad[part, pl.ds(mult(i * chunk, chunk), slab), pl.ds(base, KCOLS)] += v
-            return carry
-
-        lax.fori_loop(0, chunks, grads, 0)
+                grad[part, i * chunk : i * chunk + slab, pl.ds(base, KCOLS)] += v
         return carry
 
     lax.fori_loop(0, SPLIT, visit, 0)
@@ -626,11 +624,11 @@
         source = (q - k + SPLIT) % SPLIT
         at = pl.ds(mult(768 * (source // 2) + OWN * (source % 2), LANES), OWN)
         dobj[:, :, at] += piece[k]
-    bright = illum[0]
+    lit = illum[0]
     g_re, g_im = dobj[0], dobj[1]
     o_re, o_im = obj[0], obj[1]
-    d_re, d_im = g_re / (bright + 1.0), g_im / (bright + 1.0)
-    s_uu = jnp.sum((d_re * d_re + d_im * d_im) * bright)
+    d_re, d_im = g_re / (lit + 1.0), g_im / (lit + 1.0)
+    s_uu = jnp.sum((d_re * d_re + d_im * d_im) * lit)
     s_uc = jnp.sum(d_re * g_re + d_im * g_im)
     dobj[0] = d_re
     dobj[1] = d_im
@@ -736,12 +734,14 @@
             f32(2, 2, STRIP, OWN),
             f32(2, ROWS + 16, WIN),
             f32(2, PATCH, PATCH),
-            pltpu.VMEM((2 * PATCH, MODES * PATCH), BF16),
-            pltpu.VMEM((MODES * PATCH, 2 * PATCH), BF16),
-            f32(MODES, PATCH, 2 * PATCH),
+            f32(2, PATCH, PATCH),
+            f32(PATCH, PATCH),
             f32(2 * MODES + 1, PATCH, PATCH),
             pltpu.VMEM((2 * PATCH, 2 * PATCH), BF16),
             pltpu.VMEM((2 * PATCH, 2 * PATCH), BF16),
+            *[pltpu.VMEM((2 * PATCH, PATCH), BF16) for m in range(MODES)],
+            *[pltpu.VMEM((PATCH, 2 * PATCH), BF16) for m in range(MODES)],
+            *[f32(PATCH, 2 * PATCH) for m in range(MODES)],
             f32(2, 8, 8, 5, 8, LANES),
             f32(2, ROWS, LANES),
             f32(2, STRIP, OWN),

time: 144 us -> 136 us (0.944)
  Pallas kernels: 138 us -> 130 us
    pallas_call x1, Pallas kernels: 138 us -> 130 us  [step(): pl.pallas_call(functools.partial(step_kernel, n), out_shape=(jax.ShapeDty...]
where the time goes in v5:
time: 136 us
  Pallas kernels  130 us (96%)
  local copies, waits for them, and re-layouts  4.51 us (3%)
    pallas_call x1, Pallas kernels, step(): pl.pallas_call(functools.partial(step_kernel, n), out_shape=(jax.ShapeDty...  130 us
    unnamed x5, local copies, waits for them, and re-layouts  3.82 us

profile of v5, /device:TPU:513, one launch (start us, length us, event | category | flops | bytes accessed | tf_op | source)
XLA Modules:
  0.0 136.2 jit_solution(14266401634461870162)
XLA Ops:
  1.3 0.8 copy.12.offsets
  2.0 0.0 copy-start
  2.0 0.1 reshape.11
  2.1 0.1 pad_add_fusion
  2.2 0.6 broadcast_in_dim.2.meta
  2.8 0.0 copy-done
  2.8 130.3 %step.1 = (f32[2,24,1792]{2,1,0:T(8,128)}, f32[2,8,256]{2,1,0:T(8,128)}) custom-call(s32[4,2]{1,0:T(4,128)} %copy-done, s32[1]{0:T(128)S(6)} %copy.15.live, s32[8,128]{1,0:T(8,128)} %broadcast_in_dim.2.meta, f32[2,24,1792]{2,1,0:T(8,128)} %obj.1, f32[2,4,256,256]{3,2,1,0:T(8,128)} %bitcast.1, f32[4,256,256]{2,1,0:T(8,128)} %amps_hbm.1, ...), custom_call_target="tpu_custom_call" | custom-call | tf_op jit(solution)/shard_map/step/pallas_call | solution.py:720
  133.1 1.7 %copy.16 = f32[2,24,1792]{2,1,0:T(8,128)} copy(f32[2,24,1792]{2,1,0:T(8,128)} %get-tuple-element.4) | data formatting | bytes 688128
  134.8 1.3 copy.17
  (1 shorter events, 0.0 us)
Async XLA Ops:
  2.0 0.8 copy-start

commit v6 on v5

--- a/solution.py
+++ b/solution.py
@@ -114,8 +114,8 @@
 
 
 def step_kernel(
-    n, offsets, live, meta, obj, probe_hbm, amps_hbm, cos, sin, new_obj, new_probe,
-    metas_in, metas, probe, amps, win, relay_in, grad, patch, share, bright, sums9, ta, tb,
+    n, offsets, live, obj, probe_hbm, amps_hbm, cos, sin, obj_step, probe_out, rates,
+    meta, metas_in, metas, probe, amps, win, relay_in, grad, patch, share, bright, sums9, ta, tb,
     w0, w1, w2, w3, h0, h1, h2, h3, f0, f1, f2, f3,
     q_in, sib_in, t2_in, t1_in, t8_in, back_in, far_in, piece, q_sib, acc, minus_in, plus_in, y_in, hold_t1, hold_far,
     tile, dp, dp_in, kmine, ksib, kk, kpad, illum, place, dobj, vec, vec1, vec2,
@@ -144,6 +144,12 @@
     def rows(start, size):
         return pl.ds(mult(start, 8), size)
 
+    lanes = lax.broadcasted_iota(jnp.int32, (8, LANES), 1)
+    facts = jnp.where(lanes == 2 * SPLIT, live[0], 0)
+    for p in range(SPLIT):
+        for i in range(2):
+            facts = jnp.where(lanes == 2 * p + i, offsets[i, p], facts)
+    meta[...] = facts
     load_probe = pltpu.make_async_copy(probe_hbm, probe, lsem.at[0])
     load_probe.start()
     load_amps = pltpu.make_async_copy(amps_hbm, amps, lsem.at[1])
@@ -197,7 +203,7 @@
     own_cols = pl.ds(own_at, OWN)
     sib_cols = pl.ds(mult(OWN * (1 - core), LANES), LANES)
     win[:, rows(JITTER + STRIP * q, STRIP), own_cols] = obj[:, :, columns(q)]
-    metas_in[2 * SPLIT + q] = meta[...]
+    metas_in[2 * SPLIT + q] = facts
 
     c, s = cos[...], sin[...]
     ta[0:256, 0:256] = c
@@ -287,9 +293,9 @@
     slab = chunk + 2 * JITTER
 
     def visit(p, carry):
-        ahead = jnp.clip(offsets[p, 0] - (STEP * row - JITTER), 0, 2 * JITTER)
+        ahead = jnp.clip(offsets[0, p] - (STEP * row - JITTER), 0, 2 * JITTER)
         base = mult((STEP * p + 40) // LANES * LANES, LANES)
-        shift = jnp.clip(offsets[p, 1] - STEP * SPLIT * q - base, 0, LANES)
+        shift = jnp.clip(offsets[1, p] - STEP * SPLIT * q - base, 0, LANES)
         weight = jnp.where(p < live[0], 1.0, 0.0).astype(F32)
         steps = [slice(i * chunk, (i + 1) * chunk) for i in range(chunks)]
         lows = [slice(PATCH + i * chunk, PATCH + (i + 1) * chunk) for i in range(chunks)]
@@ -494,7 +500,6 @@
     x_step(2)
     t2.wait_recv()
     grad[:, JITTER + STEP : JITTER + STEP + STRIP, own_cols] += t2_in[...]
-    start_t1(0)
     x_step(3)
     far_final = []
     for j in range(2):
@@ -517,7 +522,8 @@
         )
         copy.start()
         y_copies.append(copy)
-    for i in range(len(held)):
+    start_t1(0)
+    for i in range(3):
         release(i)
     pltpu.make_async_copy(y_in, y_in, ysem).wait()
     tile[...] = acc[x, y] + jnp.sum(y_in[...], 0)
@@ -576,6 +582,8 @@
         copy.start()
         ky_copies.append(copy)
 
+    for i in range(3, 6):
+        release(i)
     pltpu.make_async_copy(kk.at[0, 0, pl.ds(0, 7)], kk.at[0, 0, pl.ds(0, 7)], kysem).wait()
     kx_copies = []
     for k in range(1, side):
@@ -694,11 +702,14 @@
     det = a * d - uv * uv
     rate_obj = (uc * d - uv * vc) / det
     rate_probe = (a * vc - uv * uc) / det
+    at = lax.broadcasted_iota(jnp.int32, (8, LANES), 1)
+    rates[...] = jnp.where(at == 0, rate_obj, rate_probe)
+    obj_step[...] = dobj[...]
     for part in range(2):
-        new_obj[part] = obj[part] + rate_obj * dobj[part]
         for at_lane in range(2):
             cols = slice(LANES * at_lane, LANES * at_lane + LANES)
-            new_probe[part, :, cols] = probe[part, out_mode, pl.ds(mult(8 * out_band, 8), 8), cols] + rate_probe * dp_in[at_lane, part]
+            probe_out[0, part, :, cols] = dp_in[at_lane, part]
+            probe_out[1, part, :, cols] = probe[part, out_mode, pl.ds(mult(8 * out_band, 8), 8), cols]
 
     msg.drain()
     for copy in y_copies + ky_copies + kx_copies + v2_copies:
@@ -707,7 +718,28 @@
         pl.when(when)(copy.wait_send)
 
 
-def step(n, offsets, live, meta, obj, probe, amps, cos, sin):
+def finish_kernel(obj, obj_step, probe_out, rates, new_obj, new_probe):
+    rate_obj, rate_probe = rates[0:1, 0:1], rates[0:1, 1:2]
+    for part in range(2):
+        new_obj[part] = obj[part] + rate_obj * obj_step[part]
+        new_probe[part] = probe_out[1, part] + rate_probe * probe_out[0, part]
+
+
+def finish(obj, obj_step, probe_out, rates):
+    vmem = pl.BlockSpec(memory_space=pltpu.VMEM)
+    return pl.pallas_call(
+        finish_kernel,
+        out_shape=(
+            jax.ShapeDtypeStruct(obj.shape, F32),
+            jax.ShapeDtypeStruct(probe_out.shape[1:], F32),
+        ),
+        in_specs=[vmem] * 4,
+        out_specs=[vmem] * 2,
+        name="finish",
+    )(obj, obj_step, probe_out, rates)
+
+
+def step(n, offsets, live, obj, probe, amps, cos, sin):
     vmem = pl.BlockSpec(memory_space=pltpu.VMEM)
     smem = pl.BlockSpec(memory_space=pltpu.SMEM)
     hbm = pl.BlockSpec(memory_space=pl.ANY)
@@ -721,11 +753,13 @@
         functools.partial(step_kernel, n),
         out_shape=(
             jax.ShapeDtypeStruct((2, STRIP, columns), F32),
-            jax.ShapeDtypeStruct((2, 8, PATCH), F32),
+            jax.ShapeDtypeStruct((2, 2, 8, PATCH), F32),
+            jax.ShapeDtypeStruct((8, LANES), F32),
         ),
-        in_specs=[smem, smem, vmem, vmem, hbm, hbm, vmem, vmem],
-        out_specs=[vmem] * 2,
+        in_specs=[smem, smem, vmem, hbm, hbm, vmem, vmem],
+        out_specs=[vmem] * 3,
         scratch_shapes=[
+            pltpu.VMEM((8, LANES), jnp.int32),
             pltpu.VMEM((4 * SPLIT, 8, LANES), jnp.int32),
             pltpu.SMEM((4 * SPLIT, 8, LANES), jnp.int32),
             f32(2, MODES, PATCH, PATCH),
@@ -793,7 +827,7 @@
         ],
         compiler_params=pltpu.CompilerParams(collective_id=0, has_side_effects=True),
         name="step",
-    )(offsets, live, meta, obj, probe, amps, cos, sin)
+    )(offsets, live, obj, probe, amps, cos, sin)
 
 
 def tables(length):
@@ -806,10 +840,9 @@
 
 def on_device(n, object_field, probe_field, amplitudes, offsets, live_counts):
     probe = probe_field.reshape(2, MODES, PATCH, PATCH)
-    meta = jnp.concatenate([offsets.reshape(-1), live_counts])
-    meta = jnp.broadcast_to(jnp.pad(meta, (0, LANES - meta.shape[0]))[None], (8, LANES))
     cos, sin = tables(PATCH)
-    return step(n, offsets, live_counts, meta, object_field, probe, amplitudes, cos, sin)
+    updates = step(n, offsets.T, live_counts, object_field, probe, amplitudes, cos, sin)
+    return finish(object_field, *updates)
 
 
 def solution(mesh):

time: 136 us -> 131 us (0.963)
  local copies, waits for them, and re-layouts: 4.51 us -> 0 us
    unnamed x5 -> x0, local copies, waits for them, and re-layouts: 3.82 us -> none
    pallas_call x1, Pallas kernels: 130 us -> 128 us  [step(): pl.pallas_call(functools.partial(step_kernel, n), out_shape=(jax.ShapeDty...]
    pallas_call x0 -> x1, Pallas kernels: none -> 1.89 us  [finish(): pl.pallas_call(finish_kernel, out_shape=(jax.ShapeDtypeStruct(obj.shape,...]
where the time goes in v6:
time: 131 us
  Pallas kernels  129 us (98%)
    pallas_call x1, Pallas kernels, step(): pl.pallas_call(functools.partial(step_kernel, n), out_shape=(jax.ShapeDty...  128 us

profile of v6, /device:TPU:513, one launch (start us, length us, event | category | flops | bytes accessed | tf_op | source)
XLA Modules:
  0.0 130.7 jit_solution(17690163983248971459)
XLA Ops:
  1.3 127.5 %step.1 = (f32[2,24,1792]{2,1,0:T(8,128)}, f32[2,2,8,256]{3,2,1,0:T(8,128)}, f32[8,128]{1,0:T(8,128)}) custom-call(s32[2,4]{1,0:T(2,128)} %bitcast.3, s32[1]{0:T(128)S(6)} %copy.9.live, f32[2,24,1792]{2,1,0:T(8,128)} %obj.3, f32[2,4,256,256]{3,2,1,0:T(8,128)} %bitcast.2, f32[4,256,256]{2,1,0:T(8,128)} %amps_hbm.1, bf16[256,256]{1,0:T(8,128)(2,1)} %constant.10.cos, ...), custom_call_target="tpu_custom_call" | custom-call | tf_op jit(solution)/shard_map/step/pallas_call | solution.py:752
  128.8 1.9 %finish.1 = (f32[2,24,1792]{2,1,0:T(8,128)}, f32[2,8,256]{2,1,0:T(8,128)}) custom-call(f32[2,24,1792]{2,1,0:T(8,128)} %obj.3, f32[2,24,1792]{2,1,0:T(8,128)} %get-tuple-element.5.obj_step, f32[2,2,8,256]{3,2,1,0:T(8,128)} %get-tuple-element.6.probe_out, f32[8,128]{1,0:T(8,128)} %get-tuple-element.7.rates), custom_call_target="tpu_custom_call" | custom-call | tf_op jit(solution)/shard_map/finish/pallas_call | solution.py:730

commit v7 on v6

--- a/solution.py
+++ b/solution.py
@@ -158,6 +158,21 @@
     peers += [chip(x + k, y, cc) for k in range(1, side) for cc in range(2)]
     peers += [chip(x, y + k, cc) for k in range(1, side) for cc in range(2)]
     peers += [sibling]
+    def clear_outside(ref):
+        @pl.when(row == 0)
+        def _():
+            ref[:, 0:JITTER, :] = jnp.zeros((2, JITTER, WIN), F32)
+
+        @pl.when(row == rows_all - 1)
+        def _():
+            ref[:, JITTER + STEP : JITTER + 2 * STEP, :] = jnp.zeros((2, STEP, WIN), F32)
+
+        @pl.when(row >= rows_all - 2)
+        def _():
+            ref[:, JITTER + 2 * STEP : ROWS, :] = jnp.zeros((2, 72, WIN), F32)
+
+    clear_outside(win)
+    metas_in[...] = jnp.zeros_like(metas_in)
     greet(peers)
 
     sends = []
@@ -184,21 +199,27 @@
         for k in range(SPLIT):
             if e or k:
                 there = (first + SPLIT * e + (q + k) % SPLIT + n) % n
-                put(meta, metas_in.at[(2 - e) * SPLIT + q], mrecv, there)
+                to = row + e
+                known = jnp.logical_and(to >= 0, to < rows_all)
+                slot = (2 - e) * SPLIT + q
+                put(meta, metas_in.at[slot], mrecv.at[slot], there, when=known)
     relay, origin, target, source = long_way(me, -1)
-    middle = jnp.logical_or(q == 1, q == 2)
+    above1, above2 = row >= 1, row >= 2
+    below1, below2 = row <= rows_all - 2, row <= rows_all - 3
+    middle = jnp.logical_and(jnp.logical_or(q == 1, q == 2), above2)
+    passing = origin // SPLIT >= 2
     middle_at = jnp.clip(q - 1, 0, 1)
     around = [(q + k) % SPLIT for k in range(SPLIT)]
     for there in around:
         block = obj.at[:, :, columns(there)]
         put(block, relay_in.at[middle_at], relaysem.at[middle_at], relay - q + there, when=middle)
-        put(block, landing(there, JITTER + STEP + STRIP * q), aheadsem.at[q], (first - SPLIT + there + n) % n)
+        put(block, landing(there, JITTER + STEP + STRIP * q), aheadsem.at[q], (first - SPLIT + there + n) % n, when=above1)
     for there in around[1:]:
         block = obj.at[:, :, columns(there)]
         put(block, landing(there, JITTER + STRIP * q), ownsem.at[q], first + there)
     for there in around:
         block = obj.at[:, pl.ds(STRIP - JITTER, JITTER), columns(there)]
-        put(block, landing(there, 0, JITTER), tailsem, (first + SPLIT + there) % n, when=q == SPLIT - 1)
+        put(block, landing(there, 0, JITTER), tailsem, (first + SPLIT + there) % n, when=jnp.logical_and(q == SPLIT - 1, below1))
     own_at = mult(LANES * core, LANES)
     own_cols = pl.ds(own_at, OWN)
     sib_cols = pl.ds(mult(OWN * (1 - core), LANES), LANES)
@@ -239,45 +260,39 @@
         return copy
 
     def far_on(j):
-        arrived(relay_in.at[j - 1], relaysem.at[j - 1]).wait()
-        put(relay_in.at[j - 1], landing(q, JITTER + 2 * STEP + STRIP * j), finalsem.at[j], target)
+        pl.when(passing)(arrived(relay_in.at[j - 1], relaysem.at[j - 1]).wait)
+        put(relay_in.at[j - 1], landing(q, JITTER + 2 * STEP + STRIP * j), finalsem.at[j], target, when=passing)
 
     for j in range(SPLIT):
         pl.when(q != j)(arrived(landing(q, JITTER + STRIP * j), ownsem.at[j]).wait)
         if j == 0:
-            arrived(landing(q, JITTER + STEP), aheadsem.at[0]).wait()
-            put(landing(q, JITTER + STEP), landing(q, JITTER + 2 * STEP), finalsem.at[0], up)
+            pl.when(below1)(arrived(landing(q, JITTER + STEP), aheadsem.at[0]).wait)
+            onward = jnp.logical_and(above1, below1)
+            put(landing(q, JITTER + STEP), landing(q, JITTER + 2 * STEP), finalsem.at[0], up, when=onward)
             far_on(1)
         if j == 1:
             far_on(2)
     borders = [border(JITTER, STEP)]
-    arrived(landing(q, 0, JITTER), tailsem).wait()
+    pl.when(above1)(arrived(landing(q, 0, JITTER), tailsem).wait)
     borders.append(border(0, JITTER))
     for j in range(1, SPLIT):
-        arrived(landing(q, JITTER + STEP + STRIP * j), aheadsem.at[j]).wait()
+        pl.when(below1)(arrived(landing(q, JITTER + STEP + STRIP * j), aheadsem.at[j]).wait)
     borders.append(border(JITTER + STEP, STEP))
     for j in range(3):
-        arrived(landing(q, JITTER + 2 * STEP + STRIP * j), finalsem.at[j]).wait()
+        pl.when(below2)(arrived(landing(q, JITTER + 2 * STEP + STRIP * j), finalsem.at[j]).wait)
     borders.append(border(JITTER + 2 * STEP, 72))
-    arrived(metas_in.at[pl.ds(0, 15)], mrecv).wait()
+    for line in range(4):
+        there = row - 2 + line
+        known = jnp.logical_and(there >= 0, there < rows_all)
+        for at in range(SPLIT):
+            slot = line * SPLIT + at
+            other = known if line != 2 else q != at
+            pl.when(other)(arrived(metas_in.at[slot], mrecv.at[slot]).wait)
     to_smem = pltpu.make_async_copy(metas_in, metas, msem)
     to_smem.start()
     load_amps.wait()
     for copy in borders:
         copy.wait_recv()
-
-    def clear_outside(ref):
-        @pl.when(row == 0)
-        def _():
-            ref[:, 0:JITTER, :] = jnp.zeros((2, JITTER, WIN), F32)
-
-        @pl.when(row == rows_all - 1)
-        def _():
-            ref[:, JITTER + STEP : JITTER + 2 * STEP, :] = jnp.zeros((2, STEP, WIN), F32)
-
-        @pl.when(row >= rows_all - 2)
-        def _():
-            ref[:, JITTER + 2 * STEP : ROWS, :] = jnp.zeros((2, 72, WIN), F32)
 
     msg.drain()
     for copy, when in sends:
@@ -285,7 +300,6 @@
             copy.wait_send()
         else:
             pl.when(when)(copy.wait_send)
-    clear_outside(win)
 
     wave, half_done, far = (w0, w1, w2, w3), (h0, h1, h2, h3), (f0, f1, f2, f3)
     chunk = 32
@@ -821,7 +835,7 @@
             dma((2,)),
             dma((3,)),
             dma,
-            dma,
+            dma((16,)),
             dma,
             dma((6,)),
         ],

time: 131 us -> 127 us (0.969)
  Pallas kernels: 129 us -> 125 us
    pallas_call x1, Pallas kernels: 128 us -> 123 us  [step(): pl.pallas_call(functools.partial(step_kernel, n), out_shape=(jax.ShapeDty...]
where the time goes in v7:
time: 127 us
  Pallas kernels  125 us (98%)
  between operations  1.29 us (1%)
    pallas_call x1, Pallas kernels, step(): pl.pallas_call(functools.partial(step_kernel, n), out_shape=(jax.ShapeDty...  123 us

profile of v7, /device:TPU:513, one launch (start us, length us, event | category | flops | bytes accessed | tf_op | source)
XLA Modules:
  0.0 126.6 jit_solution(7415131079813252114)
XLA Ops:
  1.3 123.4 %step.1 = (f32[2,24,1792]{2,1,0:T(8,128)}, f32[2,2,8,256]{3,2,1,0:T(8,128)}, f32[8,128]{1,0:T(8,128)}) custom-call(s32[2,4]{1,0:T(2,128)} %bitcast.3, s32[1]{0:T(128)S(6)} %copy.9.live, f32[2,24,1792]{2,1,0:T(8,128)} %obj.3, f32[2,4,256,256]{3,2,1,0:T(8,128)} %bitcast.2, f32[4,256,256]{2,1,0:T(8,128)} %amps_hbm.1, bf16[256,256]{1,0:T(8,128)(2,1)} %constant.10.cos, ...), custom_call_target="tpu_custom_call" | custom-call | tf_op jit(solution)/shard_map/step/pallas_call | solution.py:766
  124.7 1.9 %finish.1 = (f32[2,24,1792]{2,1,0:T(8,128)}, f32[2,8,256]{2,1,0:T(8,128)}) custom-call(f32[2,24,1792]{2,1,0:T(8,128)} %obj.3, f32[2,24,1792]{2,1,0:T(8,128)} %get-tuple-element.5.obj_step, f32[2,2,8,256]{3,2,1,0:T(8,128)} %get-tuple-element.6.probe_out, f32[8,128]{1,0:T(8,128)} %get-tuple-element.7.rates), custom_call_target="tpu_custom_call" | custom-call | tf_op jit(solution)/shard_map/finish/pallas_call | solution.py:744

commit v8 on v7

--- a/solution.py
+++ b/solution.py
@@ -113,12 +113,41 @@
     lax.fori_loop(0, 16, one, 0, unroll=4)
 
 
+def collect(n, strip, out, metas, line):
+    me = lax.axis_index("scan")
+    q = me % SPLIT
+    line = line + jnp.where(q == SPLIT - 1, 1, 0)
+    there = me // SPLIT - 2 + line
+    inside = jnp.logical_and(there >= 0, there < n // SPLIT)
+    start = mult(STRIP * q + STEP * (2 - line) - JITTER + ZTOP, 8)
+    tall = STRIP + 2 * JITTER
+
+    def one(col, carry):
+        slot = line * SPLIT + col // SPLIT
+        place = col % SPLIT
+        top = metas[slot, 0, 2 * place]
+        left = metas[slot, 0, 2 * place + 1]
+        weight = jnp.where(jnp.logical_and(inside, place < metas[slot, 0, 8]), 1.0, 0.0).astype(F32)
+        ahead = jnp.clip(STEP * there - top + JITTER, 0, 2 * JITTER)
+        base = mult((STEP * col + 40) // LANES * LANES, LANES)
+        shift = jnp.clip(left - base, 0, LANES)
+        below = jnp.zeros((2 * JITTER, PATCH), F32)
+        for part in range(2):
+            value = strip[part, :, pl.ds(base, KCOLS)]
+            value = pltpu.roll(value, (KCOLS - shift) % KCOLS, 1)[:, 0:PATCH] * weight
+            value = pltpu.roll(jnp.concatenate([value, below], 0), ahead, 0)
+            out[part, pl.ds(start, tall), :] += value
+        return carry
+
+    lax.fori_loop(0, 16, one, 0, unroll=4)
+
+
 def step_kernel(
     n, offsets, live, obj, probe_hbm, amps_hbm, cos, sin, obj_step, probe_out, rates,
     meta, metas_in, metas, probe, amps, win, relay_in, grad, patch, share, bright, sums9, ta, tb,
     w0, w1, w2, w3, h0, h1, h2, h3, f0, f1, f2, f3,
     q_in, sib_in, t2_in, t1_in, t8_in, back_in, far_in, piece, q_sib, acc, minus_in, plus_in, y_in, hold_t1, hold_far,
-    tile, dp, dp_in, kmine, ksib, kk, kpad, illum, place, dobj, vec, vec1, vec2,
+    tile, dp, dp_in, kmine, ksib, kk, kpad, illum, place, dobj, cross, cross_in, vec, vec1, vec2,
     send, recv, ysem, kysem, kxsem, v1sem, v2sem, bsend, dpsem, psem, lsem,
     gsend, ownsem, aheadsem, relaysem, finalsem, tailsem, mrecv, msem, holdsem,
 ):
@@ -239,7 +268,7 @@
     sums9[...] = jnp.zeros_like(sums9)
     kpad[...] = jnp.zeros_like(kpad)
     illum[...] = jnp.zeros_like(illum)
-    place[...] = jnp.zeros_like(place)
+    cross[...] = jnp.zeros_like(cross)
     dobj[...] = jnp.zeros_like(dobj)
     win[:, ROWS:, :] = jnp.zeros((2, 16, WIN), F32)
     load_probe.wait()
@@ -381,8 +410,6 @@
     lax.fori_loop(0, SPLIT, visit, 0)
     clear_outside(grad)
 
-    to_sib = msg.make(grad.at[:, pl.ds(0, ROWS), sib_cols], sib_in, sibling)
-    to_sib.start()
     for at_band in range(PATCH // 8):
         yy = (at_band // 2) % 8
         for at_lane in range(2):
@@ -398,6 +425,9 @@
         copy = msg.make(q_in.at[1 - core, at], q_sib.at[at], sibling)
         copy.start()
         q_copies.append(copy)
+        if not q_copies[1:]:
+            to_sib = msg.make(grad.at[:, pl.ds(0, ROWS), sib_cols], sib_in, sibling)
+            to_sib.start()
     relay, origin, target, source = long_way(me, 1)
 
     band = (x // 4) * 16 + y * 2 + (x // 2) % 2
@@ -405,10 +435,6 @@
     out_mode = x // 2
     out_band = (x % 2) * 16 + y * 2 + core
     p_tile = probe[:, pl.ds(2 * core, 2), pl.ds(mult(8 * band, 8), 8), pl.ds(mult(LANES * lane, LANES), LANES)]
-
-    to_sib.wait_recv()
-    edge = pl.ds(mult(LANES * core + 384 * (1 - core), LANES), LANES)
-    grad[:, 0:ROWS, edge] += sib_in[...]
 
     def sums(start):
         return grad.at[:, pl.ds(start, STRIP), own_cols]
@@ -438,6 +464,10 @@
     chains[-1, 1] = send_chain(-1, 1)
     add_sibling(2)
     chains[1, 1] = send_chain(1, 1)
+    to_sib.wait_recv()
+    edge = pl.ds(mult(LANES * core + 384 * (1 - core), LANES), LANES)
+    grad[:, 0:ROWS, edge] += sib_in[...]
+
     far_out = []
     for j in (1, 2):
         copy = msg.make(sums(JITTER + 2 * STEP + STRIP * j), back_in.at[j - 1], relay)
@@ -507,10 +537,10 @@
     to_smem.wait()
     x_step(0)
     start_t1(1)
-    spread(n, kpad.at[pl.ds(0, 1)], illum, metas, 0)
+    spread(n, kpad, illum, metas, 0)
     x_step(1)
     start_t1(2)
-    spread(n, kpad.at[pl.ds(0, 1)], illum, metas, 1)
+    spread(n, kpad, illum, metas, 1)
     x_step(2)
     t2.wait_recv()
     grad[:, JITTER + STEP : JITTER + STEP + STRIP, own_cols] += t2_in[...]
@@ -520,7 +550,7 @@
         far_out[j].wait_recv()
         far_final.append(pass_far(j))
     x_step(4)
-    spread(n, kpad.at[pl.ds(0, 1)], illum, metas, 2)
+    spread(n, kpad, illum, metas, 2)
     x_step(5)
     x_step(6)
 
@@ -636,10 +666,6 @@
 
     piece[0] = grad[:, pl.ds(mult(JITTER + STRIP * q, 8), STRIP), own_cols]
 
-    pltpu.make_async_copy(kk.at[0, pl.ds(0, 7)], kk.at[0, pl.ds(0, 7)], kxsem).wait()
-    ks_copy = msg.make(kk.at[core], kk.at[core], sibling)
-    ks_copy.start()
-
     for k in range(SPLIT):
         if k > 0:
             pltpu.make_async_copy(piece.at[k], piece.at[k], psem.at[k]).wait()
@@ -655,21 +681,24 @@
     dobj[0] = d_re
     dobj[1] = d_im
 
-    ks_copy.wait_recv()
+    place[0] = d_re * o_re + d_im * o_im
+    place[1] = d_re * o_im - d_im * o_re
+    for line in range(3):
+        collect(n, place, cross, metas, line)
+    cross_copy = msg.make(cross.at[1 - core, pl.ds(ZTOP, PATCH)], cross_in, sibling)
+    cross_copy.start()
+    pltpu.make_async_copy(kk.at[0, pl.ds(0, 7)], kk.at[0, pl.ds(0, 7)], kxsem).wait()
+    cross_copy.wait_recv()
+    product = jnp.zeros((8, LANES), F32)
     for at_band in range(PATCH // 8):
         for at_lane in range(2):
             xx = (at_band // 16) * 4 + (at_band % 2) * 2 + at_lane
             yy = (at_band // 2) % 8
-            rows = slice(ZTOP + 8 * at_band, ZTOP + 8 * at_band + 8)
+            rows_at = slice(8 * at_band, 8 * at_band + 8)
             cols = slice(LANES * at_lane, LANES * at_lane + LANES)
-            kpad[0, rows, cols] = kk[0, xx, yy]
-            kpad[1, rows, cols] = kk[1, xx, yy]
-    for line in range(3):
-        spread(n, kpad, place, metas, line)
-    d_re, d_im = dobj[0], dobj[1]
-    s_uv = jnp.sum(
-        place[0] * (d_re * o_re + d_im * o_im) - place[1] * (d_re * o_im - d_im * o_re)
-    )
+            both = cross[core, ZTOP + 8 * at_band : ZTOP + 8 * at_band + 8, cols] + cross_in[rows_at, cols]
+            product = product + kk[core, xx, yy] * both
+    s_uv = jnp.sum(product) * jnp.where(core == 0, 1.0, -1.0).astype(F32)
 
     at = lax.broadcasted_iota(jnp.int32, (8, LANES), 1)
     own_sums = jnp.zeros((8, LANES), F32)
@@ -811,10 +840,12 @@
             f32(2, 8, LANES),
             f32(8, LANES),
             f32(2, 8, 8, 8, LANES),
-            f32(2, KROWS, KCOLS),
+            f32(1, KROWS, KCOLS),
             f32(1, STRIP, columns),
             f32(2, STRIP, columns),
             f32(2, STRIP, columns),
+            f32(2, KROWS, PATCH),
+            f32(PATCH, PATCH),
             f32(8, LANES),
             f32(16, LANES),
             f32(8, LANES),

time: 127 us -> 126 us (level)
    pallas_call x1, Pallas kernels: 123 us -> 122 us  [step(): pl.pallas_call(functools.partial(step_kernel, n), out_shape=(jax.ShapeDty...]
where the time goes in v8:
time: 126 us; the launch traced here: 125 us
  Pallas kernels  124 us (98%)
  between operations  1.29 us (1%)
    pallas_call x1, Pallas kernels, step(): pl.pallas_call(functools.partial(step_kernel, n), out_shape=(jax.ShapeDty...  122 us

profile of v8, /device:TPU:513, one launch (start us, length us, event | category | flops | bytes accessed | tf_op | source)
XLA Modules:
  0.0 124.8 jit_solution(3290022930677102925)
XLA Ops:
  1.3 121.7 %step.1 = (f32[2,24,1792]{2,1,0:T(8,128)}, f32[2,2,8,256]{3,2,1,0:T(8,128)}, f32[8,128]{1,0:T(8,128)}) custom-call(s32[2,4]{1,0:T(2,128)} %bitcast.3, s32[1]{0:T(128)S(6)} %copy.9.live, f32[2,24,1792]{2,1,0:T(8,128)} %obj.3, f32[2,4,256,256]{3,2,1,0:T(8,128)} %bitcast.2, f32[4,256,256]{2,1,0:T(8,128)} %amps_hbm.1, bf16[256,256]{1,0:T(8,128)(2,1)} %constant.10.cos, ...), custom_call_target="tpu_custom_call" | custom-call | tf_op jit(solution)/shard_map/step/pallas_call | solution.py:795
  122.9 1.9 %finish.1 = (f32[2,24,1792]{2,1,0:T(8,128)}, f32[2,8,256]{2,1,0:T(8,128)}) custom-call(f32[2,24,1792]{2,1,0:T(8,128)} %obj.3, f32[2,24,1792]{2,1,0:T(8,128)} %get-tuple-element.5.obj_step, f32[2,2,8,256]{3,2,1,0:T(8,128)} %get-tuple-element.6.probe_out, f32[8,128]{1,0:T(8,128)} %get-tuple-element.7.rates), custom_call_target="tpu_custom_call" | custom-call | tf_op jit(solution)/shard_map/finish/pallas_call | solution.py:773

commit v9 on v8

--- a/solution.py
+++ b/solution.py
@@ -570,6 +570,8 @@
     for i in range(3):
         release(i)
     pltpu.make_async_copy(y_in, y_in, ysem).wait()
+    release(3)
+    release(4)
     tile[...] = acc[x, y] + jnp.sum(y_in[...], 0)
     norm = tile[4]
     inverse = norm + 1.0
@@ -626,8 +628,7 @@
         copy.start()
         ky_copies.append(copy)
 
-    for i in range(3, 6):
-        release(i)
+    release(5)
     pltpu.make_async_copy(kk.at[0, 0, pl.ds(0, 7)], kk.at[0, 0, pl.ds(0, 7)], kysem).wait()
     kx_copies = []
     for k in range(1, side):

time: 126 us -> 125 us (level)
  no operation moved by 1% of the time
where the time goes in v9:
time: 125 us
  Pallas kernels  124 us (99%)
  between operations  1.29 us (1%)
    pallas_call x1, Pallas kernels, step(): pl.pallas_call(functools.partial(step_kernel, n), out_shape=(jax.ShapeDty...  122 us

profile of v9, /device:TPU:513, one launch (start us, length us, event | category | flops | bytes accessed | tf_op | source)
XLA Modules:
  0.0 124.8 jit_solution(5938343742721990814)
XLA Ops:
  1.3 121.7 %step.1 = (f32[2,24,1792]{2,1,0:T(8,128)}, f32[2,2,8,256]{3,2,1,0:T(8,128)}, f32[8,128]{1,0:T(8,128)}) custom-call(s32[2,4]{1,0:T(2,128)} %bitcast.3, s32[1]{0:T(128)S(6)} %copy.9.live, f32[2,24,1792]{2,1,0:T(8,128)} %obj.3, f32[2,4,256,256]{3,2,1,0:T(8,128)} %bitcast.2, f32[4,256,256]{2,1,0:T(8,128)} %amps_hbm.1, bf16[256,256]{1,0:T(8,128)(2,1)} %constant.10.cos, ...), custom_call_target="tpu_custom_call" | custom-call | tf_op jit(solution)/shard_map/step/pallas_call | solution.py:796
  122.9 1.9 %finish.1 = (f32[2,24,1792]{2,1,0:T(8,128)}, f32[2,8,256]{2,1,0:T(8,128)}) custom-call(f32[2,24,1792]{2,1,0:T(8,128)} %obj.3, f32[2,24,1792]{2,1,0:T(8,128)} %get-tuple-element.5.obj_step, f32[2,2,8,256]{3,2,1,0:T(8,128)} %get-tuple-element.6.probe_out, f32[8,128]{1,0:T(8,128)} %get-tuple-element.7.rates), custom_call_target="tpu_custom_call" | custom-call | tf_op jit(solution)/shard_map/finish/pallas_call | solution.py:774

commit v10 on v9

--- a/solution.py
+++ b/solution.py
@@ -132,14 +132,18 @@
         base = mult((STEP * col + 40) // LANES * LANES, LANES)
         shift = jnp.clip(left - base, 0, LANES)
         below = jnp.zeros((2 * JITTER, PATCH), F32)
+        summed = []
         for part in range(2):
             value = strip[part, :, pl.ds(base, KCOLS)]
             value = pltpu.roll(value, (KCOLS - shift) % KCOLS, 1)[:, 0:PATCH] * weight
             value = pltpu.roll(jnp.concatenate([value, below], 0), ahead, 0)
-            out[part, pl.ds(start, tall), :] += value
-        return carry
-
-    lax.fori_loop(0, 16, one, 0, unroll=4)
+            summed.append(carry[part] + value)
+        return tuple(summed)
+
+    blank = jnp.zeros((tall, PATCH), F32)
+    total = lax.fori_loop(0, 16, one, (blank, blank), unroll=4)
+    for part in range(2):
+        out[part, pl.ds(start, tall), :] += total[part]
 
 
 def step_kernel(

time: 125 us -> 125 us (level)
  no operation moved by 1% of the time
where the time goes in v10:
time: 125 us
  Pallas kernels  124 us (99%)
  between operations  1.29 us (1%)
    pallas_call x1, Pallas kernels, step(): pl.pallas_call(functools.partial(step_kernel, n), out_shape=(jax.ShapeDty...  122 us

profile of v10, /device:TPU:513, one launch (start us, length us, event | category | flops | bytes accessed | tf_op | source)
XLA Modules:
  0.0 124.9 jit_solution(11003441262034210253)
XLA Ops:
  1.3 121.7 %step.1 = (f32[2,24,1792]{2,1,0:T(8,128)}, f32[2,2,8,256]{3,2,1,0:T(8,128)}, f32[8,128]{1,0:T(8,128)}) custom-call(s32[2,4]{1,0:T(2,128)} %bitcast.3, s32[1]{0:T(128)S(6)} %copy.9.live, f32[2,24,1792]{2,1,0:T(8,128)} %obj.3, f32[2,4,256,256]{3,2,1,0:T(8,128)} %bitcast.2, f32[4,256,256]{2,1,0:T(8,128)} %amps_hbm.1, bf16[256,256]{1,0:T(8,128)(2,1)} %constant.10.cos, ...), custom_call_target="tpu_custom_call" | custom-call | tf_op jit(solution)/shard_map/step/pallas_call | solution.py:800
  123.0 1.9 %finish.1 = (f32[2,24,1792]{2,1,0:T(8,128)}, f32[2,8,256]{2,1,0:T(8,128)}) custom-call(f32[2,24,1792]{2,1,0:T(8,128)} %obj.3, f32[2,24,1792]{2,1,0:T(8,128)} %get-tuple-element.5.obj_step, f32[2,2,8,256]{3,2,1,0:T(8,128)} %get-tuple-element.6.probe_out, f32[8,128]{1,0:T(8,128)} %get-tuple-element.7.rates), custom_call_target="tpu_custom_call" | custom-call | tf_op jit(solution)/shard_map/finish/pallas_call | solution.py:778
